TPU v7x, 32 devices: a whole 2x2x4 slice. The times are simulated.
32 devices in a mesh: dp: 16 (over z, y, core), tensor: 2 (over x).
Axes of the slice: x: 2, y: 2, z: 4, core: 2. Of those that a mesh axis runs over, the one named last changes fastest.
Arguments:
- tokens: bfloat16 [8192, 2048], P(('dp', 'tensor')), may hold values from -6 to 6
- seg_ids: int32 [16, 512], P('dp'), may hold values from 0 to 1, as said below
- w_query: bfloat16 [2048, 2048], P('dp', 'tensor'), may hold values from -0.125 to 0.125
- w_key: bfloat16 [2048, 1024], P('dp', 'tensor'), may hold values from -0.125 to 0.125
- w_value: bfloat16 [2048, 1024], P('dp', 'tensor'), may hold values from -0.125 to 0.125
- w_output: bfloat16 [2048, 2048], P('tensor', 'dp'), may hold values from -0.5 to 0.5
- w_gate: bfloat16 [2048, 6144], P('dp', 'tensor'), may hold values from -0.125 to 0.125
- w_up: bfloat16 [2048, 6144], P('dp', 'tensor'), may hold values from -0.125 to 0.125
- w_down: bfloat16 [6144, 2048], P('tensor', 'dp'), may hold values from -0.078125 to 0.078125
- gain_attn: bfloat16 [2048], P('dp'), may hold values from 0.5 to 1.5
- gain_mlp: bfloat16 [2048], P('dp'), may hold values from 0.5 to 1.5
- gain_qk: bfloat16 [256], P('dp'), may hold values from 0.5 to 1.5
- cotangent: bfloat16 [8192, 2048], P(('dp', 'tensor')), may hold values from -6 to 6
Outputs:
- result: bfloat16 [8192, 2048], P(('dp', 'tensor'))
- input_grad: bfloat16 [8192, 2048], P(('dp', 'tensor'))
- grad_query: float32 [2048, 2048], P('dp', 'tensor')
- grad_key: float32 [2048, 1024], P('dp', 'tensor')
- grad_value: float32 [2048, 1024], P('dp', 'tensor')
- grad_output: float32 [2048, 2048], P('tensor', 'dp')
- grad_gate: float32 [2048, 6144], P('dp', 'tensor')
- grad_up: float32 [2048, 6144], P('dp', 'tensor')
- grad_down: float32 [6144, 2048], P('tensor', 'dp')
- grad_gain_attn: float32 [2048], P('dp')
- grad_gain_mlp: float32 [2048], P('dp')
- grad_gain_qk: float32 [256], P('dp')
Inputs may be any that keep to these rules, and one draw needn't show every extreme that they name: `seg_ids`: within each sequence the ids never fall and cover all 2 documents, each of 200 tokens or more.
All inputs are finite; a program needn't handle non-finite values.
Results may differ from a plain program's by a relative error of at most 0.017.
Values may be sent and summed in bfloat16 or wider, within the bound.
A program may use at most 256 MiB of HBM per device.

v0:
```python
import jax
import jax.numpy as jnp
from jax import lax
from jax.sharding import PartitionSpec as P

HD = 128


epsilon = 1e-06
rope_base = 1000000.0


def product(left, right):
    return jnp.dot(left, right, preferred_element_type=jnp.float32)


def lead_product(left, right):
    return lax.dot_general(
        left, right, (((0,), (0,)), ((), ())), preferred_element_type=jnp.float32
    )


def tail_product(left, right):
    return lax.dot_general(
        left, right, (((1,), (1,)), ((), ())), preferred_element_type=jnp.float32
    )


def norm_rows(values):
    return lax.rsqrt(jnp.mean(values * values, axis=-1, keepdims=True) + epsilon)


def norm_back(incoming, normed, inverse):
    return inverse * (incoming - normed * jnp.mean(incoming * normed, axis=-1, keepdims=True))


def rotate(values, cosine_table, sine_table):
    half_width = values.shape[-1] // 2
    turned = jnp.concatenate([-values[..., half_width:], values[..., :half_width]], axis=-1)
    return values * cosine_table + turned * sine_table


def rotate_back(incoming, cosine_table, sine_table):
    half_width = incoming.shape[-1] // 2
    scaled = incoming * sine_table
    return incoming * cosine_table + jnp.concatenate(
        [scaled[..., half_width:], -scaled[..., :half_width]], axis=-1
    )


def tables(segments):
    seq_len = segments.shape[0]
    token_index = jnp.arange(seq_len, dtype=jnp.int32)
    doc_start = jnp.sum((segments[None, :] < segments[:, None]).astype(jnp.int32), axis=1)
    doc_pos = (token_index - doc_start).astype(jnp.float32)
    frequency = rope_base ** (-jnp.arange(0, HD, 2).astype(jnp.float32) / HD)
    angles = doc_pos[:, None] * frequency[None, :]
    cosine_table = jnp.concatenate([jnp.cos(angles), jnp.cos(angles)], axis=1)
    sine_table = jnp.concatenate([jnp.sin(angles), jnp.sin(angles)], axis=1)
    allowed = (segments[:, None] == segments[None, :]) & (
        token_index[None, :] <= token_index[:, None]
    )
    return (cosine_table, sine_table, allowed)


def on_device(
    tokens,
    seg_ids,
    w_query,
    w_key,
    w_value,
    w_output,
    w_gate,
    w_up,
    w_down,
    gain_attn,
    gain_mlp,
    gain_qk,
    cotangent,
):
    gathered = (
        lax.all_gather(w_query, "dp", axis=0, tiled=True),
        lax.all_gather(w_key, "dp", axis=0, tiled=True),
        lax.all_gather(w_value, "dp", axis=0, tiled=True),
        lax.all_gather(w_output, "dp", axis=1, tiled=True),
        lax.all_gather(w_gate, "dp", axis=0, tiled=True),
        lax.all_gather(w_up, "dp", axis=0, tiled=True),
        lax.all_gather(w_down, "dp", axis=1, tiled=True),
        lax.all_gather(gain_attn, "dp", axis=0, tiled=True),
        lax.all_gather(gain_mlp, "dp", axis=0, tiled=True),
        lax.all_gather(gain_qk, "dp", axis=0, tiled=True),
    )
    (
        q_weight,
        k_weight,
        v_weight,
        o_weight,
        gate_weight,
        up_weight,
        down_weight,
        attn_norm,
        mlp_norm,
        qk_norm,
    ) = gathered
    attn_gain = attn_norm.astype(jnp.float32)
    mlp_gain = mlp_norm.astype(jnp.float32)
    query_gain = qk_norm[:HD].astype(jnp.float32)
    key_gain = qk_norm[HD:].astype(jnp.float32)
    score_scale = HD ** (-0.5)
    cosine_table, sine_table, allowed = tables(seg_ids[0])
    cosine_heads = cosine_table[:, None, :]
    sine_heads = sine_table[:, None, :]
    input_rows = tokens.astype(jnp.float32)
    inverse_one = norm_rows(input_rows)
    normed_one = input_rows * inverse_one
    full_one = lax.all_gather(
        (normed_one * attn_gain).astype(jnp.bfloat16), "tensor", axis=0, tiled=True
    )
    seq_len = full_one.shape[0]
    q_heads = q_weight.shape[1] // HD
    kv_heads = k_weight.shape[1] // HD
    per_group = q_heads // kv_heads
    query_raw = product(full_one, q_weight).reshape(seq_len, q_heads, HD)
    key_raw = product(full_one, k_weight).reshape(seq_len, kv_heads, HD)
    value_all = product(full_one, v_weight).astype(jnp.bfloat16).reshape(seq_len, kv_heads, HD)
    query_inverse = norm_rows(query_raw)
    query_hat = query_raw * query_inverse
    query_rot = (
        rotate(query_hat * query_gain, cosine_heads, sine_heads)
        .astype(jnp.bfloat16)
        .reshape(seq_len, kv_heads, per_group, HD)
    )
    key_inverse = norm_rows(key_raw)
    key_hat = key_raw * key_inverse
    key_all = rotate(key_hat * key_gain, cosine_heads, sine_heads).astype(jnp.bfloat16)
    scores = (
        jnp.einsum("sgrd,tgd->grst", query_rot, key_all, preferred_element_type=jnp.float32)
        * score_scale
    )
    exp_scores = jnp.where(allowed, jnp.exp(scores), 0.0)
    row_totals = jnp.sum(exp_scores, axis=-1, keepdims=True)
    log_totals = jnp.log(row_totals)
    probs_low = (exp_scores / row_totals).astype(jnp.bfloat16)
    attn_heads = jnp.einsum(
        "grst,tgd->sgrd", probs_low, value_all, preferred_element_type=jnp.float32
    )
    attn_rows = attn_heads.astype(jnp.bfloat16).reshape(seq_len, q_heads * HD)
    attn_branch = lax.psum_scatter(
        product(attn_rows, o_weight), "tensor", scatter_dimension=0, tiled=True
    )
    resid = input_rows + attn_branch
    inverse_two = norm_rows(resid)
    normed_two = resid * inverse_two
    full_two = lax.all_gather(
        (normed_two * mlp_gain).astype(jnp.bfloat16), "tensor", axis=0, tiled=True
    )
    gate_rows = product(full_two, gate_weight)
    up_rows = product(full_two, up_weight)
    gate_sig = jax.nn.sigmoid(gate_rows)
    act_rows = (gate_rows * gate_sig * up_rows).astype(jnp.bfloat16)
    mlp_branch = lax.psum_scatter(
        product(act_rows, down_weight).astype(jnp.bfloat16),
        "tensor",
        scatter_dimension=0,
        tiled=True,
    ).astype(jnp.float32)
    result_rows = (resid + mlp_branch).astype(jnp.bfloat16)
    again = (
        lax.all_gather(w_query, "dp", axis=0, tiled=True),
        lax.all_gather(w_key, "dp", axis=0, tiled=True),
        lax.all_gather(w_value, "dp", axis=0, tiled=True),
        lax.all_gather(w_output, "dp", axis=1, tiled=True),
        lax.all_gather(w_gate, "dp", axis=0, tiled=True),
        lax.all_gather(w_up, "dp", axis=0, tiled=True),
        lax.all_gather(w_down, "dp", axis=1, tiled=True),
        lax.all_gather(gain_attn, "dp", axis=0, tiled=True),
        lax.all_gather(gain_mlp, "dp", axis=0, tiled=True),
        lax.all_gather(gain_qk, "dp", axis=0, tiled=True),
    )
    (
        q_weight,
        k_weight,
        v_weight,
        o_weight,
        gate_weight,
        up_weight,
        down_weight,
        attn_norm,
        mlp_norm,
        qk_norm,
    ) = again
    cot_rows = cotangent.astype(jnp.float32)
    full_cot = lax.all_gather(cotangent, "tensor", axis=0, tiled=True)
    grad_down = lead_product(act_rows, full_cot)
    d_act = tail_product(full_cot, down_weight)
    d_gate = (d_act * up_rows * gate_sig * (1.0 + gate_rows * (1.0 - gate_sig))).astype(
        jnp.bfloat16
    )
    d_up = (d_act * gate_rows * gate_sig).astype(jnp.bfloat16)
    grad_gate = lead_product(full_two, d_gate)
    grad_up = lead_product(full_two, d_up)
    d_normed_two = lax.psum_scatter(
        (tail_product(d_gate, gate_weight) + tail_product(d_up, up_weight)).astype(jnp.bfloat16),
        "tensor",
        scatter_dimension=0,
        tiled=True,
    ).astype(jnp.float32)
    mlp_gain_part = jnp.sum(d_normed_two * normed_two, axis=0)
    d_resid = cot_rows + norm_back(d_normed_two * mlp_gain, normed_two, inverse_two)
    full_resid = lax.all_gather(d_resid.astype(jnp.bfloat16), "tensor", axis=0, tiled=True)
    grad_output = lead_product(attn_rows, full_resid)
    d_attn = (
        tail_product(full_resid, o_weight)
        .astype(jnp.bfloat16)
        .reshape(seq_len, kv_heads, per_group, HD)
    )
    scores_again = (
        jnp.einsum("sgrd,tgd->grst", query_rot, key_all, preferred_element_type=jnp.float32)
        * score_scale
    )
    probs_again = jnp.where(allowed, jnp.exp(scores_again - log_totals), 0.0)
    d_value_all = jnp.einsum(
        "grst,sgrd->tgd",
        probs_again.astype(jnp.bfloat16),
        d_attn,
        preferred_element_type=jnp.float32,
    )
    d_probs = jnp.einsum("sgrd,tgd->grst", d_attn, value_all, preferred_element_type=jnp.float32)
    row_delta = jnp.sum(probs_again * d_probs, axis=-1, keepdims=True)
    d_scores = (probs_again * (d_probs - row_delta)).astype(jnp.bfloat16)
    d_query = (
        jnp.einsum("grst,tgd->sgrd", d_scores, key_all, preferred_element_type=jnp.float32)
        * score_scale
    )
    d_key = (
        jnp.einsum("grst,sgrd->tgd", d_scores, query_rot, preferred_element_type=jnp.float32)
        * score_scale
    )
    d_value = d_value_all.astype(jnp.bfloat16).reshape(seq_len, kv_heads * HD)
    d_query_norm = rotate_back(d_query.reshape(seq_len, q_heads, HD), cosine_heads, sine_heads)
    d_key_norm = rotate_back(d_key, cosine_heads, sine_heads)
    query_gain_part = jnp.sum(d_query_norm * query_hat, axis=(0, 1))
    key_gain_part = jnp.sum(d_key_norm * key_hat, axis=(0, 1))
    d_query_raw = (
        norm_back(d_query_norm * query_gain, query_hat, query_inverse)
        .astype(jnp.bfloat16)
        .reshape(seq_len, q_heads * HD)
    )
    d_key_raw = (
        norm_back(d_key_norm * key_gain, key_hat, key_inverse)
        .astype(jnp.bfloat16)
        .reshape(seq_len, kv_heads * HD)
    )
    grad_query = lead_product(full_one, d_query_raw)
    grad_key = lead_product(full_one, d_key_raw)
    grad_value = lead_product(full_one, d_value)
    d_sum_one = (
        tail_product(d_query_raw, q_weight)
        + tail_product(d_key_raw, k_weight)
        + tail_product(d_value, v_weight)
    )
    d_normed_one = lax.psum_scatter(
        d_sum_one.astype(jnp.bfloat16), "tensor", scatter_dimension=0, tiled=True
    ).astype(jnp.float32)
    attn_gain_part = jnp.sum(d_normed_one * normed_one, axis=0)
    input_grad = (d_resid + norm_back(d_normed_one * attn_gain, normed_one, inverse_one)).astype(
        jnp.bfloat16
    )
    gain_sums = lax.psum(
        (attn_gain_part, mlp_gain_part, jnp.concatenate([query_gain_part, key_gain_part])), "tensor"
    )
    summed = (
        lax.psum_scatter(grad_query, "dp", scatter_dimension=0, tiled=True),
        lax.psum_scatter(grad_key, "dp", scatter_dimension=0, tiled=True),
        lax.psum_scatter(grad_value, "dp", scatter_dimension=0, tiled=True),
        lax.psum_scatter(grad_output, "dp", scatter_dimension=1, tiled=True),
        lax.psum_scatter(grad_gate, "dp", scatter_dimension=0, tiled=True),
        lax.psum_scatter(grad_up, "dp", scatter_dimension=0, tiled=True),
        lax.psum_scatter(grad_down, "dp", scatter_dimension=1, tiled=True),
        lax.psum_scatter(gain_sums[0], "dp", scatter_dimension=0, tiled=True),
        lax.psum_scatter(gain_sums[1], "dp", scatter_dimension=0, tiled=True),
        lax.psum_scatter(gain_sums[2], "dp", scatter_dimension=0, tiled=True),
    )
    return (
        result_rows,
        input_grad,
        summed[0],
        summed[1],
        summed[2],
        summed[3],
        summed[4],
        summed[5],
        summed[6],
        summed[7],
        summed[8],
        summed[9],
    )


def solution(mesh):
    return jax.shard_map(
        on_device,
        mesh=mesh,
        in_specs=(
            P(("dp", "tensor"), None),
            P("dp", None),
            P("dp", "tensor"),
            P("dp", "tensor"),
            P("dp", "tensor"),
            P("tensor", "dp"),
            P("dp", "tensor"),
            P("dp", "tensor"),
            P("tensor", "dp"),
            P("dp"),
            P("dp"),
            P("dp"),
            P(("dp", "tensor"), None),
        ),
        out_specs=(
            P(("dp", "tensor"), None),
            P(("dp", "tensor"), None),
            P("dp", "tensor"),
            P("dp", "tensor"),
            P("dp", "tensor"),
            P("tensor", "dp"),
            P("dp", "tensor"),
            P("dp", "tensor"),
            P("tensor", "dp"),
            P("dp"),
            P("dp"),
            P("dp"),
        ),
        check_vma=False,
    )
```

profile of v0, /device:TPU:0, one launch (start us, length us, event | category | flops | bytes accessed | tf_op | source)
XLA Modules:
  0.0 2065.3 jit_solution(12029931556056270963)
XLA Ops:
  7.2 23.3 %all-gather = bf16[16,1,128]{2,1,0:T(2,128)(2,1)S(1)} all-gather(bf16[1,1,128]{2,1,0:T(2,128)(2,1)} %bitcast.217), channel_id=1, replica_groups=mesh['dp'=16,'tensor'=2] {'dp'}, dimensions={0}, use_global_device_ids=true | all-gather | bytes 4352 | tf_op jit(solution)/shard_map/all_gather | solution.py:89
  39.4 29.8 %all-reduce = bf16[256]{0:T(256)(128)(2,1)S(1)} all-reduce(bf16[256]{0:T(256)(128)(2,1)S(1)} %dynamic-update-slice), channel_id=1, replica_groups=mesh['dp'=16,'tensor'=2] {'dp'}, use_global_device_ids=true, to_apply=%add | all-reduce | flops 256 | bytes 1024
  71.1 38.2 %all-gather.18.cloned.1.call-done = bf16[2048,512]{1,0:T(8,128)(2,1)} async-done(((bf16[128,512]{1,0:T(8,128)(2,1)}), bf16[2048,512]{1,0:T(8,128)(2,1)}) %all-gather.18.cloned.1.call-update) | async-done | bytes 2097168 | tf_op jit(solution)/shard_map/all_gather | solution.py:83
  109.3 3.5 multiply_reduce_fusion.6
  114.2 37.4 %all-gather.16.cloned.1.call-done = bf16[2048,512]{1,0:T(8,128)(2,1)} async-done(((bf16[128,512]{1,0:T(8,128)(2,1)}), bf16[2048,512]{1,0:T(8,128)(2,1)}) %all-gather.16.cloned.1.call-update) | async-done | bytes 2097168 | tf_op jit(solution)/shard_map/all_gather | solution.py:84
  151.7 3.7 convolution_convert_fusion.2
  155.4 47.5 %all-gather.20.cloned.1.call-done = bf16[2048,1024]{1,0:T(8,128)(2,1)} async-done(((bf16[128,1024]{1,0:T(8,128)(2,1)}), bf16[2048,1024]{1,0:T(8,128)(2,1)}) %all-gather.20.cloned.1.call-update) | async-done | bytes 4194320 | tf_op jit(solution)/shard_map/all_gather | solution.py:82
  202.8 5.8 fusion.55
  215.0 3.3 copy-done.6
  220.9 35.0 %all-gather.22.cloned.1.call-done = bf16[1024,2048]{1,0:T(8,128)(2,1)} async-done(((bf16[1024,128]{1,0:T(8,128)(2,1)}), bf16[1024,2048]{1,0:T(8,128)(2,1)}) %all-gather.22.cloned.1.call-update) | async-done | bytes 4194320 | tf_op jit(solution)/shard_map/all_gather | solution.py:85
  255.9 6.5 fusion.56
  263.0 18.5 all-gather.1
  281.6 33.5 %reduce-scatter.12.cloned.1.call-done = f32[256,2048]{1,0:T(8,128)} async-done(((f32[512,2048]{1,0:T(8,128)}), f32[256,2048]{1,0:T(8,128)}) %reduce-scatter.12.cloned.1.call-update) | async-done | bytes 2097168 | tf_op jit(solution)/shard_map/reduce_scatter | solution.py:148
  321.4 30.4 %all-gather.24.cloned.1.call-done = bf16[512,2048]{1,0:T(8,128)(2,1)} async-done(((bf16[256,2048]{1,0:T(8,128)(2,1)}), bf16[512,2048]{1,0:T(8,128)(2,1)}) %all-gather.24.cloned.1.call-update) | async-done | bytes 2097168 | tf_op jit(solution)/shard_map/all_gather | solution.py:154
  351.8 102.7 %all-gather.26.cloned.1.call-done = bf16[2048,3072]{1,0:T(8,128)(2,1)} async-done(((bf16[128,3072]{1,0:T(8,128)(2,1)}), bf16[2048,3072]{1,0:T(8,128)(2,1)}) %all-gather.26.cloned.1.call-update) | async-done | bytes 12582928 | tf_op jit(solution)/shard_map/all_gather | solution.py:86
  454.5 12.0 fusion.57
  466.5 89.0 %all-gather.28.cloned.1.call-done = bf16[2048,3072]{1,0:T(8,128)(2,1)} async-done(((bf16[128,3072]{1,0:T(8,128)(2,1)}), bf16[2048,3072]{1,0:T(8,128)(2,1)}) %all-gather.28.cloned.1.call-update) | async-done | bytes 12582928 | tf_op jit(solution)/shard_map/all_gather | solution.py:87
  555.5 12.0 fusion.58
  567.5 20.8 %all-gather.32.cloned.1.call-done = bf16[512,2048]{1,0:T(8,128)(2,1)} async-done(((bf16[256,2048]{1,0:T(8,128)(2,1)}), bf16[512,2048]{1,0:T(8,128)(2,1)}) %all-gather.32.cloned.1.call-update) | async-done | bytes 2097168 | tf_op jit(solution)/shard_map/all_gather | solution.py:193
  588.3 105.7 %all-gather.30.cloned.1.call-done = bf16[3072,2048]{1,0:T(8,128)(2,1)} async-done(((bf16[3072,128]{1,0:T(8,128)(2,1)}), bf16[3072,2048]{1,0:T(8,128)(2,1)}) %all-gather.30.cloned.1.call-update) | async-done | bytes 12582928 | tf_op jit(solution)/shard_map/all_gather | solution.py:88
  694.0 17.5 multiply_convert_fusion
  711.4 12.1 fusion.59
  723.5 25.4 %add_convert_fusion.1 = bf16[512,2048]{1,0:T(8,128)(2,1)} fusion(f32[512,2048]{1,0:T(8,128)} %fusion.59, bf16[512,3072]{1,0:T(8,128)(2,1)S(1)} %copy-done.67, bf16[2048,3072]{1,0:T(8,128)(2,1)} %all-gather.28.cloned.1.call-done), kind=kOutput, calls=%fused_computation.18 | convolution fusion | flops 6444548096 | bytes 22020096 | tf_op jit(solution)/shard_map/dot_general | solution.py:24
  749.0 30.2 %reduce-scatter.16.cloned.1.call-done = bf16[256,2048]{1,0:T(8,128)(2,1)} async-done(((bf16[512,2048]{1,0:T(8,128)(2,1)}), bf16[256,2048]{1,0:T(8,128)(2,1)}) %reduce-scatter.16.cloned.1.call-update) | async-done | bytes 1048592 | tf_op jit(solution)/shard_map/reduce_scatter | solution.py:202
  787.7 29.1 %all-gather.34.cloned.1.call-done = bf16[512,2048]{1,0:T(8,128)(2,1)} async-done(((bf16[256,2048]{1,0:T(8,128)(2,1)}), bf16[512,2048]{1,0:T(8,128)(2,1)}) %all-gather.34.cloned.1.call-update) | async-done | bytes 2097168 | tf_op jit(solution)/shard_map/all_gather | solution.py:210
  816.8 5.2 convolution_convert_fusion.1
  823.2 5.5 fusion
  828.6 6.2 fusion.40
  846.3 3.1 copy.97
  852.6 4.3 pad_maximum_fusion
  870.2 3.6 fusion.32
  881.6 11.6 convolution_convert_fusion
  894.8 3.3 fusion.64
  899.1 3.4 fusion.63
  903.8 5.7 fusion.62
  911.4 5.7 fusion.65
  918.7 13.8 fusion.66
  932.8 13.8 fusion.67
  948.2 14.2 fusion.68
  966.4 61.7 %all-reduce.4 = (f32[2048]{0:T(1024)S(1)}, f32[2048]{0:T(1024)S(1)}, f32[256]{0:T(256)S(1)}) all-reduce(f32[2048]{0:T(1024)S(1)} %get-tuple-element.16, f32[2048]{0:T(1024)S(1)} %copy-done.50, f32[256]{0:T(256)S(1)} %pad_maximum_fusion.3), channel_id=13, replica_groups=mesh['dp'=16,'tensor'=2] {'dp'}, use_global_device_ids=true, to_apply=%region_24.25.clone | all-reduce | flops 4352 | bytes 34816
  1028.3 5.4 all-reduce.5
  1033.7 4.8 fusion.21
  1038.6 62.8 %reduce-scatter.22.cloned.1.call-done = f32[128,512]{1,0:T(8,128)} async-done(((f32[2048,512]{1,0:T(8,128)}), f32[128,512]{1,0:T(8,128)}) %reduce-scatter.22.cloned.1.call-update) | async-done | bytes 262160 | tf_op jit(solution)/shard_map/reduce_scatter | solution.py:274
  1101.4 106.9 %reduce-scatter.20.cloned.1.call-done = f32[128,1024]{1,0:T(8,128)} async-done(((f32[2048,1024]{1,0:T(8,128)}), f32[128,1024]{1,0:T(8,128)}) %reduce-scatter.20.cloned.1.call-update) | async-done | bytes 524304 | tf_op jit(solution)/shard_map/reduce_scatter | solution.py:273
  1208.2 107.9 %reduce-scatter.26.cloned.1.call-done = f32[1024,128]{1,0:T(8,128)} async-done(((f32[1024,2048]{1,0:T(8,128)}), f32[1024,128]{1,0:T(8,128)}) %reduce-scatter.26.cloned.1.call-update) | async-done | bytes 524304 | tf_op jit(solution)/shard_map/reduce_scatter | solution.py:276
  1316.1 247.8 %reduce-scatter.28.cloned.1.call-done = f32[128,3072]{1,0:T(8,128)} async-done(((f32[2048,3072]{1,0:T(8,128)}), f32[128,3072]{1,0:T(8,128)}) %reduce-scatter.28.cloned.1.call-update) | async-done | bytes 1572880 | tf_op jit(solution)/shard_map/reduce_scatter | solution.py:277
  1563.9 247.3 %reduce-scatter.30.cloned.1.call-done = f32[128,3072]{1,0:T(8,128)} async-done(((f32[2048,3072]{1,0:T(8,128)}), f32[128,3072]{1,0:T(8,128)}) %reduce-scatter.30.cloned.1.call-update) | async-done | bytes 1572880 | tf_op jit(solution)/shard_map/reduce_scatter | solution.py:278
  1811.2 247.0 %reduce-scatter.32.cloned.1.call-done = f32[3072,128]{1,0:T(8,128)} async-done(((f32[3072,2048]{1,0:T(8,128)}), f32[3072,128]{1,0:T(8,128)}) %reduce-scatter.32.cloned.1.call-update) | async-done | bytes 1572880 | tf_op jit(solution)/shard_map/reduce_scatter | solution.py:279
  (256 shorter events, 83.6 us)
Async XLA Ops:
  7.2 64.0 %all-gather.14.cloned.1.call-start = ((), (), s32[]{:S(2)}) async-start(), calls=%async_computation.11 | async-start | bytes 3145728 | tf_op jit(solution)/shard_map/all_gather | solution.py:116
  32.1 5.8 copy-start.60
  32.1 7.1 copy-start.66
  32.1 37.1 %copy-start.51 = (s32[1,512]{1,0:T(1,128)S(1)}, s32[1,512]{1,0:T(1,128)}, u32[]{:S(2)}) copy-start(s32[1,512]{1,0:T(1,128)} %param.14) | copy-start | bytes 6148
  35.2 74.2 %all-gather.18.cloned.1.call-start = ((), (), s32[]{:S(2)}) async-start(), calls=%async_computation.13 | async-start | bytes 2228224 | tf_op jit(solution)/shard_map/all_gather | solution.py:83
  35.9 115.8 %all-gather.16.cloned.1.call-start = ((), (), s32[]{:S(2)}) async-start(), calls=%async_computation.12 | async-start | bytes 2228224 | tf_op jit(solution)/shard_map/all_gather | solution.py:84
  36.6 166.2 %all-gather.20.cloned.1.call-start = ((), (), s32[]{:S(2)}) async-start(), calls=%async_computation.14 | async-start | bytes 4456448 | tf_op jit(solution)/shard_map/all_gather | solution.py:82
  37.2 218.7 %all-gather.22.cloned.1.call-start = ((), (), s32[]{:S(2)}) async-start(), calls=%async_computation.15 | async-start | bytes 4456448 | tf_op jit(solution)/shard_map/all_gather | solution.py:85
  37.8 277.3 %reduce-scatter.12.cloned.1.call-start = ((), (), s32[]{:S(2)}) async-start(), calls=%async_computation.16 | async-start | bytes 6291456 | tf_op jit(solution)/shard_map/reduce_scatter | solution.py:148
  70.9 140.8 %copy-start.25 = (f32[512,128]{0,1:T(8,128)}, f32[512,128]{0,1:T(8,128)S(1)}, u32[]{:S(2)}) copy-start(f32[512,128]{0,1:T(8,128)S(1)} %get-tuple-element.43) | copy-start | bytes 786436
  70.9 42.3 %copy-start.56 = (f32[128]{0:T(128)}, f32[128]{0:T(128)S(1)}, u32[]{:S(2)}) copy-start(f32[128]{0:T(128)S(1)} %get-tuple-element.51) | copy-start | bytes 1540
  71.1 143.9 %copy-start.26 = (pred[512,512]{0,1:T(8,128)(4,1)}, pred[512,512]{0,1:T(8,128)(4,1)S(1)}, u32[]{:S(2)}) copy-start(pred[512,512]{0,1:T(8,128)(4,1)S(1)} %fusion.45) | copy-start | bytes 786436
  113.2 38.5 %copy-start.11 = (bf16[512,2048]{1,0:T(8,128)(2,1)S(1)}, bf16[512,2048]{1,0:T(8,128)(2,1)}, u32[]{:S(2)}) copy-start(bf16[512,2048]{1,0:T(8,128)(2,1)} %all-gather.14.cloned.1.call-done) | copy-start | bytes 6291460
  114.2 98.4 %copy-start.34 = (bf16[512,4,128,1]{0,2,3,1:T(8,128)(2,1)}, bf16[512,4,128,1]{0,2,3,1:T(8,128)(2,1)S(1)}, u32[]{:S(2)}) copy-start(bf16[512,4,128,1]{0,2,3,1:T(8,128)(2,1)S(1)} %fusion.46) | copy-start | bytes 1572868
  212.7 5.6 copy-start.40
  220.9 41.5 %copy-start.29 = (bf16[4,128,2,512]{3,1,2,0:T(8,128)(2,1)}, bf16[4,128,2,512]{3,1,2,0:T(8,128)(2,1)S(1)}, u32[]{:S(2)}) copy-start(bf16[4,128,2,512]{3,1,2,0:T(8,128)(2,1)S(1)} %fusion.36) | copy-start | bytes 3145732
  262.4 52.7 %copy-start.7 = (bf16[256,2048]{1,0:T(8,128)(2,1)S(1)}, bf16[256,2048]{1,0:T(8,128)(2,1)}, u32[]{:S(2)}) copy-start(bf16[256,2048]{1,0:T(8,128)(2,1)} %param.13) | copy-start | bytes 3145732
  262.4 89.4 %all-gather.24.cloned.1.call-start = ((), (), s32[]{:S(2)}) async-start(), calls=%async_computation.17 | async-start | bytes 3145728 | tf_op jit(solution)/shard_map/all_gather | solution.py:154
  281.6 500.3 %copy-start.44 = (f32[16,1,128]{2,1,0:T(1,128)}, f32[16,1,128]{2,1,0:T(1,128)S(1)}, u32[]{:S(2)}) copy-start(f32[16,1,128]{2,1,0:T(1,128)S(1)} %convert_element_type.155) | copy-start | bytes 24580
  317.1 464.8 %copy-start.2 = (f32[256,2048]{1,0:T(8,128)}, f32[256,2048]{1,0:T(8,128)S(1)}, u32[]{:S(2)}) copy-start(f32[256,2048]{1,0:T(8,128)S(1)} %get-tuple-element.28) | copy-start | bytes 6291460
  317.1 464.8 %copy-start.52 = (f32[256]{0:T(256)}, f32[256]{0:T(256)S(1)}, u32[]{:S(2)}) copy-start(f32[256]{0:T(256)S(1)} %add_rsqrt_fusion.2) | copy-start | bytes 3076
  318.5 136.0 %all-gather.26.cloned.1.call-start = ((), (), s32[]{:S(2)}) async-start(), calls=%async_computation.18 | async-start | bytes 13369344 | tf_op jit(solution)/shard_map/all_gather | solution.py:86
  319.3 236.2 %all-gather.28.cloned.1.call-start = ((), (), s32[]{:S(2)}) async-start(), calls=%async_computation.19 | async-start | bytes 13369344 | tf_op jit(solution)/shard_map/all_gather | solution.py:87
  320.0 268.3 %all-gather.32.cloned.1.call-start = ((), (), s32[]{:S(2)}) async-start(), calls=%async_computation.22 | async-start | bytes 3145728 | tf_op jit(solution)/shard_map/all_gather | solution.py:193
  320.6 373.4 %all-gather.30.cloned.1.call-start = ((), (), s32[]{:S(2)}) async-start(), calls=%async_computation.20 | async-start | bytes 13369344 | tf_op jit(solution)/shard_map/all_gather | solution.py:88
  321.4 457.8 %reduce-scatter.16.cloned.1.call-start = ((), (), s32[]{:S(2)}) async-start(), calls=%async_computation.23 | async-start | bytes 3145728 | tf_op jit(solution)/shard_map/reduce_scatter | solution.py:202
  711.4 12.1 copy-start.67
  749.0 32.9 %copy-start.13 = (bf16[256,2048]{1,0:T(8,128)(2,1)S(1)}, bf16[256,2048]{1,0:T(8,128)(2,1)}, u32[]{:S(2)}) copy-start(bf16[256,2048]{1,0:T(8,128)(2,1)} %param.25) | copy-start | bytes 3145732
  749.0 67.9 %all-gather.34.cloned.1.call-start = ((), (), s32[]{:S(2)}) async-start(), calls=%async_computation.24 | async-start | bytes 3145728 | tf_op jit(solution)/shard_map/all_gather | solution.py:210
  783.6 180.7 %reduce-scatter.18.cloned.1.call-start = ((), (), s32[]{:S(2)}) async-start(), calls=%async_computation.25 | async-start | bytes 3145728 | tf_op jit(solution)/shard_map/reduce_scatter | solution.py:262
  823.2 11.7 slice-start
  828.6 6.2 slice-start.1
  852.6 4.3 copy-start.5
  852.6 4.3 copy-start.24
  852.6 4.3 copy-start.31
  867.7 6.2 copy-start.19
  881.6 152.1 %reduce-scatter.14.cloned.1.call-start = ((), (), s32[]{:S(2)}) async-start(), calls=%async_computation.21 | async-start | bytes 3145728 | tf_op jit(solution)/shard_map/reduce_scatter | solution.py:161
  893.3 145.3 %reduce-scatter.24.cloned.1.call-start = ((), (), s32[]{:S(2)}) async-start(), calls=%async_computation.28 | async-start | bytes 4456448 | tf_op jit(solution)/shard_map/reduce_scatter | solution.py:275
  898.1 203.2 %reduce-scatter.22.cloned.1.call-start = ((), (), s32[]{:S(2)}) async-start(), calls=%async_computation.27 | async-start | bytes 4456448 | tf_op jit(solution)/shard_map/reduce_scatter | solution.py:274
  902.6 305.6 %reduce-scatter.20.cloned.1.call-start = ((), (), s32[]{:S(2)}) async-start(), calls=%async_computation.26 | async-start | bytes 8912896 | tf_op jit(solution)/shard_map/reduce_scatter | solution.py:273
  909.6 406.6 %reduce-scatter.26.cloned.1.call-start = ((), (), s32[]{:S(2)}) async-start(), calls=%async_computation.29 | async-start | bytes 8912896 | tf_op jit(solution)/shard_map/reduce_scatter | solution.py:276
  917.1 646.7 %reduce-scatter.28.cloned.1.call-start = ((), (), s32[]{:S(2)}) async-start(), calls=%async_computation.30 | async-start | bytes 26738688 | tf_op jit(solution)/shard_map/reduce_scatter | solution.py:277
  932.5 878.7 %reduce-scatter.30.cloned.1.call-start = ((), (), s32[]{:S(2)}) async-start(), calls=%async_computation.31 | async-start | bytes 26738688 | tf_op jit(solution)/shard_map/reduce_scatter | solution.py:278
  946.6 1111.6 %reduce-scatter.32.cloned.1.call-start = ((), (), s32[]{:S(2)}) async-start(), calls=%async_computation.32 | async-start | bytes 26738688 | tf_op jit(solution)/shard_map/reduce_scatter | solution.py:279
  962.4 71.3 %copy-start.3 = (f32[256,2048]{1,0:T(8,128)S(1)}, f32[256,2048]{1,0:T(8,128)}, u32[]{:S(2)}) copy-start(f32[256,2048]{1,0:T(8,128)} %copy-done.2) | copy-start | bytes 6291460
  962.4 71.3 %copy-start.45 = (f32[16,1,128]{2,1,0:T(1,128)S(1)}, f32[16,1,128]{2,1,0:T(1,128)}, u32[]{:S(2)}) copy-start(f32[16,1,128]{2,1,0:T(1,128)} %copy-done.44) | copy-start | bytes 24580
  962.4 71.3 %copy-start.53 = (f32[256]{0:T(256)S(1)}, f32[256]{0:T(256)}, u32[]{:S(2)}) copy-start(f32[256]{0:T(256)} %copy-done.52) | copy-start | bytes 3076
  962.4 71.3 %copy-start.59 = (f32[256]{0:T(256)S(1)}, f32[256]{0:T(256)}, u32[]{:S(2)}) copy-start(f32[256]{0:T(256)} %copy-done.58) | copy-start | bytes 3076
  (44 other events, 83.8 us)
Sparse Core Ops, SparseCore 0:
  35.3 30.3 all-gather.13
  67.8 41.4 all-gather.17
  111.5 40.1 all-gather.15
  153.7 49.0 all-gather.19
  204.8 50.9 all-gather.21
  262.5 52.5 reduce-scatter.11
  318.7 33.0 all-gather.23
  354.1 100.4 all-gather.25
  456.8 98.6 all-gather.27
  556.9 31.3 all-gather.31
  590.4 103.4 all-gather.29
  749.1 30.0 reduce-scatter.15
  783.7 33.0 all-gather.33
  881.7 31.8 reduce-scatter.17
  915.7 31.8 reduce-scatter.13
  952.0 73.3 reduce-scatter.23
  1029.7 71.6 reduce-scatter.21
  1105.8 102.3 reduce-scatter.19
  1212.8 103.2 reduce-scatter.25
  1320.6 243.1 reduce-scatter.27
  1568.6 242.6 reduce-scatter.29
  1815.9 242.2 reduce-scatter.31
where the time goes:
time: 2070 us
  waiting for transfers between devices  1620 us (78%)
  matrix products  202 us (10%)
  blocking collectives  139 us (7%)
  other arithmetic  42 us (2%)
  local copies, waits for them, and re-layouts  39 us (2%)
    reduce_scatter x1, waiting for transfers between devices, on_device(): lax.psum_scatter(grad_gate, 'dp', scatter_dimension=0, tiled=True)  248 us
    reduce_scatter x1, waiting for transfers between devices, on_device(): lax.psum_scatter(grad_up, 'dp', scatter_dimension=0, tiled=True)  247 us
    reduce_scatter x1, waiting for transfers between devices, on_device(): lax.psum_scatter(grad_down, 'dp', scatter_dimension=1, tiled=True)  247 us
    reduce_scatter x1, waiting for transfers between devices, on_device(): lax.psum_scatter(grad_output, 'dp', scatter_dimension=1, tiled=True)  108 us
    reduce_scatter x1, waiting for transfers between devices, on_device(): lax.psum_scatter(grad_query, 'dp', scatter_dimension=0, tiled=True)  107 us
    all_gather x1, waiting for transfers between devices, on_device(): lax.all_gather(w_down, 'dp', axis=1, tiled=True)  106 us
    all_gather x1, waiting for transfers between devices, on_device(): lax.all_gather(w_gate, 'dp', axis=0, tiled=True)  103 us
    unnamed x2, blocking collectives  91.5 us
  transfers between devices with their start and end apart: 22, of which 18 were waited for; matrix products, arithmetic and copies ran while one was open for 6% of the time, Pallas kernels for 0%

commit v1 on v0

--- a/solution.py
+++ b/solution.py
@@ -1,13 +1,301 @@
+import functools
 import jax
 import jax.numpy as jnp
 from jax import lax
+from jax.experimental import pallas as pl
+from jax.experimental.pallas import tpu as pltpu
+
 from jax.sharding import PartitionSpec as P
 
+MESH = pl.DeviceIdType.MESH
 HD = 128
-
-
 epsilon = 1e-06
 rope_base = 1000000.0
+
+
+def ring_place(n):
+    me = lax.axis_index("dp")
+    chip = me // 2
+    core = me % 2
+    odd = chip % 2
+    pos = (1 - odd) * (chip // 2) + odd * (n - 1 - chip // 2)
+    return pos, core
+
+
+def chip_at(pos, n):
+    high = pos // (n // 2)
+    return (1 - high) * (2 * pos) + high * (2 * (n - 1 - pos) + 1)
+
+
+def at(pos, core, n):
+    return (chip_at(pos, n) * 2 + core, lax.axis_index("tensor"))
+
+
+def meet(peers):
+    barrier = pltpu.get_barrier_semaphore()
+    for peer in peers:
+        pl.semaphore_signal(barrier, inc=1, device_id=peer, device_id_type=MESH)
+    pl.semaphore_wait(barrier, len(peers))
+
+
+def remote(src, dst, send, recv, peer):
+    return pltpu.make_async_remote_copy(
+        src_ref=src, dst_ref=dst, send_sem=send, recv_sem=recv, device_id=peer, device_id_type=MESH
+    )
+
+
+def gather_kernel(n, parts, count, swaps, *refs):
+    shards = refs[:count]
+    halves = refs[count : count + swaps]
+    fulls = refs[count + swaps : 2 * count + swaps]
+    wholes = refs[2 * count + swaps : 2 * (count + swaps)]
+    own_sem, send_sem, recv_sem, give_sem, take_sem, swap_sem = refs[2 * (count + swaps) :]
+    pos, core = ring_place(n)
+    lane = lax.axis_index("tensor")
+    nexts = (at((pos + 1) % n, core, n), at((pos + n - 1) % n, core, n))
+    mate = at(pos, 1 - core, n)
+    twin = (lax.axis_index("dp"), 1 - lane)
+    meet((*nexts, mate, twin))
+    messages = [(w, part) for w in range(count) for part in range(parts[w])]
+
+    def sizes(w):
+        rows = shards[w].shape[0]
+        return rows, rows // 2, rows // 2 // parts[w]
+
+    def spot(w, owner, who, side, part):
+        rows, half, piece = sizes(w)
+        start = (chip_at(owner, n) * 2 + who) * rows + (side * half + part * piece)
+        return fulls[w].at[pl.ds(pl.multiple_of(start, piece), piece)]
+
+    def shard_of(w, who):
+        rows = shards[w].shape[0]
+        return fulls[w].at[pl.ds(pl.multiple_of((chip_at(pos, n) * 2 + who) * rows, rows), rows)]
+
+    def swap_spot(s, which):
+        rows = halves[s].shape[0]
+        return wholes[s].at[pl.ds(pl.multiple_of(which * rows, rows), rows)]
+
+    for k, (w, part) in enumerate(messages):
+        rows, half, piece = sizes(w)
+        for side in range(2):
+            src = shards[w].at[pl.ds(side * half + part * piece, piece)]
+            remote(
+                src, spot(w, pos, core, side, part), send_sem.at[k, side, 0], recv_sem.at[k, side, 0], nexts[side]
+            ).start()
+    for s in range(swaps):
+        remote(halves[s], swap_spot(s, lane), swap_sem.at[s, 0], swap_sem.at[s, 1], twin).start()
+        pltpu.make_async_copy(halves[s], swap_spot(s, lane), own_sem.at[count + s]).start()
+    for w in range(count):
+        remote(shards[w], shard_of(w, core), give_sem.at[w, 0, n - 1], take_sem.at[w, 0, n - 1], mate).start()
+        pltpu.make_async_copy(shards[w], shard_of(w, core), own_sem.at[w]).start()
+
+    def owner_of(side, step):
+        if side == 0:
+            return (pos - 1 - step + 2 * n) % n
+        return (pos + 1 + step) % n
+
+    def step_body(step, carry):
+        for k, (w, part) in enumerate(messages):
+            for side in range(2):
+                block = spot(w, owner_of(side, step), core, side, part)
+                remote(block, block, send_sem.at[k, side, step], recv_sem.at[k, side, step], nexts[side]).wait_recv()
+
+                @pl.when(step < n - 2)
+                def _():
+                    remote(
+                        block, block, send_sem.at[k, side, step + 1], recv_sem.at[k, side, step + 1], nexts[side]
+                    ).start()
+
+                remote(block, block, give_sem.at[k, side, step], take_sem.at[k, side, step], mate).start()
+        return carry
+
+    lax.fori_loop(0, n - 1, step_body, 0)
+
+    def drain(step, carry):
+        for k, (w, part) in enumerate(messages):
+            for side in range(2):
+                owner = owner_of(side, step)
+                block = spot(w, owner, core, side, part)
+                theirs = spot(w, owner, 1 - core, side, part)
+                remote(block, block, send_sem.at[k, side, step], recv_sem.at[k, side, step], nexts[side]).wait_send()
+                given = remote(block, theirs, give_sem.at[k, side, step], take_sem.at[k, side, step], mate)
+                given.wait_send()
+                given.wait_recv()
+        return carry
+
+    lax.fori_loop(0, n - 1, drain, 0)
+    for w in range(count):
+        pltpu.make_async_copy(shards[w], shard_of(w, core), own_sem.at[w]).wait()
+        given = remote(shards[w], shard_of(w, 1 - core), give_sem.at[w, 0, n - 1], take_sem.at[w, 0, n - 1], mate)
+        given.wait_send()
+        given.wait_recv()
+    for s in range(swaps):
+        pltpu.make_async_copy(halves[s], swap_spot(s, lane), own_sem.at[count + s]).wait()
+        other = remote(halves[s], swap_spot(s, 1 - lane), swap_sem.at[s, 0], swap_sem.at[s, 1], twin)
+        other.wait_send()
+        other.wait_recv()
+
+
+def gather_weights(shards, swaps, parts, dp, collective_id):
+    n = dp // 2
+    count = len(shards)
+    msgs = sum(parts)
+    dma = pltpu.SemaphoreType.DMA
+    outs = pl.pallas_call(
+        functools.partial(gather_kernel, n, tuple(parts), count, len(swaps)),
+        out_shape=[
+            *[jax.ShapeDtypeStruct((s.shape[0] * dp, s.shape[1]), s.dtype) for s in shards],
+            *[jax.ShapeDtypeStruct((s.shape[0] * 2, s.shape[1]), s.dtype) for s in swaps],
+        ],
+        in_specs=[pl.BlockSpec(memory_space=pltpu.VMEM)] * (count + len(swaps)),
+        out_specs=[pl.BlockSpec(memory_space=pltpu.HBM)] * (count + len(swaps)),
+        scratch_shapes=[
+            dma((count + len(swaps),)),
+            dma((msgs, 2, n - 1)),
+            dma((msgs, 2, n - 1)),
+            dma((msgs, 2, n)),
+            dma((msgs, 2, n)),
+            dma((max(1, len(swaps)), 2)),
+        ],
+        compiler_params=pltpu.CompilerParams(collective_id=collective_id, has_side_effects=True),
+    )(*shards, *swaps)
+    return outs[:count], outs[count:]
+
+
+def reduce_kernel(n, pairs, *refs):
+    n_left = 1 + max(p[0] for p in pairs)
+    n_right = 1 + max(p[1] for p in pairs)
+    count = len(pairs)
+    lefts = refs[:n_left]
+    rights = refs[n_left : n_left + n_right]
+    outs = refs[n_left + n_right : n_left + n_right + count]
+    rest = refs[n_left + n_right + count :]
+    mine, give, take, ship, land = (rest[i * count : (i + 1) * count] for i in range(5))
+    term, give_sem, take_sem, ship_sem, land_sem = rest[5 * count :]
+    pos, core = ring_place(n)
+    nexts = (at((pos + 1) % n, core, n), at((pos + n - 1) % n, core, n))
+    mate = at(pos, 1 - core, n)
+    meet((*nexts, mate))
+    rows = outs[0].shape[0]
+
+    def owner_of(side, step):
+        if side == 0:
+            return (pos - 1 - step + 2 * n) % n
+        return (pos + 1 + step) % n
+
+    def early(m, side, step):
+        left, right = pairs[m]
+        wide = outs[m].shape[1] // 2
+        slot = step % 2
+        start = pl.multiple_of(chip_at(owner_of(side, step), n) * 2 * rows, 2 * rows)
+        part = term.at[:, pl.ds(0, wide)]
+        part[...] = jnp.dot(
+            lefts[left][pl.ds(start, 2 * rows), :],
+            rights[right][:, pl.ds(side * wide, wide)],
+            preferred_element_type=jnp.float32,
+        )
+        other = pl.ds(pl.multiple_of((1 - core) * rows, rows), rows)
+        same = pl.ds(pl.multiple_of(core * rows, rows), rows)
+        given = remote(
+            give[m].at[side, slot], take[m].at[side, slot],
+            give_sem.at[m, side, slot], take_sem.at[m, side, slot], mate,
+        )
+
+        @pl.when(step >= 2)
+        def _():
+            given.wait_send()
+
+        give[m][side, slot] = part[other, :].astype(jnp.bfloat16)
+        given.start()
+        mine[m][side] = part[same, :]
+
+    def shipped(m, side, step):
+        return remote(
+            ship[m].at[side, step % 2], land[m].at[side, step],
+            ship_sem.at[m, side, step % 2], land_sem.at[m, side, step], nexts[side],
+        )
+
+    def local_sum(m, side, step):
+        slot = step % 2
+        remote(
+            give[m].at[side, slot], take[m].at[side, slot],
+            give_sem.at[m, side, slot], take_sem.at[m, side, slot], mate,
+        ).wait_recv()
+        return mine[m][side] + take[m][side, slot].astype(jnp.float32)
+
+    for m in range(count):
+        for side in range(2):
+            early(m, side, 0)
+    for m in range(count):
+        for side in range(2):
+            total = local_sum(m, side, 0)
+            ship[m][side, 0] = total.astype(jnp.bfloat16)
+            shipped(m, side, 0).start()
+            early(m, side, 1)
+
+    def step_body(step, carry):
+        for m in range(count):
+            for side in range(2):
+                total = local_sum(m, side, step)
+                shipped(m, side, step - 1).wait_recv()
+                total = total + land[m][side, step - 1].astype(jnp.float32)
+
+                @pl.when(step >= 2)
+                def _():
+                    shipped(m, side, step - 2).wait_send()
+
+                ship[m][side, step % 2] = total.astype(jnp.bfloat16)
+                shipped(m, side, step).start()
+                early(m, side, step + 1)
+        return carry
+
+    lax.fori_loop(1, n - 1, step_body, 0)
+    last = n - 1
+    for m in range(count):
+        wide = outs[m].shape[1] // 2
+        for side in range(2):
+            total = local_sum(m, side, last)
+            shipped(m, side, last - 1).wait_recv()
+            outs[m][:, pl.ds(side * wide, wide)] = total + land[m][side, last - 1].astype(jnp.float32)
+    for m in range(count):
+        for side in range(2):
+            shipped(m, side, last - 1).wait_send()
+            if last >= 2:
+                shipped(m, side, last - 2).wait_send()
+            for slot in range(2):
+                remote(
+                    give[m].at[side, slot], take[m].at[side, slot],
+                    give_sem.at[m, side, slot], take_sem.at[m, side, slot], mate,
+                ).wait_send()
+
+
+def reduce_grads(lefts, rights, pairs, dp, collective_id):
+    n = dp // 2
+    count = len(pairs)
+    rows = lefts[0].shape[0] // dp
+    wides = [rights[r].shape[1] // 2 for _, r in pairs]
+    low = jnp.bfloat16
+    return pl.pallas_call(
+        functools.partial(reduce_kernel, n, tuple(pairs)),
+        out_shape=[jax.ShapeDtypeStruct((rows, 2 * w), jnp.float32) for w in wides],
+        in_specs=[pl.BlockSpec(memory_space=pltpu.VMEM)] * (len(lefts) + len(rights)),
+        out_specs=[pl.BlockSpec(memory_space=pltpu.VMEM)] * count,
+        scratch_shapes=[
+            *[pltpu.VMEM((2, rows, w), jnp.float32) for w in wides],
+            *[pltpu.VMEM((2, 2, rows, w), low) for w in wides],
+            *[pltpu.VMEM((2, 2, rows, w), low) for w in wides],
+            *[pltpu.VMEM((2, 2, rows, w), low) for w in wides],
+            *[pltpu.VMEM((2, n - 1, rows, w), low) for w in wides],
+            pltpu.VMEM((2 * rows, max(wides)), jnp.float32),
+            pltpu.SemaphoreType.DMA((count, 2, 2)),
+            pltpu.SemaphoreType.DMA((count, 2, 2)),
+            pltpu.SemaphoreType.DMA((count, 2, 2)),
+            pltpu.SemaphoreType.DMA((count, 2, n - 1)),
+        ],
+        compiler_params=pltpu.CompilerParams(
+            collective_id=collective_id, has_side_effects=True, vmem_limit_bytes=67043328
+        ),
+    )(*lefts, *rights)
 
 
 def product(left, right):
@@ -78,51 +366,46 @@
     gain_qk,
     cotangent,
 ):
-    gathered = (
-        lax.all_gather(w_query, "dp", axis=0, tiled=True),
-        lax.all_gather(w_key, "dp", axis=0, tiled=True),
-        lax.all_gather(w_value, "dp", axis=0, tiled=True),
-        lax.all_gather(w_output, "dp", axis=1, tiled=True),
-        lax.all_gather(w_gate, "dp", axis=0, tiled=True),
-        lax.all_gather(w_up, "dp", axis=0, tiled=True),
-        lax.all_gather(w_down, "dp", axis=1, tiled=True),
-        lax.all_gather(gain_attn, "dp", axis=0, tiled=True),
-        lax.all_gather(gain_mlp, "dp", axis=0, tiled=True),
-        lax.all_gather(gain_qk, "dp", axis=0, tiled=True),
-    )
-    (
-        q_weight,
-        k_weight,
-        v_weight,
-        o_weight,
-        gate_weight,
-        up_weight,
-        down_weight,
-        attn_norm,
-        mlp_norm,
-        qk_norm,
-    ) = gathered
-    attn_gain = attn_norm.astype(jnp.float32)
-    mlp_gain = mlp_norm.astype(jnp.float32)
-    query_gain = qk_norm[:HD].astype(jnp.float32)
-    key_gain = qk_norm[HD:].astype(jnp.float32)
+    dp = lax.axis_size("dp")
+    input_rows = tokens.astype(jnp.float32)
+    model = input_rows.shape[1]
+    inverse_one = norm_rows(input_rows)
+    normed_one = input_rows * inverse_one
+    gain_row = jnp.concatenate(
+        [
+            jnp.pad(g.astype(jnp.float32), (0, 128 - g.shape[0]))
+            for g in (gain_attn, gain_mlp, gain_qk)
+        ]
+    )
+    gain_shard = jnp.broadcast_to(gain_row[None, :], (16, gain_row.shape[0]))
+    shard_qkv = jnp.concatenate([w_query, w_key, w_value], axis=1)
+    (qkv_weight, out_weight, gain_all), (full_rows, full_cot) = gather_weights(
+        [shard_qkv, w_output.T, gain_shard], [tokens, cotangent], [2, 1, 1], dp, 0
+    )
+    gain_all = gain_all.reshape(dp, 16, 3, 128)[:, 0]
+    attn_gain = gain_all[:, 0, : gain_attn.shape[0]].reshape(-1)
+    full_rows = full_rows.astype(jnp.float32)
+    full_one = (full_rows * norm_rows(full_rows) * attn_gain).astype(jnp.bfloat16)
+    mlp_gain = gain_all[:, 1, : gain_mlp.shape[0]].reshape(-1)
+    qk_gain = gain_all[:, 2, : gain_qk.shape[0]].reshape(-1)
+    query_gain = qk_gain[:HD]
+    key_gain = qk_gain[HD:]
     score_scale = HD ** (-0.5)
     cosine_table, sine_table, allowed = tables(seg_ids[0])
     cosine_heads = cosine_table[:, None, :]
     sine_heads = sine_table[:, None, :]
-    input_rows = tokens.astype(jnp.float32)
-    inverse_one = norm_rows(input_rows)
-    normed_one = input_rows * inverse_one
-    full_one = lax.all_gather(
-        (normed_one * attn_gain).astype(jnp.bfloat16), "tensor", axis=0, tiled=True
-    )
     seq_len = full_one.shape[0]
-    q_heads = q_weight.shape[1] // HD
-    kv_heads = k_weight.shape[1] // HD
+    q_width = w_query.shape[1]
+    kv_width = w_key.shape[1]
+    q_heads = q_width // HD
+    kv_heads = kv_width // HD
     per_group = q_heads // kv_heads
-    query_raw = product(full_one, q_weight).reshape(seq_len, q_heads, HD)
-    key_raw = product(full_one, k_weight).reshape(seq_len, kv_heads, HD)
-    value_all = product(full_one, v_weight).astype(jnp.bfloat16).reshape(seq_len, kv_heads, HD)
+    projected = product(full_one, qkv_weight)
+    query_raw = projected[:, :q_width].reshape(seq_len, q_heads, HD)
+    key_raw = projected[:, q_width : q_width + kv_width].reshape(seq_len, kv_heads, HD)
+    value_all = (
+        projected[:, q_width + kv_width :].astype(jnp.bfloat16).reshape(seq_len, kv_heads, HD)
+    )
     query_inverse = norm_rows(query_raw)
     query_hat = query_raw * query_inverse
     query_rot = (
@@ -146,59 +429,40 @@
     )
     attn_rows = attn_heads.astype(jnp.bfloat16).reshape(seq_len, q_heads * HD)
     attn_branch = lax.psum_scatter(
-        product(attn_rows, o_weight), "tensor", scatter_dimension=0, tiled=True
-    )
+        tail_product(attn_rows, out_weight).astype(jnp.bfloat16),
+        "tensor",
+        scatter_dimension=0,
+        tiled=True,
+    ).astype(jnp.float32)
     resid = input_rows + attn_branch
     inverse_two = norm_rows(resid)
     normed_two = resid * inverse_two
     full_two = lax.all_gather(
         (normed_two * mlp_gain).astype(jnp.bfloat16), "tensor", axis=0, tiled=True
     )
+    (gate_weight, up_weight, down_weight), _ = gather_weights(
+        [w_gate, w_up, w_down.T], [], [1, 1, 1], dp, 1
+    )
     gate_rows = product(full_two, gate_weight)
     up_rows = product(full_two, up_weight)
     gate_sig = jax.nn.sigmoid(gate_rows)
     act_rows = (gate_rows * gate_sig * up_rows).astype(jnp.bfloat16)
     mlp_branch = lax.psum_scatter(
-        product(act_rows, down_weight).astype(jnp.bfloat16),
+        tail_product(act_rows, down_weight).astype(jnp.bfloat16),
         "tensor",
         scatter_dimension=0,
         tiled=True,
     ).astype(jnp.float32)
     result_rows = (resid + mlp_branch).astype(jnp.bfloat16)
-    again = (
-        lax.all_gather(w_query, "dp", axis=0, tiled=True),
-        lax.all_gather(w_key, "dp", axis=0, tiled=True),
-        lax.all_gather(w_value, "dp", axis=0, tiled=True),
-        lax.all_gather(w_output, "dp", axis=1, tiled=True),
-        lax.all_gather(w_gate, "dp", axis=0, tiled=True),
-        lax.all_gather(w_up, "dp", axis=0, tiled=True),
-        lax.all_gather(w_down, "dp", axis=1, tiled=True),
-        lax.all_gather(gain_attn, "dp", axis=0, tiled=True),
-        lax.all_gather(gain_mlp, "dp", axis=0, tiled=True),
-        lax.all_gather(gain_qk, "dp", axis=0, tiled=True),
-    )
-    (
-        q_weight,
-        k_weight,
-        v_weight,
-        o_weight,
-        gate_weight,
-        up_weight,
-        down_weight,
-        attn_norm,
-        mlp_norm,
-        qk_norm,
-    ) = again
     cot_rows = cotangent.astype(jnp.float32)
-    full_cot = lax.all_gather(cotangent, "tensor", axis=0, tiled=True)
-    grad_down = lead_product(act_rows, full_cot)
-    d_act = tail_product(full_cot, down_weight)
+    d_act = product(full_cot, down_weight)
     d_gate = (d_act * up_rows * gate_sig * (1.0 + gate_rows * (1.0 - gate_sig))).astype(
         jnp.bfloat16
     )
     d_up = (d_act * gate_rows * gate_sig).astype(jnp.bfloat16)
-    grad_gate = lead_product(full_two, d_gate)
-    grad_up = lead_product(full_two, d_up)
+    grad_gate, grad_up, grad_down = reduce_grads(
+        [full_two.T, full_cot.T], [d_gate, d_up, act_rows], [(0, 0), (0, 1), (1, 2)], dp, 2
+    )
     d_normed_two = lax.psum_scatter(
         (tail_product(d_gate, gate_weight) + tail_product(d_up, up_weight)).astype(jnp.bfloat16),
         "tensor",
@@ -208,9 +472,8 @@
     mlp_gain_part = jnp.sum(d_normed_two * normed_two, axis=0)
     d_resid = cot_rows + norm_back(d_normed_two * mlp_gain, normed_two, inverse_two)
     full_resid = lax.all_gather(d_resid.astype(jnp.bfloat16), "tensor", axis=0, tiled=True)
-    grad_output = lead_product(attn_rows, full_resid)
     d_attn = (
-        tail_product(full_resid, o_weight)
+        product(full_resid, out_weight)
         .astype(jnp.bfloat16)
         .reshape(seq_len, kv_heads, per_group, HD)
     )
@@ -251,49 +514,40 @@
         .astype(jnp.bfloat16)
         .reshape(seq_len, kv_heads * HD)
     )
-    grad_query = lead_product(full_one, d_query_raw)
-    grad_key = lead_product(full_one, d_key_raw)
-    grad_value = lead_product(full_one, d_value)
-    d_sum_one = (
-        tail_product(d_query_raw, q_weight)
-        + tail_product(d_key_raw, k_weight)
-        + tail_product(d_value, v_weight)
+    d_projected = jnp.concatenate([d_query_raw, d_key_raw, d_value], axis=1)
+    grad_qkv, grad_out = reduce_grads(
+        [full_one.T, full_resid.T], [d_projected, attn_rows], [(0, 0), (1, 1)], dp, 3
     )
     d_normed_one = lax.psum_scatter(
-        d_sum_one.astype(jnp.bfloat16), "tensor", scatter_dimension=0, tiled=True
+        tail_product(d_projected, qkv_weight).astype(jnp.bfloat16),
+        "tensor",
+        scatter_dimension=0,
+        tiled=True,
     ).astype(jnp.float32)
     attn_gain_part = jnp.sum(d_normed_one * normed_one, axis=0)
     input_grad = (d_resid + norm_back(d_normed_one * attn_gain, normed_one, inverse_one)).astype(
         jnp.bfloat16
     )
     gain_sums = lax.psum(
-        (attn_gain_part, mlp_gain_part, jnp.concatenate([query_gain_part, key_gain_part])), "tensor"
-    )
-    summed = (
-        lax.psum_scatter(grad_query, "dp", scatter_dimension=0, tiled=True),
-        lax.psum_scatter(grad_key, "dp", scatter_dimension=0, tiled=True),
-        lax.psum_scatter(grad_value, "dp", scatter_dimension=0, tiled=True),
-        lax.psum_scatter(grad_output, "dp", scatter_dimension=1, tiled=True),
-        lax.psum_scatter(grad_gate, "dp", scatter_dimension=0, tiled=True),
-        lax.psum_scatter(grad_up, "dp", scatter_dimension=0, tiled=True),
-        lax.psum_scatter(grad_down, "dp", scatter_dimension=1, tiled=True),
-        lax.psum_scatter(gain_sums[0], "dp", scatter_dimension=0, tiled=True),
-        lax.psum_scatter(gain_sums[1], "dp", scatter_dimension=0, tiled=True),
-        lax.psum_scatter(gain_sums[2], "dp", scatter_dimension=0, tiled=True),
-    )
+        jnp.concatenate([attn_gain_part, mlp_gain_part, query_gain_part, key_gain_part]),
+        ("dp", "tensor"),
+    )
+    me = lax.axis_index("dp")
+    share = model // dp
+    qk_share = 2 * HD // dp
     return (
         result_rows,
         input_grad,
-        summed[0],
-        summed[1],
-        summed[2],
-        summed[3],
-        summed[4],
-        summed[5],
-        summed[6],
-        summed[7],
-        summed[8],
-        summed[9],
+        grad_qkv[:, :q_width],
+        grad_qkv[:, q_width : q_width + kv_width],
+        grad_qkv[:, q_width + kv_width :],
+        grad_out.T,
+        grad_gate,
+        grad_up,
+        grad_down.T,
+        lax.dynamic_slice(gain_sums, (me * share,), (share,)),
+        lax.dynamic_slice(gain_sums, (model + me * share,), (share,)),
+        lax.dynamic_slice(gain_sums, (2 * model + me * qk_share,), (qk_share,)),
     )
 
 

time: 2070 us -> 923 us (0.45)
  waiting for transfers between devices: 1620 us -> 85.3 us
  Pallas kernels: 0 us -> 521 us
  blocking collectives: 139 us -> 39 us
  matrix products: 202 us -> 121 us
  local copies, waits for them, and re-layouts: 39 us -> 84.1 us
    reduce_scatter x10 -> x3, waiting for transfers between devices: 1050 us -> 30.7 us  [the longest x1 30.7 us: on_device(): lax.psum_scatter(tail_product(attn_rows, out_weight).astype(jnp.bfloat16)...]
    pallas_call x0 -> x4, Pallas kernels: none -> 521 us  [the longest x2 264 us: reduce_grads(): pl.pallas_call(functools.partial(reduce_kernel, n, tuple(pairs)), out_sha...]
    all_gather x9 -> x0, waiting for transfers between devices: 476 us -> none  [the longest x1 106 us: on_device(): lax.all_gather(w_down, 'dp', axis=1, tiled=True)]
    unnamed x2 -> x0, blocking collectives: 91.5 us -> none
    dot_general x7 -> x0, matrix products: 59.8 us -> none  [lead_product(): lax.dot_general(left, right, (((0,), (0,)), ((), ())), preferred_element_...]
    all_gather x2 -> x0, blocking collectives: 41.8 us -> none  [the longest x1 23.3 us: on_device(): lax.all_gather(gain_attn, 'dp', axis=0, tiled=True)]
    psum x1, blocking collectives: 5.42 us -> 39 us  [on_device(): lax.psum(jnp.concatenate([attn_gain_part, mlp_gain_part, query_gain_part,...]
    all_gather x1, waiting for transfers between devices: 30.4 us -> 0.02 us  [on_device(): lax.all_gather((normed_two * mlp_gain).astype(jnp.bfloat16), 'tensor', ax...]
  transfers between devices with their start and end apart: 22 -> 6, of which waited for: 18 -> 3; matrix products, arithmetic and copies ran while one was open for 6% -> 5% of each run, Pallas kernels for 0% -> 49%
where the time goes in v1:
time: 923 us; the launch traced here: 915 us
  Pallas kernels  521 us (56%)
  matrix products  121 us (13%)
  waiting for transfers between devices  85.3 us (9%)
  local copies, waits for them, and re-layouts  84.1 us (9%)
  other arithmetic  49.4 us (5%)
  blocking collectives  39 us (4%)
  between operations  15.5 us (2%)
    pallas_call x2, Pallas kernels, reduce_grads(): pl.pallas_call(functools.partial(reduce_kernel, n, tuple(pairs)), out_sha...  264 us
    pallas_call x2, Pallas kernels, gather_weights(): pl.pallas_call(functools.partial(gather_kernel, n, tuple(parts), count, l...  257 us
    dot_general x5, matrix products, product(): return jnp.dot(left, right, preferred_element_type=jnp.float32)  50.8 us
    dot_general x5, matrix products, tail_product(): lax.dot_general(left, right, (((1,), (1,)), ((), ())), preferred_element_...  46.6 us
    psum x1, blocking collectives, on_device(): lax.psum(jnp.concatenate([attn_gain_part, mlp_gain_part, query_gain_part,...  39 us
    unnamed x161, local copies, waits for them, and re-layouts  32.5 us
    reduce_scatter x1, waiting for transfers between devices, on_device(): lax.psum_scatter(tail_product(attn_rows, out_weight).astype(jnp.bfloat16)...  30.7 us
    reduce_scatter x1, waiting for transfers between devices, on_device(): lax.psum_scatter((tail_product(d_gate, gate_weight) + tail_product(d_up,...  28.9 us
  transfers between devices with their start and end apart: 6, of which 3 were waited for; matrix products, arithmetic and copies ran while one was open for 5% of the time, Pallas kernels for 49%

profile of v1, /device:TPU:0, one launch (start us, length us, event | category | flops | bytes accessed | tf_op | source)
XLA Modules:
  0.0 915.2 jit_solution(9170942426267847678)
XLA Ops:
  12.2 71.4 %shard_map.220 = (bf16[2048,2048]{1,0:T(8,128)(2,1)}, bf16[2048,1024]{1,0:T(8,128)(2,1)}, f32[256,384]{1,0:T(8,128)}, bf16[512,2048]{1,0:T(8,128)(2,1)}, bf16[512,2048]{1,0:T(8,128)(2,1)}) custom-call(bf16[128,2048]{1,0:T(8,128)(2,1)} %pad_maximum_fusion.2.refs_0_, bf16[128,1024]{1,0:T(8,128)(2,1)} %bitcast.179, f32[16,384]{1,0:T(8,128)} %broadcast_in_dim.10.refs_2_, ...), custom_call_target="tpu_custom_call" | custom-call | tf_op jit(solution)/shard_map/pallas_call | solution.py:144
  84.8 2.9 copy.231
  88.3 7.3 fusion.49
  99.8 3.2 fusion.63
  107.0 2.1 slice.108
  114.3 2.4 copy.290
  123.1 2.4 fusion.6
  125.5 2.3 fusion.38
  130.8 3.7 convolution_convert_fusion.1
  136.1 30.7 %reduce-scatter.5.cloned.1.call-done = bf16[256,2048]{0,1:T(8,128)(2,1)} async-done(((bf16[512,2048]{0,1:T(8,128)(2,1)}), bf16[256,2048]{0,1:T(8,128)(2,1)}) %reduce-scatter.5.cloned.1.call-update) | async-done | bytes 1048592 | tf_op jit(solution)/shard_map/reduce_scatter | solution.py:431
  170.0 2.3 copy.243
  172.3 185.8 %shard_map.221 = (bf16[2048,3072]{1,0:T(8,128)(2,1)}, bf16[2048,3072]{1,0:T(8,128)(2,1)}, bf16[2048,3072]{1,0:T(8,128)(2,1)}) custom-call(bf16[128,3072]{1,0:T(8,128)(2,1)} %refs_0_.1, bf16[128,3072]{1,0:T(8,128)(2,1)} %refs_1_.1, bf16[128,3072]{1,0:T(8,128)(2,1)} %bitcast.170), custom_call_target="tpu_custom_call" | custom-call | tf_op jit(solution)/shard_map/pallas_call | solution.py:144
  358.1 12.2 %fusion.69 = f32[512,3072]{1,0:T(8,128)} fusion(bf16[512,2048]{0,1:T(8,128)(2,1)} %all-gather.3.cloned.1.call-done, bf16[2048,3072]{1,0:T(8,128)(2,1)} %get-tuple-element.29), kind=kOutput, calls=%fused_computation.143 | convolution fusion | flops 6442450944 | bytes 20971520 | tf_op jit(solution)/shard_map/dot_general | solution.py:302
  370.4 8.7 fusion.70
  379.1 16.4 %multiply_convert_fusion = (bf16[512,3072]{1,0:T(8,128)(2,1)S(1)}, bf16[512,3072]{1,0:T(8,128)(2,1)S(1)}, bf16[512,3072]{1,0:T(8,128)(2,1)}) fusion(f32[512,3072]{1,0:T(8,128)} %fusion.69, f32[512,3072]{1,0:T(8,128)} %fusion.70, bf16[512,2048]{1,0:T(8,128)(2,1)S(1)} %copy-done.38, bf16[2048,3072]{1,0:T(8,128)(2,1)} %get-tuple-element.31), kind=kOutput, calls=%fused_computation.12 | convolution fusion | flops 6467616768 | bytes 36700160 | tf_op jit(solution)/shard_map/dot_general | solution.py:302
  395.5 12.0 %fusion.71 = f32[512,2048]{0,1:T(8,128)S(1)} fusion(bf16[512,3072]{1,0:T(8,128)(2,1)S(1)} %get-tuple-element.123.refs_2_, bf16[2048,3072]{1,0:T(8,128)(2,1)} %get-tuple-element.29), kind=kOutput, calls=%fused_computation.145 | convolution fusion | flops 6442450944 | bytes 19922944 | tf_op jit(solution)/shard_map/dot_general | solution.py:312
  407.5 10.7 %add_convert_fusion = bf16[512,2048]{0,1:T(8,128)(2,1)} fusion(f32[512,2048]{0,1:T(8,128)S(1)} %fusion.71, bf16[512,3072]{1,0:T(8,128)(2,1)S(1)} %get-tuple-element.122.refs_3_, bf16[2048,3072]{1,0:T(8,128)(2,1)} %get-tuple-element.30), kind=kOutput, calls=%fused_computation.22 | convolution fusion | flops 6444548096 | bytes 22020096 | tf_op jit(solution)/shard_map/dot_general | solution.py:312
  418.2 2.3 copy.245
  420.5 28.9 %reduce-scatter.9.cloned.1.call-done = bf16[256,2048]{0,1:T(8,128)(2,1)} async-done(((bf16[512,2048]{0,1:T(8,128)(2,1)}), bf16[256,2048]{0,1:T(8,128)(2,1)}) %reduce-scatter.9.cloned.1.call-update) | async-done | bytes 1048592 | tf_op jit(solution)/shard_map/reduce_scatter | solution.py:466
  449.3 3.5 fusion.27
  459.0 3.3 copy.292
  462.4 25.6 %all-gather.5.cloned.1.call-done = bf16[512,2048]{0,1:T(8,128)(2,1)} async-done(((bf16[256,2048]{0,1:T(8,128)(2,1)}), bf16[512,2048]{0,1:T(8,128)(2,1)}) %all-gather.5.cloned.1.call-update) | async-done | bytes 2097168 | tf_op jit(solution)/shard_map/all_gather | solution.py:474
  487.9 6.1 convolution_convert_fusion.3
  495.7 5.5 fusion
  502.1 2.6 fusion.2
  504.7 3.2 bitcast_multiply_fusion.4
  508.0 2.9 copy.255
  512.7 2.6 fusion.64
  515.4 2.2 copy.256
  517.6 4.1 pad_maximum_fusion
  521.7 3.1 copy.257
  524.8 6.5 fusion.42
  533.6 2.2 copy.295
  535.9 3.7 broadcast_multiply_fusion.1
  543.1 2.0 copy.297
  547.3 3.6 fusion.33
  551.9 9.4 %convolution_convert_fusion.2 = bf16[512,2048]{0,1:T(8,128)(2,1)} fusion(bf16[2048,2048]{1,0:T(8,128)(2,1)} %get-tuple-element.27, bf16[512,512]{1,0:T(8,128)(2,1)S(1)} %copy-done.45, bf16[512,512]{1,0:T(8,128)(2,1)S(1)} %copy-done.43, bf16[512,1024]{1,0:T(8,128)(2,1)S(1)} %fusion.33), kind=kOutput, calls=%fused_computation.31 | convolution fusion | flops 4302307328 | bytes 12582912 | tf_op jit(solution)/shard_map/dot_general | solution.py:312
  561.4 10.9 %convolution_convert_fusion = bf16[512,2048]{0,1:T(8,128)(2,1)} fusion(bf16[512,3072]{1,0:T(8,128)(2,1)S(1)} %copy-done.33, bf16[2048,3072]{1,0:T(8,128)(2,1)} %get-tuple-element.31), kind=kOutput, calls=%fused_computation.29 | convolution fusion | flops 6443499520 | bytes 17825792 | tf_op jit(solution)/shard_map/dot_general | solution.py:312
  573.8 2.5 copy.265
  580.3 193.3 %shard_map.223 = (f32[128,3072]{1,0:T(8,128)}, f32[128,3072]{1,0:T(8,128)}, f32[128,3072]{1,0:T(8,128)}) custom-call(bf16[2048,512]{1,0:T(8,128)(2,1)} %bitcast.175, bf16[2048,512]{1,0:T(8,128)(2,1)} %bitcast.163, bf16[512,3072]{1,0:T(8,128)(2,1)} %copy-done.32, bf16[512,3072]{1,0:T(8,128)(2,1)} %copy-done.31, bf16[512,3072]{1,0:T(8,128)(2,1)} %get-tuple-element.124.refs_4_), custom_call_target="tpu_custom_call" | custom-call | tf_op jit(solution)/shard_map/pallas_call | solution.py:278
  773.6 3.2 copy.269
  779.0 70.4 %shard_map.222 = (f32[128,2048]{1,0:T(8,128)}, f32[128,1024]{1,0:T(8,128)}) custom-call(bf16[2048,512]{1,0:T(8,128)(2,1)} %fusion.48.refs_0_, bf16[2048,512]{1,0:T(8,128)(2,1)} %bitcast.171, bf16[512,2048]{1,0:T(8,128)(2,1)} %pad_maximum_fusion.1.refs_2_, bf16[512,1024]{1,0:T(8,128)(2,1)} %copy.291.refs_3_), custom_call_target="tpu_custom_call" | custom-call | tf_op jit(solution)/shard_map/pallas_call | solution.py:278
  849.3 2.1 copy.268
  851.5 2.0 slice.79
  855.4 2.2 fusion.29
  857.6 39.0 %psum.7 = f32[4352]{0:T(1024)S(1)} all-reduce(f32[4352]{0:T(1024)S(1)} %pad_maximum_fusion.5), channel_id=1, replica_groups=mesh['dp'=16,'tensor'=2] {'dp','tensor'}, use_global_device_ids=true, to_apply=%region_20.21 | all-reduce | flops 4352 | bytes 34816 | tf_op jit(solution)/shard_map/psum | solution.py:531
  896.7 3.8 fusion.23
  900.5 2.4 copy.266
  (239 shorter events, 68.0 us)
Async XLA Ops:
  7.2 159.6 %reduce-scatter.5.cloned.1.call-start = ((), (), s32[]{:S(2)}) async-start(), calls=%async_computation.4 | async-start | bytes 3145728 | tf_op jit(solution)/shard_map/reduce_scatter | solution.py:431
  84.8 3.4 copy-start.56
  84.8 368.0 %copy-start.54 = (f32[16,1,128]{2,1,0:T(1,128)}, f32[16,1,128]{2,1,0:T(1,128)S(1)}, u32[]{:S(2)}) copy-start(f32[16,1,128]{2,1,0:T(1,128)S(1)} %get-tuple-element.143) | copy-start | bytes 24580
  87.7 7.8 copy-start.9
  88.2 7.3 copy-start.66
  98.4 21.8 %copy-start.4 = (f32[512,4,128]{0,2,1:T(8,128)}, f32[512,4,128]{0,2,1:T(8,128)S(1)}, u32[]{:S(2)}) copy-start(f32[512,4,128]{0,2,1:T(8,128)S(1)} %copy.233) | copy-start | bytes 3145732
  125.5 4.3 copy-start.3
  125.5 5.3 copy-start.72
  134.5 223.6 %all-gather.3.cloned.1.call-start = ((), (), s32[]{:S(2)}) async-start(), calls=%async_computation.5 | async-start | bytes 3145728 | tf_op jit(solution)/shard_map/all_gather | solution.py:440
  136.1 316.8 %copy-start = (bf16[256,2048]{0,1:T(8,128)(2,1)}, bf16[256,2048]{0,1:T(8,128)(2,1)S(1)}, u32[]{:S(2)}) copy-start(bf16[256,2048]{0,1:T(8,128)(2,1)S(1)} %copy.229) | copy-start | bytes 3145732
  168.5 284.3 %copy-start.61 = (f32[256]{0:T(256)}, f32[256]{0:T(256)S(1)}, u32[]{:S(2)}) copy-start(f32[256]{0:T(256)S(1)} %add_rsqrt_fusion.4) | copy-start | bytes 3076
  170.0 279.4 %reduce-scatter.9.cloned.1.call-start = ((), (), s32[]{:S(2)}) async-start(), calls=%async_computation.7 | async-start | bytes 3145728 | tf_op jit(solution)/shard_map/reduce_scatter | solution.py:466
  358.1 12.2 %copy-start.42 = (bf16[512,2048]{0,1:T(8,128)(2,1)S(1)}, bf16[512,2048]{0,1:T(8,128)(2,1)}, u32[]{:S(2)}) copy-start(bf16[512,2048]{0,1:T(8,128)(2,1)} %all-gather.3.cloned.1.call-done) | copy-start | bytes 6291460
  358.1 12.2 %copy-start.71 = (bf16[2048,3072]{1,0:T(8,128)(2,1)S(1)}, bf16[2048,3072]{1,0:T(8,128)(2,1)}, u32[]{:S(2)}) copy-start(bf16[2048,3072]{1,0:T(8,128)(2,1)} %get-tuple-element.30) | copy-start | bytes 37748740
  370.4 8.7 copy-start.38
  395.5 12.0 %copy-start.32 = (bf16[512,3072]{1,0:T(8,128)(2,1)}, bf16[512,3072]{1,0:T(8,128)(2,1)S(1)}, u32[]{:S(2)}) copy-start(bf16[512,3072]{1,0:T(8,128)(2,1)S(1)} %get-tuple-element.123.refs_2_) | copy-start | bytes 9437188
  395.5 12.0 %copy-start.31 = (bf16[512,3072]{1,0:T(8,128)(2,1)}, bf16[512,3072]{1,0:T(8,128)(2,1)S(1)}, u32[]{:S(2)}) copy-start(bf16[512,3072]{1,0:T(8,128)(2,1)S(1)} %get-tuple-element.122.refs_3_) | copy-start | bytes 9437188
  418.2 69.7 %all-gather.5.cloned.1.call-start = ((), (), s32[]{:S(2)}) async-start(), calls=%async_computation.8 | async-start | bytes 3145728 | tf_op jit(solution)/shard_map/all_gather | solution.py:474
  449.3 3.5 copy-start.7
  449.3 3.5 copy-start.11
  449.3 3.5 copy-start.13
  454.7 400.7 %reduce-scatter.11.cloned.1.call-start = ((), (), s32[]{:S(2)}) async-start(), calls=%async_computation.9 | async-start | bytes 3145728 | tf_op jit(solution)/shard_map/reduce_scatter | solution.py:521
  495.6 5.5 copy-start.20
  495.6 5.5 slice-start
  495.6 6.4 slice-start.1
  524.8 6.5 copy-start.15
  524.8 6.5 copy-start.19
  524.8 6.5 copy-start.34
  542.1 3.7 copy-start.49
  547.3 4.6 copy-start.43
  547.3 4.6 copy-start.45
  551.9 9.4 %copy-start.33 = (bf16[512,3072]{1,0:T(8,128)(2,1)S(1)}, bf16[512,3072]{1,0:T(8,128)(2,1)}, u32[]{:S(2)}) copy-start(bf16[512,3072]{1,0:T(8,128)(2,1)} %get-tuple-element.124.refs_4_) | copy-start | bytes 9437188
  561.3 335.4 %reduce-scatter.7.cloned.1.call-start = ((), (), s32[]{:S(2)}) async-start(), calls=%async_computation.6 | async-start | bytes 3145728 | tf_op jit(solution)/shard_map/reduce_scatter | solution.py:450
  773.6 3.8 copy-start.24
  773.6 3.8 copy-start.44
  773.6 3.8 copy-start.46
  849.3 6.1 copy-start.1
  849.3 6.1 copy-start.58
  849.3 6.1 copy-start.63
  851.5 6.1 copy-start.59
  851.5 6.1 copy-start.69
  851.5 6.2 copy-start.70
  851.5 45.2 %copy-start.8 = (bf16[256,2048]{0,1:T(8,128)(2,1)S(1)}, bf16[256,2048]{0,1:T(8,128)(2,1)}, u32[]{:S(2)}) copy-start(bf16[256,2048]{0,1:T(8,128)(2,1)} %reduce-scatter.5.cloned.1.call-done) | copy-start | bytes 3145732
  851.5 45.2 %copy-start.12 = (bf16[256,2048]{0,1:T(8,128)(2,1)S(1)}, bf16[256,2048]{0,1:T(8,128)(2,1)}, u32[]{:S(2)}) copy-start(bf16[256,2048]{0,1:T(8,128)(2,1)} %reduce-scatter.9.cloned.1.call-done) | copy-start | bytes 3145732
  851.5 45.2 %copy-start.55 = (f32[16,1,128]{2,1,0:T(1,128)S(1)}, f32[16,1,128]{2,1,0:T(1,128)}, u32[]{:S(2)}) copy-start(f32[16,1,128]{2,1,0:T(1,128)} %copy-done.54) | copy-start | bytes 24580
  851.5 45.2 %copy-start.62 = (f32[256]{0:T(256)S(1)}, f32[256]{0:T(256)}, u32[]{:S(2)}) copy-start(f32[256]{0:T(256)} %copy-done.61) | copy-start | bytes 3076
  851.5 45.2 %copy-start.65 = (f32[256]{0:T(256)S(1)}, f32[256]{0:T(256)}, u32[]{:S(2)}) copy-start(f32[256]{0:T(256)} %copy-done.64) | copy-start | bytes 3076
  900.5 5.0 copy-start.48
  (33 other events, 68.5 us)
Sparse Core Ops, SparseCore 0:
  134.6 32.0 reduce-scatter.4
  170.1 33.0 all-gather.2
  418.3 30.9 reduce-scatter.8
  454.8 33.0 all-gather.4
  561.4 31.8 reduce-scatter.10
  595.5 31.8 reduce-scatter.6

commit v2 on v1

--- a/solution.py
+++ b/solution.py
@@ -351,6 +351,675 @@
     return (cosine_table, sine_table, allowed)
 
 
+def turn(values):
+    return pltpu.roll(values, values.shape[-1] // 2, 1)
+
+
+def row_scale(values):
+    return lax.rsqrt(jnp.mean(values * values, axis=-1, keepdims=True) + epsilon)
+
+
+def head_at(index):
+    return pl.ds(pl.multiple_of(index * HD, HD), HD)
+
+
+def prepared(raw, gain, cosine, sine):
+    inverse = row_scale(raw)
+    hat = raw * inverse
+    scaled = hat * gain
+    return inverse, hat, (scaled * cosine + turn(scaled) * sine).astype(jnp.bfloat16)
+
+
+def exp_block(query, keys, seg_col, seg_row, first):
+    width = keys.shape[0]
+    scores = tail_product(query, keys) * HD ** (-0.5)
+    rows = lax.broadcasted_iota(jnp.int32, scores.shape, 0) + first
+    columns = lax.broadcasted_iota(jnp.int32, scores.shape, 1)
+    allowed = (seg_col[first : first + scores.shape[0], :] == seg_row[:, :width]) & (
+        columns <= rows
+    )
+    return jnp.where(allowed, jnp.exp(scores), 0.0)
+
+
+def attend_group(group, dims, qkv, tab, seg_col, seg_row, gains, attn, kept):
+    q_heads, kv_heads, seq, block = dims
+    per_group = q_heads // kv_heads
+    cosine, sine = tab[0], tab[1]
+    raw = qkv[:, head_at(q_heads + group)]
+    kept[0] = prepared(raw, gains[1:2, :], cosine, sine)[2]
+    kept[1] = qkv[:, head_at(q_heads + kv_heads + group)].astype(jnp.bfloat16)
+    for r in range(per_group):
+        head = group * per_group + r
+        raw = qkv[:, head_at(head)]
+        query = prepared(raw, gains[0:1, :], cosine, sine)[2]
+        for first in range(0, seq, block):
+            width = first + block
+            exps = exp_block(query[first:width], kept[0, :width, :], seg_col, seg_row, first)
+            probs = (exps / jnp.sum(exps, axis=-1, keepdims=True)).astype(jnp.bfloat16)
+            attn[first:width, head_at(head)] = product(probs, kept[1, :width, :]).astype(jnp.bfloat16)
+
+
+def block_columns(ref, index, width):
+    if width % 128 == 0:
+        return ref[:, pl.ds(pl.multiple_of(index * width, width), width)]
+    fold = 128 // width
+    tile = ref[:, pl.ds(pl.multiple_of((index // fold) * 128, 128), 128)]
+    picked = tile[:, :width]
+    for i in range(1, fold):
+        picked = jnp.where(index % fold == i, tile[:, i * width : (i + 1) * width], picked)
+    return picked
+
+
+def forward_kernel(n, dims, *refs):
+    (
+        shards, qkv, out_weight, tokens, cot_full, tab, seg_col, seg_row, gains, mlp_gain,
+        weights, attn, resid, full_two, act,
+        kept, part, peer, acc, blocks,
+        own_sem, send_sem, recv_sem, give_sem, take_sem, swap_sem, load_sem,
+    ) = refs
+    q_heads, kv_heads, seq, block = dims
+    pos, core = ring_place(n)
+    lane = lax.axis_index("tensor")
+    nexts = (at((pos + 1) % n, core, n), at((pos + n - 1) % n, core, n))
+    mate = at(pos, 1 - core, n)
+    twin = (lax.axis_index("dp"), 1 - lane)
+    count, rows, width = shards.shape
+    wide = width // 2
+    model = 2 * n * rows
+    half = seq // 2
+    meet((*nexts, mate, twin))
+
+    def owner_of(side, step):
+        if side == 0:
+            return (pos - step + 2 * n) % n
+        return (pos + step) % n
+
+    def spot(w, chip, who, side):
+        start = w * model + (chip * 2 + who) * rows
+        return weights.at[pl.ds(pl.multiple_of(start, rows), rows), pl.ds(side * wide, wide)]
+
+    def hop(w, side, step):
+        here = spot(w, chip_at(owner_of(side, step), n), core, side)
+        return remote(here, here, send_sem.at[w, side, step], recv_sem.at[w, side, step], nexts[side])
+
+    def first_hop(w, side):
+        return remote(
+            shards.at[w, :, pl.ds(side * wide, wide)],
+            spot(w, chip_at(pos, n), core, side),
+            send_sem.at[w, side, 1], recv_sem.at[w, side, 1], nexts[side],
+        )
+
+    def onward(w, side, step):
+        here = spot(w, chip_at(owner_of(side, step), n), core, side)
+        return remote(here, here, send_sem.at[w, side, step + 1], recv_sem.at[w, side, step + 1], nexts[side])
+
+    def hand(w, side, step, who):
+        here = spot(w, chip_at(owner_of(side, step), n), who, side)
+        return remote(here, here, give_sem.at[w, side, step], take_sem.at[w, side, step], mate)
+
+    def hand_own(w, side, who):
+        return remote(
+            shards.at[w, :, pl.ds(side * wide, wide)],
+            spot(w, chip_at(pos, n), who, side),
+            give_sem.at[w, side, 0], take_sem.at[w, side, 0], mate,
+        )
+
+    def keep_own(w, side):
+        return pltpu.make_async_copy(
+            shards.at[w, :, pl.ds(side * wide, wide)], spot(w, chip_at(pos, n), core, side), own_sem.at[w, side]
+        )
+
+    for w in range(count):
+        for side in range(2):
+            first_hop(w, side).start()
+    for w in range(count):
+        for side in range(2):
+            hand_own(w, side, core).start()
+            keep_own(w, side).start()
+
+    def service(event):
+        step, w = event // count + 1, event % count
+        for side in range(2):
+            hop(w, side, step).wait_recv()
+
+            @pl.when(step < n - 1)
+            def _():
+                onward(w, side, step).start()
+
+            hand(w, side, step, core).start()
+
+    def load(job, side):
+        step, w = job // count, job % count
+        start = w * model + chip_at(owner_of(side, step), n) * 2 * rows
+        return pltpu.make_async_copy(
+            weights.at[pl.ds(pl.multiple_of(start, 2 * rows), 2 * rows), pl.ds(side * wide, wide)],
+            blocks.at[side], load_sem.at[side],
+        )
+
+    def work(job):
+        step, w = job // count, job % count
+        for side in range(2):
+            @pl.when(step > 0)
+            def _():
+                hand(w, side, step, 1 - core).wait_recv()
+
+            @pl.when(step == 0)
+            def _():
+                hand_own(w, side, 1 - core).wait_recv()
+                keep_own(w, side).wait()
+
+            load(job, side).start()
+        for side in range(2):
+            load(job, side).wait()
+            chip = chip_at(owner_of(side, step), n)
+
+            def with_left(left):
+                tile = wide // 3
+
+                def one(i, carry):
+                    there = pl.ds(pl.multiple_of(side * wide + i * tile, tile), tile)
+                    gained = product(left, blocks[side, :, pl.ds(pl.multiple_of(i * tile, tile), tile)])
+
+                    @pl.when(step == 0)
+                    def _():
+                        acc[w, :, there] = gained
+
+                    @pl.when(step > 0)
+                    def _():
+                        acc[w, :, there] += gained
+
+                    return carry
+
+                lax.fori_loop(0, 3, one, 0)
+
+            @pl.when(w < 2)
+            def _():
+                with_left(block_columns(full_two, chip, 2 * rows))
+
+            @pl.when(w == 2)
+            def _():
+                with_left(block_columns(cot_full, chip, 2 * rows))
+
+    groups = (qkv, tab, seg_col, seg_row, gains, attn, kept)
+
+    def attend(first, last):
+        def one(group, carry):
+            attend_group(group, dims, *groups)
+            return carry
+
+        lax.fori_loop(first, last, one, 0)
+
+    attend(0, kv_heads // 2)
+    service(0)
+    attend(kv_heads // 2, kv_heads)
+    service(1)
+    theirs = pl.ds(pl.multiple_of((1 - lane) * half, half), half)
+    ours = pl.ds(pl.multiple_of(lane * half, half), half)
+    part[...] = tail_product(attn[theirs, :], out_weight[...]).astype(jnp.bfloat16)
+    send_part = remote(part, peer, swap_sem.at[0, 0], swap_sem.at[0, 1], twin)
+    send_part.start()
+    resid[...] = tokens[...].astype(jnp.float32) + tail_product(attn[ours, :], out_weight[...])
+    for event in range(2, 6):
+        service(event)
+    send_part.wait_recv()
+    summed = resid[...] + peer[...].astype(jnp.float32)
+    resid[...] = summed
+    send_part.wait_send()
+    part[...] = (summed * row_scale(summed) * mlp_gain[...]).astype(jnp.bfloat16)
+    send_two = remote(part, full_two.at[ours], swap_sem.at[1, 0], swap_sem.at[1, 1], twin)
+    send_two.start()
+    full_two[ours, :] = part[...]
+    ready = 9
+    for event in range(6, ready):
+        service(event)
+    remote(part, full_two.at[theirs], swap_sem.at[1, 0], swap_sem.at[1, 1], twin).wait_recv()
+
+    def both(i, carry):
+        service(ready + i)
+
+        @pl.when(i < ready + 3)
+        def _():
+            def one(q, carry):
+                work(2 * i + q)
+                return carry
+
+            lax.fori_loop(0, 2, one, 0)
+
+        @pl.when(i >= ready + 3)
+        def _():
+            work(ready + 3 + i)
+
+        return carry
+
+    lax.fori_loop(0, count * (n - 1) - ready, both, 0)
+    send_two.wait_send()
+
+    strip = 32
+
+    def finish(i, carry):
+        there = pl.ds(pl.multiple_of(i * strip, strip), strip)
+        gate = acc[0, there, :]
+        up = acc[1, there, :]
+        d_act = acc[2, there, :]
+        sig = 1.0 / (1.0 + jnp.exp(-gate))
+        silu = gate * sig
+        act[0, there, :] = (d_act * up * sig * (1.0 + gate * (1.0 - sig))).astype(jnp.bfloat16)
+        act[1, there, :] = (d_act * silu).astype(jnp.bfloat16)
+        act[2, there, :] = (silu * up).astype(jnp.bfloat16)
+        return carry
+
+    lax.fori_loop(0, seq // strip, finish, 0)
+
+    def drain(step, carry):
+        for w in range(count):
+            for side in range(2):
+                hop(w, side, step).wait_send()
+                hand(w, side, step, core).wait_send()
+        return carry
+
+    lax.fori_loop(1, n, drain, 0)
+    for w in range(count):
+        for side in range(2):
+            hand_own(w, side, core).wait_send()
+
+
+def forward_block(shards, qkv, out_weight, tokens, cot_full, tab, segments, gains, mlp_gain, q_heads, kv_heads, dp):
+    n = dp // 2
+    count, rows, width = shards.shape
+    seq, model = cot_full.shape
+    half = seq // 2
+    low, dma, vmem = jnp.bfloat16, pltpu.SemaphoreType.DMA, pltpu.VMEM
+    shape = jax.ShapeDtypeStruct
+    place = lambda kind: pl.BlockSpec(memory_space=kind)
+    return pl.pallas_call(
+        functools.partial(forward_kernel, n, (q_heads, kv_heads, seq, seq // 2)),
+        out_shape=[
+            shape((count * model, width), low),
+            shape((seq, q_heads * HD), low),
+            shape((half, model), jnp.float32),
+            shape((seq, model), low),
+            shape((count, seq, width), low),
+        ],
+        in_specs=[place(vmem)] * 10,
+        out_specs=[place(pltpu.HBM)] + [place(vmem)] * 4,
+        scratch_shapes=[
+            vmem((2, seq, HD), low),
+            vmem((half, model), low),
+            vmem((half, model), low),
+            vmem((count, seq, width), jnp.float32),
+            vmem((2, 2 * rows, width // 2), low),
+            dma((count, 2)),
+            dma((count, 2, n)),
+            dma((count, 2, n)),
+            dma((count, 2, n)),
+            dma((count, 2, n)),
+            dma((2, 2)),
+            dma((2,)),
+        ],
+        compiler_params=pltpu.CompilerParams(
+            collective_id=1, has_side_effects=True, vmem_limit_bytes=67043328
+        ),
+    )(
+        shards, qkv, out_weight, tokens, cot_full, tab,
+        segments.reshape(seq, 1), segments.reshape(1, seq), gains, mlp_gain,
+    )
+
+
+SLOTS = 3
+
+
+def undo(incoming, hat, inverse, gain, cosine, sine):
+    turned = incoming * cosine - turn(incoming) * sine
+    total = jnp.sum(turned * hat, axis=0, keepdims=True)
+    scaled = turned * gain
+    raw = inverse * (scaled - hat * jnp.mean(scaled * hat, axis=-1, keepdims=True))
+    return total, raw.astype(jnp.bfloat16)
+
+
+def attend_back(group, dims, heads, tab, seg_col, seg_row, gains, d_attn, d_proj, sums, kept):
+    q_heads, kv_heads, seq, block = dims
+    per_group = q_heads // kv_heads
+    low = jnp.bfloat16
+    scale = HD ** (-0.5)
+    cosine, sine = tab[0], tab[1]
+    keys = prepared(heads[per_group], gains[1:2, :], cosine, sine)[2]
+    values = heads[per_group + 1].astype(low)
+    for r in range(per_group):
+        head = group * per_group + r
+        q_inverse, q_hat, query = prepared(heads[r], gains[0:1, :], cosine, sine)
+        for first in range(0, seq, block):
+            width = first + block
+            exps = exp_block(query[first:width], keys[:width], seg_col, seg_row, first)
+            probs = exps / jnp.sum(exps, axis=-1, keepdims=True)
+            incoming = d_attn[first:width, head_at(head)]
+            d_probs = tail_product(incoming, values[:width])
+            delta = jnp.sum(probs * d_probs, axis=-1, keepdims=True)
+            d_scores = (probs * (d_probs - delta)).astype(low)
+            kept[0, first:width, :] = product(d_scores, keys[:width]) * scale
+            d_keys = lead_product(d_scores, query[first:width])
+            d_values = lead_product(probs.astype(low), incoming)
+            if r == 0 and first == 0:
+                kept[1] = jnp.zeros_like(kept[1])
+                kept[2] = jnp.zeros_like(kept[2])
+            kept[1, :width, :] += d_keys
+            kept[2, :width, :] += d_values
+        total, raw = undo(kept[0], q_hat, q_inverse, gains[0:1, :], cosine, sine)
+        sums[0:1, :] += total
+        d_proj[:, head_at(head)] = raw
+    k_inverse, k_hat, _ = prepared(heads[per_group], gains[1:2, :], cosine, sine)
+    total, raw = undo(kept[1] * scale, k_hat, k_inverse, gains[1:2, :], cosine, sine)
+    sums[1:2, :] += total
+    d_proj[:, head_at(q_heads + group)] = raw
+    d_proj[:, head_at(q_heads + kv_heads + group)] = kept[2].astype(low)
+
+
+def reducer(n, pos, core, nexts, mate, refs, left_of):
+    lefts, rights, out, mine, term, give, take, ship, land, give_sem, take_sem, ship_sem, land_sem, free_sem, out_sem = refs
+    count = rights.shape[0]
+    wide = rights.shape[2] // 2
+    rows = out.shape[1]
+
+    def owner_of(side, step):
+        if side == 0:
+            return (pos - 1 - step + 2 * n) % n
+        return (pos + 1 + step) % n
+
+    def given(m, side, step):
+        return remote(
+            give.at[m, side], take.at[m, side, step % 2],
+            give_sem.at[m, side], take_sem.at[m, side, step % 2], mate,
+        )
+
+    def shipped(m, side, step):
+        return remote(
+            ship.at[m, side], land.at[m, side, step % SLOTS],
+            ship_sem.at[m, side], land_sem.at[m, side, step % SLOTS], nexts[side],
+        )
+
+    def early(m, step):
+        for side in range(2):
+            start = pl.multiple_of(chip_at(owner_of(side, step), n) * 2 * rows, 2 * rows)
+            left = lefts[left_of(m), pl.ds(start, 2 * rows), :]
+            tile = wide // 3
+
+            def one(i, carry):
+                there = pl.multiple_of(i * tile, tile)
+                term[:, pl.ds(there, tile)] = product(
+                    left, rights[m, :, pl.ds(pl.multiple_of(side * wide + there, tile), tile)]
+                )
+                return carry
+
+            lax.fori_loop(0, 3, one, 0)
+
+            @pl.when(step >= 1)
+            def _():
+                given(m, side, step - 1).wait_send()
+
+            give[m, side] = term[pl.ds(pl.multiple_of((1 - core) * rows, rows), rows), :].astype(jnp.bfloat16)
+            given(m, side, step).start()
+            mine[m, side] = term[pl.ds(pl.multiple_of(core * rows, rows), rows), :]
+
+    def event(e):
+        step, m = e // count, e % count
+        for side in range(2):
+            given(m, side, step).wait_recv()
+
+            @pl.when(step == 0)
+            def _():
+                mine[m, side] += take[m, side, 0].astype(jnp.float32)
+
+            @pl.when(step > 0)
+            def _():
+                shipped(m, side, step - 1).wait_recv()
+                mine[m, side] += take[m, side, step % 2].astype(jnp.float32) + land[
+                    m, side, (step - 1) % SLOTS
+                ].astype(jnp.float32)
+
+                @pl.when(step - 1 + SLOTS <= n - 2)
+                def _():
+                    pl.semaphore_signal(
+                        free_sem.at[m, side], inc=1, device_id=nexts[1 - side], device_id_type=MESH
+                    )
+
+                shipped(m, side, step - 1).wait_send()
+
+            @pl.when(step < n - 1)
+            def _():
+                @pl.when(step >= SLOTS)
+                def _():
+                    pl.semaphore_wait(free_sem.at[m, side], 1)
+
+                ship[m, side] = mine[m, side].astype(jnp.bfloat16)
+                shipped(m, side, step).start()
+
+            @pl.when(step == n - 1)
+            def _():
+                written(m, side).start()
+
+        @pl.when(step < n - 1)
+        def _():
+            early(m, step + 1)
+
+    def written(m, side):
+        return pltpu.make_async_copy(mine.at[m, side], out.at[m, :, pl.ds(side * wide, wide)], out_sem.at[m, side])
+
+    def finish():
+        for m in range(count):
+            for side in range(2):
+                given(m, side, n - 1).wait_send()
+                written(m, side).wait()
+
+    return early, event, finish
+
+
+def reduce_scratch(n, count, rows, wide):
+    low, dma, vmem = jnp.bfloat16, pltpu.SemaphoreType.DMA, pltpu.VMEM
+    return [
+        vmem((count, 2, rows, wide), jnp.float32),
+        vmem((2 * rows, wide), jnp.float32),
+        vmem((count, 2, rows, wide), low),
+        vmem((count, 2, 2, rows, wide), low),
+        vmem((count, 2, rows, wide), low),
+        vmem((count, 2, SLOTS, rows, wide), low),
+        dma((count, 2)),
+        dma((count, 2, 2)),
+        dma((count, 2)),
+        dma((count, 2, SLOTS)),
+        pltpu.SemaphoreType.REGULAR((count, 2)),
+        dma((count, 2)),
+    ]
+
+
+def backward_kernel(n, dims, *refs):
+    (
+        lefts, act, weights, qkv, out_weight, cot, resid, tab, seg_col, seg_row, gains, mlp_gain,
+        grads, d_proj, d_full, d_resid, mlp_sum, qk_sum,
+        gate_block, up_block, own, part, peer, d_attn, heads, kept,
+        swap_sem, load_sem, head_sem,
+    ) = refs[:29]
+    q_heads, kv_heads, seq, block = dims
+    pos, core = ring_place(n)
+    lane = lax.axis_index("tensor")
+    nexts = (at((pos + 1) % n, core, n), at((pos + n - 1) % n, core, n))
+    mate = at(pos, 1 - core, n)
+    twin = (lax.axis_index("dp"), 1 - lane)
+    meet((*nexts, mate, twin))
+    count = act.shape[0]
+    model = resid.shape[1]
+    half = seq // 2
+    early, event, finish = reducer(
+        n, pos, core, nexts, mate, (lefts, act, grads, *refs[29:]), lambda m: m // 2
+    )
+    for m in range(count):
+        early(m, 0)
+    for m in range(count):
+        event(m)
+
+    theirs = pl.ds(pl.multiple_of((1 - lane) * half, half), half)
+    ours = pl.ds(pl.multiple_of(lane * half, half), half)
+    deep = gate_block.shape[0]
+    turns = model // deep
+
+    def fetch(i, which):
+        target = (gate_block, up_block)[which]
+        start = which * model + i * deep
+        return pltpu.make_async_copy(
+            weights.at[pl.ds(pl.multiple_of(start, deep), deep), :], target, load_sem.at[which]
+        )
+
+    fetch(0, 0).start()
+    fetch(0, 1).start()
+
+    def narrow(i, carry):
+        there = pl.ds(pl.multiple_of(i * deep, deep), deep)
+        for which, target in enumerate((gate_block, up_block)):
+            fetch(i, which).wait()
+            other = tail_product(act[which, theirs, :], target[...])
+            same = tail_product(act[which, ours, :], target[...])
+            if which == 0:
+                own[:, there] = same
+                d_resid[:, there] = other
+            else:
+                own[:, there] += same
+                part[:, there] = (d_resid[:, there] + other).astype(jnp.bfloat16)
+
+            @pl.when(i < turns - 1)
+            def _():
+                fetch(i + 1, which).start()
+
+        @pl.when(i % 3 == 2)
+        def _():
+            event(count + i // 3)
+
+        return carry
+
+    lax.fori_loop(0, turns, narrow, 0)
+    done = count + turns // 3
+    send = remote(part, peer, swap_sem.at[0, 0], swap_sem.at[0, 1], twin)
+    send.start()
+    for e in range(done, done + 3):
+        event(e)
+    done = done + 3
+    send.wait_recv()
+    send.wait_send()
+    strip = 32
+
+    def norm_strip(i, carry):
+        there = pl.ds(pl.multiple_of(i * strip, strip), strip)
+        incoming = own[there, :] + peer[there, :].astype(jnp.float32)
+        hidden = resid[there, :]
+        inverse = row_scale(hidden)
+        normed = hidden * inverse
+        scaled = incoming * mlp_gain[...]
+        change = cot[there, :].astype(jnp.float32) + inverse * (
+            scaled - normed * jnp.mean(scaled * normed, axis=-1, keepdims=True)
+        )
+        d_resid[there, :] = change
+        part[there, :] = change.astype(jnp.bfloat16)
+        total = jnp.sum(incoming * normed, axis=0, keepdims=True)
+
+        @pl.when(i == 0)
+        def _():
+            mlp_sum[...] = total
+
+        @pl.when(i > 0)
+        def _():
+            mlp_sum[...] += total
+
+        return carry
+
+    lax.fori_loop(0, half // strip, norm_strip, 0)
+    send = remote(part, d_full.at[ours], swap_sem.at[1, 0], swap_sem.at[1, 1], twin)
+    send.start()
+    d_full[ours, :] = part[...]
+    columns = out_weight.shape[1]
+    quarter = columns // 4
+
+    for e in range(done, done + 3):
+        event(e)
+    done = done + 3
+    remote(part, d_full.at[theirs], swap_sem.at[1, 0], swap_sem.at[1, 1], twin).wait_recv()
+    send.wait_send()
+    for i in range(4):
+        there = pl.ds(i * quarter, quarter)
+        d_attn[:, there] = product(d_full[...], out_weight[:, there]).astype(jnp.bfloat16)
+    event(done)
+    done = done + 1
+    per_group = q_heads // kv_heads
+    qk_sum[...] = jnp.zeros_like(qk_sum)
+
+    def group_step(group, carry):
+        places = [group * per_group + r for r in range(per_group)]
+        places += [q_heads + group, q_heads + kv_heads + group]
+        copies = [
+            pltpu.make_async_copy(qkv.at[:, head_at(place)], heads.at[i], head_sem.at[i])
+            for i, place in enumerate(places)
+        ]
+        for copy in copies:
+            copy.start()
+        for copy in copies:
+            copy.wait()
+        attend_back(group, dims, heads, tab, seg_col, seg_row, gains, d_attn, d_proj, qk_sum, kept)
+        event(done + group)
+        return carry
+
+    lax.fori_loop(0, kv_heads, group_step, 0)
+    done = done + kv_heads
+
+    def rest(e, carry):
+        event(e)
+        return carry
+
+    lax.fori_loop(done, count * n, rest, 0)
+    finish()
+
+
+def backward_block(
+    lefts, act, weights, qkv, out_weight, cot, resid, tab, segments, gains, mlp_gain, q_heads, kv_heads, dp
+):
+    n = dp // 2
+    count, seq, width = act.shape
+    half, model = resid.shape
+    rows = model // dp
+    low, dma, vmem = jnp.bfloat16, pltpu.SemaphoreType.DMA, pltpu.VMEM
+    shape = jax.ShapeDtypeStruct
+    place = lambda kind: pl.BlockSpec(memory_space=kind)
+    deep = 256
+    return pl.pallas_call(
+        functools.partial(backward_kernel, n, (q_heads, kv_heads, seq, seq // 2)),
+        out_shape=[
+            shape((count, rows, width), jnp.float32),
+            shape((seq, (q_heads + 2 * kv_heads) * HD), low),
+            shape((seq, model), low),
+            shape((half, model), jnp.float32),
+            shape((1, model), jnp.float32),
+            shape((8, HD), jnp.float32),
+        ],
+        in_specs=[place(vmem)] * 2 + [place(pltpu.HBM)] * 2 + [place(vmem)] * 8,
+        out_specs=[place(pltpu.HBM)] + [place(vmem)] * 5,
+        scratch_shapes=[
+            vmem((deep, width), low),
+            vmem((deep, width), low),
+            vmem((half, model), jnp.float32),
+            vmem((half, model), low),
+            vmem((half, model), low),
+            vmem((seq, q_heads * HD), low),
+            vmem((q_heads // kv_heads + 2, seq, HD), jnp.float32),
+            vmem((3, seq, HD), jnp.float32),
+            dma((2, 2)),
+            dma((2,)),
+            dma((q_heads // kv_heads + 2,)),
+            *reduce_scratch(n, count, rows, width // 2),
+        ],
+        compiler_params=pltpu.CompilerParams(
+            collective_id=2, has_side_effects=True, vmem_limit_bytes=67043328
+        ),
+    )(
+        lefts, act, weights, qkv, out_weight, cot, resid, tab,
+        segments.reshape(seq, 1), segments.reshape(1, seq), gains, mlp_gain,
+    )
+
+
 def on_device(
     tokens,
     seg_ids,
@@ -390,131 +1059,56 @@
     qk_gain = gain_all[:, 2, : gain_qk.shape[0]].reshape(-1)
     query_gain = qk_gain[:HD]
     key_gain = qk_gain[HD:]
-    score_scale = HD ** (-0.5)
-    cosine_table, sine_table, allowed = tables(seg_ids[0])
-    cosine_heads = cosine_table[:, None, :]
-    sine_heads = sine_table[:, None, :]
+    cosine_table, sine_table, _ = tables(seg_ids[0])
     seq_len = full_one.shape[0]
     q_width = w_query.shape[1]
     kv_width = w_key.shape[1]
     q_heads = q_width // HD
     kv_heads = kv_width // HD
-    per_group = q_heads // kv_heads
     projected = product(full_one, qkv_weight)
-    query_raw = projected[:, :q_width].reshape(seq_len, q_heads, HD)
-    key_raw = projected[:, q_width : q_width + kv_width].reshape(seq_len, kv_heads, HD)
-    value_all = (
-        projected[:, q_width + kv_width :].astype(jnp.bfloat16).reshape(seq_len, kv_heads, HD)
-    )
-    query_inverse = norm_rows(query_raw)
-    query_hat = query_raw * query_inverse
-    query_rot = (
-        rotate(query_hat * query_gain, cosine_heads, sine_heads)
-        .astype(jnp.bfloat16)
-        .reshape(seq_len, kv_heads, per_group, HD)
-    )
-    key_inverse = norm_rows(key_raw)
-    key_hat = key_raw * key_inverse
-    key_all = rotate(key_hat * key_gain, cosine_heads, sine_heads).astype(jnp.bfloat16)
-    scores = (
-        jnp.einsum("sgrd,tgd->grst", query_rot, key_all, preferred_element_type=jnp.float32)
-        * score_scale
-    )
-    exp_scores = jnp.where(allowed, jnp.exp(scores), 0.0)
-    row_totals = jnp.sum(exp_scores, axis=-1, keepdims=True)
-    log_totals = jnp.log(row_totals)
-    probs_low = (exp_scores / row_totals).astype(jnp.bfloat16)
-    attn_heads = jnp.einsum(
-        "grst,tgd->sgrd", probs_low, value_all, preferred_element_type=jnp.float32
-    )
-    attn_rows = attn_heads.astype(jnp.bfloat16).reshape(seq_len, q_heads * HD)
-    attn_branch = lax.psum_scatter(
-        tail_product(attn_rows, out_weight).astype(jnp.bfloat16),
-        "tensor",
-        scatter_dimension=0,
-        tiled=True,
-    ).astype(jnp.float32)
-    resid = input_rows + attn_branch
-    inverse_two = norm_rows(resid)
-    normed_two = resid * inverse_two
-    full_two = lax.all_gather(
-        (normed_two * mlp_gain).astype(jnp.bfloat16), "tensor", axis=0, tiled=True
-    )
-    (gate_weight, up_weight, down_weight), _ = gather_weights(
-        [w_gate, w_up, w_down.T], [], [1, 1, 1], dp, 1
-    )
-    gate_rows = product(full_two, gate_weight)
-    up_rows = product(full_two, up_weight)
-    gate_sig = jax.nn.sigmoid(gate_rows)
-    act_rows = (gate_rows * gate_sig * up_rows).astype(jnp.bfloat16)
+    pair = jnp.stack([query_gain, key_gain])
+    signed = jnp.concatenate([-sine_table[:, : HD // 2], sine_table[:, HD // 2 :]], axis=1)
+    rope_tab = jnp.stack([cosine_table, signed])
+    weights, attn_rows, resid, full_two, act = forward_block(
+        jnp.stack([w_gate, w_up, w_down.T]),
+        projected,
+        out_weight,
+        tokens,
+        full_cot,
+        rope_tab,
+        seg_ids[0],
+        pair,
+        mlp_gain[None, :],
+        q_heads,
+        kv_heads,
+        dp,
+    )
     mlp_branch = lax.psum_scatter(
-        tail_product(act_rows, down_weight).astype(jnp.bfloat16),
+        tail_product(act[2], weights[2 * model :]).astype(jnp.bfloat16),
         "tensor",
         scatter_dimension=0,
         tiled=True,
     ).astype(jnp.float32)
     result_rows = (resid + mlp_branch).astype(jnp.bfloat16)
-    cot_rows = cotangent.astype(jnp.float32)
-    d_act = product(full_cot, down_weight)
-    d_gate = (d_act * up_rows * gate_sig * (1.0 + gate_rows * (1.0 - gate_sig))).astype(
-        jnp.bfloat16
-    )
-    d_up = (d_act * gate_rows * gate_sig).astype(jnp.bfloat16)
-    grad_gate, grad_up, grad_down = reduce_grads(
-        [full_two.T, full_cot.T], [d_gate, d_up, act_rows], [(0, 0), (0, 1), (1, 2)], dp, 2
-    )
-    d_normed_two = lax.psum_scatter(
-        (tail_product(d_gate, gate_weight) + tail_product(d_up, up_weight)).astype(jnp.bfloat16),
-        "tensor",
-        scatter_dimension=0,
-        tiled=True,
-    ).astype(jnp.float32)
-    mlp_gain_part = jnp.sum(d_normed_two * normed_two, axis=0)
-    d_resid = cot_rows + norm_back(d_normed_two * mlp_gain, normed_two, inverse_two)
-    full_resid = lax.all_gather(d_resid.astype(jnp.bfloat16), "tensor", axis=0, tiled=True)
-    d_attn = (
-        product(full_resid, out_weight)
-        .astype(jnp.bfloat16)
-        .reshape(seq_len, kv_heads, per_group, HD)
-    )
-    scores_again = (
-        jnp.einsum("sgrd,tgd->grst", query_rot, key_all, preferred_element_type=jnp.float32)
-        * score_scale
-    )
-    probs_again = jnp.where(allowed, jnp.exp(scores_again - log_totals), 0.0)
-    d_value_all = jnp.einsum(
-        "grst,sgrd->tgd",
-        probs_again.astype(jnp.bfloat16),
-        d_attn,
-        preferred_element_type=jnp.float32,
-    )
-    d_probs = jnp.einsum("sgrd,tgd->grst", d_attn, value_all, preferred_element_type=jnp.float32)
-    row_delta = jnp.sum(probs_again * d_probs, axis=-1, keepdims=True)
-    d_scores = (probs_again * (d_probs - row_delta)).astype(jnp.bfloat16)
-    d_query = (
-        jnp.einsum("grst,tgd->sgrd", d_scores, key_all, preferred_element_type=jnp.float32)
-        * score_scale
-    )
-    d_key = (
-        jnp.einsum("grst,sgrd->tgd", d_scores, query_rot, preferred_element_type=jnp.float32)
-        * score_scale
-    )
-    d_value = d_value_all.astype(jnp.bfloat16).reshape(seq_len, kv_heads * HD)
-    d_query_norm = rotate_back(d_query.reshape(seq_len, q_heads, HD), cosine_heads, sine_heads)
-    d_key_norm = rotate_back(d_key, cosine_heads, sine_heads)
-    query_gain_part = jnp.sum(d_query_norm * query_hat, axis=(0, 1))
-    key_gain_part = jnp.sum(d_key_norm * key_hat, axis=(0, 1))
-    d_query_raw = (
-        norm_back(d_query_norm * query_gain, query_hat, query_inverse)
-        .astype(jnp.bfloat16)
-        .reshape(seq_len, q_heads * HD)
-    )
-    d_key_raw = (
-        norm_back(d_key_norm * key_gain, key_hat, key_inverse)
-        .astype(jnp.bfloat16)
-        .reshape(seq_len, kv_heads * HD)
-    )
-    d_projected = jnp.concatenate([d_query_raw, d_key_raw, d_value], axis=1)
+    grads, d_projected, full_resid, d_resid, mlp_gain_part, qk_part = backward_block(
+        jnp.stack([full_two.T, full_cot.T]),
+        act,
+        weights,
+        projected,
+        out_weight,
+        cotangent,
+        resid,
+        rope_tab,
+        seg_ids[0],
+        pair,
+        mlp_gain[None, :],
+        q_heads,
+        kv_heads,
+        dp,
+    )
+    grad_gate, grad_up, grad_down = grads[0], grads[1], grads[2]
+    mlp_gain_part = mlp_gain_part[0]
+    query_gain_part, key_gain_part = qk_part[0], qk_part[1]
     grad_qkv, grad_out = reduce_grads(
         [full_one.T, full_resid.T], [d_projected, attn_rows], [(0, 0), (1, 1)], dp, 3
     )

time: 923 us -> 694 us (0.75)
  matrix products: 121 us -> 31.7 us
  waiting for transfers between devices: 85.3 us -> 0.04 us
  local copies, waits for them, and re-layouts: 84.1 us -> 35.7 us
  other arithmetic: 49.4 us -> 20.2 us
  Pallas kernels: 521 us -> 543 us
    pallas_call x0 -> x2, Pallas kernels: none -> 403 us  [the longest x1 204 us: forward_block(): pl.pallas_call(functools.partial(forward_kernel, n, (q_heads, kv_heads, s...]
    pallas_call x2 -> x1, Pallas kernels: 264 us -> 69.5 us  [reduce_grads(): pl.pallas_call(functools.partial(reduce_kernel, n, tuple(pairs)), out_sha...]
    pallas_call x2 -> x1, Pallas kernels: 257 us -> 71.4 us  [gather_weights(): pl.pallas_call(functools.partial(gather_kernel, n, tuple(parts), count, l...]
    reduce_scatter x3 -> x1, waiting for transfers between devices: 59.6 us -> 0.01 us  [on_device(): lax.psum_scatter(tail_product(act[2], weights[2 * model:]).astype(jnp.bfl...]
    dot_general x5 -> x1, matrix products: 50.8 us -> 9.78 us  [product(): return jnp.dot(left, right, preferred_element_type=jnp.float32)]
    all_gather x2 -> x0, waiting for transfers between devices: 25.6 us -> none  [the longest x1 25.6 us: on_device(): lax.all_gather(d_resid.astype(jnp.bfloat16), 'tensor', axis=0, tiled=True)]
    unnamed x161 -> x36, local copies, waits for them, and re-layouts: 32.5 us -> 7.09 us
    dot_general x5 -> x2, matrix products: 46.6 us -> 21.9 us  [tail_product(): lax.dot_general(left, right, (((1,), (1,)), ((), ())), preferred_element_...]
  transfers between devices with their start and end apart: 6 -> 2, of which waited for: 3 -> 0; matrix products, arithmetic and copies ran while one was open for 5% -> 5% of each run, Pallas kernels for 49% -> 10%
where the time goes in v2:
time: 694 us; the launch traced here: 685 us
  Pallas kernels  543 us (78%)
  blocking collectives  38.8 us (6%)
  local copies, waits for them, and re-layouts  35.7 us (5%)
  matrix products  31.7 us (5%)
  other arithmetic  20.2 us (3%)
  between operations  14.7 us (2%)
    pallas_call x1, Pallas kernels, forward_block(): pl.pallas_call(functools.partial(forward_kernel, n, (q_heads, kv_heads, s...  204 us
    pallas_call x1, Pallas kernels, backward_block(): pl.pallas_call(functools.partial(backward_kernel, n, (q_heads, kv_heads,...  198 us
    pallas_call x1, Pallas kernels, gather_weights(): pl.pallas_call(functools.partial(gather_kernel, n, tuple(parts), count, l...  71.4 us
    pallas_call x1, Pallas kernels, reduce_grads(): pl.pallas_call(functools.partial(reduce_kernel, n, tuple(pairs)), out_sha...  69.5 us
    psum x1, blocking collectives, on_device(): lax.psum(jnp.concatenate([attn_gain_part, mlp_gain_part, query_gain_part,...  38.8 us
    dot_general x2, matrix products, tail_product(): lax.dot_general(left, right, (((1,), (1,)), ((), ())), preferred_element_...  21.9 us
  transfers between devices with their start and end apart: 2, of which 0 were waited for; matrix products, arithmetic and copies ran while one was open for 5% of the time, Pallas kernels for 10%

profile of v2, /device:TPU:0, one launch (start us, length us, event | category | flops | bytes accessed | tf_op | source)
XLA Modules:
  0.0 684.6 jit_solution(2734597898976573692)
XLA Ops:
  7.2 0.0 reduce-scatter.5.cloned.1.call-start
  7.2 1.8 copy.45
  9.0 1.9 pad_maximum_fusion.2.refs_0_
  11.0 0.7 fusion.27
  11.6 0.6 broadcast_in_dim.2.refs_2_
  12.3 71.4 %shard_map.220 = (bf16[2048,2048]{1,0:T(8,128)(2,1)}, bf16[2048,1024]{1,0:T(8,128)(2,1)}, f32[256,384]{1,0:T(8,128)}, bf16[512,2048]{1,0:T(8,128)(2,1)}, bf16[512,2048]{1,0:T(8,128)(2,1)}) custom-call(bf16[128,2048]{1,0:T(8,128)(2,1)} %pad_maximum_fusion.2.refs_0_, bf16[128,1024]{1,0:T(8,128)(2,1)} %bitcast.52, f32[16,384]{1,0:T(8,128)} %broadcast_in_dim.2.refs_2_, ...), custom_call_target="tpu_custom_call" | custom-call | tf_op jit(solution)/shard_map/pallas_call | solution.py:144
  83.6 1.1 reshape.69
  84.8 0.6 slice_bitcast_fusion.4
  85.5 2.9 copy.46
  88.3 0.5 fusion.2
  88.9 0.2 copy-done.12
  89.0 0.2 convert_reduce_fusion
  89.3 0.1 stack.46
  89.4 0.1 stack.47
  89.5 0.9 copy.47.refs_6_.refs_8_
  90.3 1.4 copy.44
  91.7 3.9 copy.49
  95.6 1.0 multiply_cosine_fusion
  96.6 0.2 maximum_bitcast_fusion
  96.8 0.8 pad_maximum_fusion.3.refs_5_.refs_7_
  97.7 0.6 pad_maximum_fusion.5.refs_8_.refs_10_
  98.3 9.8 %fusion.22.refs_1_.refs_3_ = f32[512,2048]{1,0:T(8,128)} fusion(bf16[2048,2048]{1,0:T(8,128)(2,1)} %get-tuple-element.32, bf16[512,2048]{0,1:T(8,128)(2,1)S(1)} %copy.46, f32[2048]{0:T(1024)S(1)} %bitcast.56, f32[512]{0:T(512)S(1)} %add_rsqrt_fusion), kind=kOutput, calls=%fused_computation.32 | convolution fusion | flops 4299161600 | bytes 14690304 | tf_op jit(solution)/shard_map/dot_general | solution.py:302
  108.1 1.6 pad_maximum_fusion.1.refs_0_
  109.7 204.5 %shard_map.221 = (bf16[6144,3072]{1,0:T(8,128)(2,1)}, bf16[512,1024]{1,0:T(8,128)(2,1)}, f32[256,2048]{1,0:T(8,128)}, bf16[512,2048]{1,0:T(8,128)(2,1)}, bf16[3,512,3072]{2,1,0:T(8,128)(2,1)}) custom-call(bf16[3,128,3072]{2,1,0:T(8,128)(2,1)} %pad_maximum_fusion.1.refs_0_, f32[512,2048]{1,0:T(8,128)} %fusion.22.refs_1_.refs_3_, ...), custom_call_target="tpu_custom_call" | custom-call | tf_op jit(solution)/shard_map/pallas_call | solution.py:634
  314.2 4.1 copy.48
  318.3 4.0 pad_maximum_fusion.refs_0_
  322.3 198.0 %shard_map.222 = (f32[3,128,3072]{2,1,0:T(8,128)}, bf16[512,2048]{1,0:T(8,128)(2,1)}, bf16[512,2048]{1,0:T(8,128)(2,1)}, f32[256,2048]{1,0:T(8,128)}, f32[1,2048]{1,0:T(1,128)}, /*index=5*/f32[8,128]{1,0:T(8,128)}) custom-call(bf16[2,2048,512]{2,1,0:T(8,128)(2,1)} %pad_maximum_fusion.refs_0_, bf16[3,512,3072]{2,1,0:T(8,128)(2,1)} %get-tuple-element.36.refs_1_, ...), custom_call_target="tpu_custom_call" | custom-call | tf_op jit(solution)/shard_map/pallas_call | solution.py:988
  520.3 10.0 %convolution_convert_fusion = bf16[512,2048]{1,0:T(8,128)(2,1)} fusion(bf16[512,2048]{1,0:T(8,128)(2,1)} %get-tuple-element.40.refs_2_, bf16[2048,2048]{1,0:T(8,128)(2,1)} %get-tuple-element.32), kind=kOutput, calls=%fused_computation.11 | convolution fusion | flops 4296015872 | bytes 12582912 | tf_op jit(solution)/shard_map/dot_general | solution.py:312
  530.3 0.0 reduce-scatter.5.cloned.1.call-update
  530.3 0.0 reduce-scatter.3.cloned.1.call-start
  530.4 11.9 %fusion.7 = bf16[512,2048]{1,0:T(8,128)(2,1)} fusion(bf16[6144,3072]{1,0:T(8,128)(2,1)} %get-tuple-element.37.refs_2_, bf16[3,512,3072]{2,1,0:T(8,128)(2,1)} %get-tuple-element.36.refs_1_), kind=kOutput, calls=%fused_computation.10 | convolution fusion | flops 6443499520 | bytes 17825792 | tf_op jit(solution)/shard_map/dot_general | solution.py:312
  542.3 0.0 reduce-scatter.3.cloned.1.call-update
  542.4 4.1 copy.51
  546.5 1.9 fusion.21.refs_0_
  548.4 69.5 %shard_map.223 = (f32[128,2048]{1,0:T(8,128)}, f32[128,1024]{1,0:T(8,128)}) custom-call(bf16[2048,512]{1,0:T(8,128)(2,1)} %fusion.21.refs_0_, bf16[2048,512]{1,0:T(8,128)(2,1)} %bitcast.48, bf16[512,2048]{1,0:T(8,128)(2,1)} %get-tuple-element.40.refs_2_, bf16[512,1024]{1,0:T(8,128)(2,1)} %get-tuple-element.42.refs_3_), custom_call_target="tpu_custom_call" | custom-call | tf_op jit(solution)/shard_map/pallas_call | solution.py:278
  617.9 2.0 copy.52
  620.0 1.9 slice.57
  621.9 4.5 slice_bitcast_fusion
  626.3 1.6 copy.53
  628.0 0.3 fusion.19
  628.3 0.9 slice_bitcast_fusion.6
  629.1 1.9 fusion.28
  631.0 2.0 fusion.20
  633.0 38.8 %psum.7 = f32[4352]{0:T(1024)S(1)} all-reduce(f32[4352]{0:T(1024)S(1)} %pad_maximum_fusion.4), channel_id=1, replica_groups=mesh['dp'=16,'tensor'=2] {'dp','tensor'}, use_global_device_ids=true, to_apply=%region_7.8 | all-reduce | flops 4352 | bytes 34816 | tf_op jit(solution)/shard_map/psum | solution.py:1125
  671.9 0.6 dynamic_slice.11
  672.5 0.6 fusion.29
  673.1 2.6 add_convert_fusion
  675.7 1.7 fusion.17
  (41 shorter events, 0.2 us)
Async XLA Ops:
  7.2 623.8 %reduce-scatter.5.cloned.1.call-start = ((), (), s32[]{:S(2)}) async-start(), calls=%async_computation.3 | async-start | bytes 3145728 | tf_op jit(solution)/shard_map/reduce_scatter | solution.py:1115
  85.4 12.8 %copy-start.9 = (f32[16,1,128]{2,1,0:T(1,128)}, f32[16,1,128]{2,1,0:T(1,128)S(1)}, u32[]{:S(2)}) copy-start(f32[16,1,128]{2,1,0:T(1,128)S(1)} %get-tuple-element.94) | copy-start | bytes 24580
  88.3 9.9 %copy-start.1 = (bf16[512,2048]{0,1:T(8,128)(2,1)}, bf16[512,2048]{0,1:T(8,128)(2,1)S(1)}, u32[]{:S(2)}) copy-start(bf16[512,2048]{0,1:T(8,128)(2,1)S(1)} %copy.46) | copy-start | bytes 6291460
  88.3 0.7 copy-start.12
  88.9 9.4 %copy-start.13 = (f32[512]{0:T(512)}, f32[512]{0:T(512)S(1)}, u32[]{:S(2)}) copy-start(f32[512]{0:T(512)S(1)} %add_rsqrt_fusion) | copy-start | bytes 6148
  98.3 9.8 %copy-start.7 = (bf16[128,3072]{1,0:T(8,128)(2,1)S(1)}, bf16[128,3072]{1,0:T(8,128)(2,1)}, u32[]{:S(2)}) copy-start(bf16[128,3072]{1,0:T(8,128)(2,1)} %param.20) | copy-start | bytes 2359300
  98.3 9.8 %copy-start.8 = (bf16[128,3072]{1,0:T(8,128)(2,1)S(1)}, bf16[128,3072]{1,0:T(8,128)(2,1)}, u32[]{:S(2)}) copy-start(bf16[128,3072]{1,0:T(8,128)(2,1)} %param.19) | copy-start | bytes 2359300
  314.2 4.1 copy-start.4
  530.3 142.7 %reduce-scatter.3.cloned.1.call-start = ((), (), s32[]{:S(2)}) async-start(), calls=%async_computation.2 | async-start | bytes 3145728 | tf_op jit(solution)/shard_map/reduce_scatter | solution.py:1086
  542.3 4.2 copy-start.2
  542.4 4.1 copy-start.10
  542.4 4.1 copy-start.14
  626.3 1.6 copy-start
  626.3 4.6 copy-start.11
  628.0 5.1 copy-start.15
  628.0 45.1 %copy-start.3 = (f32[256,2048]{1,0:T(8,128)S(1)}, f32[256,2048]{1,0:T(8,128)}, u32[]{:S(2)}) copy-start(f32[256,2048]{1,0:T(8,128)} %get-tuple-element.35.refs_6_) | copy-start | bytes 6291460
  673.0 2.7 copy-start.5
  673.1 2.6 copy-start.6
Sparse Core Ops, SparseCore 0:
  530.5 30.3 reduce-scatter.4
  563.1 31.9 reduce-scatter.2

commit v3 on v2

--- a/solution.py
+++ b/solution.py
@@ -410,12 +410,35 @@
     return picked
 
 
+def flip_into(source, target, stage, stage_sem):
+    deep = stage.shape[1]
+    turns = source.shape[1] // deep
+
+    def put(i):
+        return pltpu.make_async_copy(
+            stage.at[i % 2], target.at[pl.ds(pl.multiple_of(i * deep, deep), deep)], stage_sem.at[i % 2]
+        )
+
+    def one(i, carry):
+        @pl.when(i >= 2)
+        def _():
+            put(i - 2).wait()
+
+        stage[i % 2] = source[:, pl.ds(pl.multiple_of(i * deep, deep), deep)].T
+        put(i).start()
+        return carry
+
+    lax.fori_loop(0, turns, one, 0)
+    put(turns - 2).wait()
+    put(turns - 1).wait()
+
+
 def forward_kernel(n, dims, *refs):
     (
-        shards, qkv, out_weight, tokens, cot_full, tab, seg_col, seg_row, gains, mlp_gain,
-        weights, attn, resid, full_two, act,
-        kept, part, peer, acc, blocks,
-        own_sem, send_sem, recv_sem, give_sem, take_sem, swap_sem, load_sem,
+        shards, qkv, out_weight, tokens, full_one, cot_full, tab, seg_col, seg_row, gains, mlp_gain,
+        weights, attn, resid, flipped, act,
+        full_two, kept, part, peer, acc, blocks, stage,
+        own_sem, send_sem, recv_sem, give_sem, take_sem, swap_sem, load_sem, stage_sem,
     ) = refs
     q_heads, kv_heads, seq, block = dims
     pos, core = ring_place(n)
@@ -540,6 +563,9 @@
             def _():
                 with_left(block_columns(cot_full, chip, 2 * rows))
 
+    def flip(source, target):
+        flip_into(source, flipped.at[target], stage, stage_sem)
+
     groups = (qkv, tab, seg_col, seg_row, gains, attn, kept)
 
     def attend(first, last):
@@ -559,7 +585,11 @@
     send_part = remote(part, peer, swap_sem.at[0, 0], swap_sem.at[0, 1], twin)
     send_part.start()
     resid[...] = tokens[...].astype(jnp.float32) + tail_product(attn[ours, :], out_weight[...])
-    for event in range(2, 6):
+    service(2)
+    flip(full_one, 2)
+    service(3)
+    flip(cot_full, 1)
+    for event in range(4, 6):
         service(event)
     send_part.wait_recv()
     summed = resid[...] + peer[...].astype(jnp.float32)
@@ -573,6 +603,7 @@
     for event in range(6, ready):
         service(event)
     remote(part, full_two.at[theirs], swap_sem.at[1, 0], swap_sem.at[1, 1], twin).wait_recv()
+    flip(full_two, 0)
 
     def both(i, carry):
         service(ready + i)
@@ -623,7 +654,7 @@
             hand_own(w, side, core).wait_send()
 
 
-def forward_block(shards, qkv, out_weight, tokens, cot_full, tab, segments, gains, mlp_gain, q_heads, kv_heads, dp):
+def forward_block(shards, qkv, out_weight, tokens, full_one, cot_full, tab, segments, gains, mlp_gain, q_heads, kv_heads, dp):
     n = dp // 2
     count, rows, width = shards.shape
     seq, model = cot_full.shape
@@ -637,17 +668,19 @@
             shape((count * model, width), low),
             shape((seq, q_heads * HD), low),
             shape((half, model), jnp.float32),
-            shape((seq, model), low),
+            shape((3, model, seq), low),
             shape((count, seq, width), low),
         ],
-        in_specs=[place(vmem)] * 10,
-        out_specs=[place(pltpu.HBM)] + [place(vmem)] * 4,
+        in_specs=[place(vmem)] * 11,
+        out_specs=[place(pltpu.HBM), place(vmem), place(vmem), place(pltpu.HBM), place(vmem)],
         scratch_shapes=[
+            vmem((seq, model), low),
             vmem((2, seq, HD), low),
             vmem((half, model), low),
             vmem((half, model), low),
             vmem((count, seq, width), jnp.float32),
             vmem((2, 2 * rows, width // 2), low),
+            vmem((2, 256, seq), low),
             dma((count, 2)),
             dma((count, 2, n)),
             dma((count, 2, n)),
@@ -655,12 +688,13 @@
             dma((count, 2, n)),
             dma((2, 2)),
             dma((2,)),
+            dma((2,)),
         ],
         compiler_params=pltpu.CompilerParams(
             collective_id=1, has_side_effects=True, vmem_limit_bytes=67043328
         ),
     )(
-        shards, qkv, out_weight, tokens, cot_full, tab,
+        shards, qkv, out_weight, tokens, full_one, cot_full, tab,
         segments.reshape(seq, 1), segments.reshape(1, seq), gains, mlp_gain,
     )
 
@@ -705,12 +739,12 @@
             kept[2, :width, :] += d_values
         total, raw = undo(kept[0], q_hat, q_inverse, gains[0:1, :], cosine, sine)
         sums[0:1, :] += total
-        d_proj[:, head_at(head)] = raw
+        d_proj[0, :, head_at(head)] = raw
     k_inverse, k_hat, _ = prepared(heads[per_group], gains[1:2, :], cosine, sine)
     total, raw = undo(kept[1] * scale, k_hat, k_inverse, gains[1:2, :], cosine, sine)
     sums[1:2, :] += total
-    d_proj[:, head_at(q_heads + group)] = raw
-    d_proj[:, head_at(q_heads + kv_heads + group)] = kept[2].astype(low)
+    d_proj[1, :, head_at(group)] = raw
+    d_proj[1, :, head_at(kv_heads + group)] = kept[2].astype(low)
 
 
 def reducer(n, pos, core, nexts, mate, refs, left_of):
@@ -740,7 +774,7 @@
         for side in range(2):
             start = pl.multiple_of(chip_at(owner_of(side, step), n) * 2 * rows, 2 * rows)
             left = lefts[left_of(m), pl.ds(start, 2 * rows), :]
-            tile = wide // 3
+            tile = min(512, wide)
 
             def one(i, carry):
                 there = pl.multiple_of(i * tile, tile)
@@ -749,7 +783,7 @@
                 )
                 return carry
 
-            lax.fori_loop(0, 3, one, 0)
+            lax.fori_loop(0, wide // tile, one, 0)
 
             @pl.when(step >= 1)
             def _():
@@ -832,23 +866,29 @@
 
 def backward_kernel(n, dims, *refs):
     (
-        lefts, act, weights, qkv, out_weight, cot, resid, tab, seg_col, seg_row, gains, mlp_gain,
-        grads, d_proj, d_full, d_resid, mlp_sum, qk_sum,
-        gate_block, up_block, own, part, peer, d_attn, heads, kept,
-        swap_sem, load_sem, head_sem,
-    ) = refs[:29]
+        flipped, act, weights, qkv, attn, out_weight, cot, resid, tab, seg_col, seg_row, gains, mlp_gain,
+        grads, d_proj, d_flip, d_resid, mlp_sum, qk_sum,
+        lefts, d_full, gate_block, up_block, own, part, peer, d_attn, heads, kept, stage,
+        swap_sem, load_sem, head_sem, left_sem, stage_sem,
+    ) = refs[:35]
     q_heads, kv_heads, seq, block = dims
     pos, core = ring_place(n)
     lane = lax.axis_index("tensor")
     nexts = (at((pos + 1) % n, core, n), at((pos + n - 1) % n, core, n))
     mate = at(pos, 1 - core, n)
     twin = (lax.axis_index("dp"), 1 - lane)
+    fetch_lefts = pltpu.make_async_copy(flipped.at[pl.ds(0, 2)], lefts, left_sem.at[0])
+    fetch_lefts.start()
+    fetch_attn = pltpu.make_async_copy(attn, d_proj.at[2], left_sem.at[1])
+    fetch_attn.start()
     meet((*nexts, mate, twin))
+    fetch_lefts.wait()
+    fetch_attn.wait()
     count = act.shape[0]
     model = resid.shape[1]
     half = seq // 2
     early, event, finish = reducer(
-        n, pos, core, nexts, mate, (lefts, act, grads, *refs[29:]), lambda m: m // 2
+        n, pos, core, nexts, mate, (lefts, act, grads, *refs[35:]), lambda m: m // 2
     )
     for m in range(count):
         early(m, 0)
@@ -945,6 +985,7 @@
         d_attn[:, there] = product(d_full[...], out_weight[:, there]).astype(jnp.bfloat16)
     event(done)
     done = done + 1
+    flip_into(d_full, d_flip, stage, stage_sem)
     per_group = q_heads // kv_heads
     qk_sum[...] = jnp.zeros_like(qk_sum)
 
@@ -975,7 +1016,7 @@
 
 
 def backward_block(
-    lefts, act, weights, qkv, out_weight, cot, resid, tab, segments, gains, mlp_gain, q_heads, kv_heads, dp
+    flipped, act, weights, qkv, attn, out_weight, cot, resid, tab, segments, gains, mlp_gain, q_heads, kv_heads, dp
 ):
     n = dp // 2
     count, seq, width = act.shape
@@ -989,15 +1030,17 @@
         functools.partial(backward_kernel, n, (q_heads, kv_heads, seq, seq // 2)),
         out_shape=[
             shape((count, rows, width), jnp.float32),
-            shape((seq, (q_heads + 2 * kv_heads) * HD), low),
-            shape((seq, model), low),
+            shape((3, seq, q_heads * HD), low),
+            shape((model, seq), low),
             shape((half, model), jnp.float32),
             shape((1, model), jnp.float32),
             shape((8, HD), jnp.float32),
         ],
-        in_specs=[place(vmem)] * 2 + [place(pltpu.HBM)] * 2 + [place(vmem)] * 8,
-        out_specs=[place(pltpu.HBM)] + [place(vmem)] * 5,
+        in_specs=[place(pltpu.HBM), place(vmem)] + [place(pltpu.HBM)] * 3 + [place(vmem)] * 8,
+        out_specs=[place(pltpu.HBM), place(vmem), place(pltpu.HBM)] + [place(vmem)] * 3,
         scratch_shapes=[
+            vmem((2, model, seq), low),
+            vmem((seq, model), low),
             vmem((deep, width), low),
             vmem((deep, width), low),
             vmem((half, model), jnp.float32),
@@ -1006,18 +1049,259 @@
             vmem((seq, q_heads * HD), low),
             vmem((q_heads // kv_heads + 2, seq, HD), jnp.float32),
             vmem((3, seq, HD), jnp.float32),
+            vmem((2, 256, seq), low),
             dma((2, 2)),
             dma((2,)),
             dma((q_heads // kv_heads + 2,)),
+            dma((2,)),
+            dma((2,)),
             *reduce_scratch(n, count, rows, width // 2),
         ],
         compiler_params=pltpu.CompilerParams(
             collective_id=2, has_side_effects=True, vmem_limit_bytes=67043328
         ),
     )(
-        lefts, act, weights, qkv, out_weight, cot, resid, tab,
+        flipped, act, weights, qkv, attn, out_weight, cot, resid, tab,
         segments.reshape(seq, 1), segments.reshape(1, seq), gains, mlp_gain,
     )
+
+
+def closing_kernel(n, *refs):
+    (
+        flipped, d_flip, d_proj, qkv_weight, weights, act, tokens, resid, d_resid, attn_gain, mlp_sum, qk_sum,
+        grads, result, input_grad, gain_out,
+        lefts, acts, first_block, second_block, own, part, peer, attn_sum, table, others, inbox,
+        swap_sem, load_sem, first_sem, second_sem, trade_sem, post_sem, mail_sem,
+    ) = refs[:34]
+    pos, core = ring_place(n)
+    me = lax.axis_index("dp")
+    lane = lax.axis_index("tensor")
+    nexts = (at((pos + 1) % n, core, n), at((pos + n - 1) % n, core, n))
+    mate = at(pos, 1 - core, n)
+    twin = (me, 1 - lane)
+    fetches = [
+        pltpu.make_async_copy(flipped.at[2], lefts.at[0], load_sem.at[0]),
+        pltpu.make_async_copy(d_flip, lefts.at[1], load_sem.at[1]),
+        pltpu.make_async_copy(act.at[2], acts, load_sem.at[2]),
+    ]
+    for fetch in fetches:
+        fetch.start()
+    barrier = pltpu.get_barrier_semaphore()
+
+    def greet(o, carry):
+        pl.semaphore_signal(barrier, inc=1, device_id=at((pos + o) % n, core, n), device_id_type=MESH)
+        return carry
+
+    lax.fori_loop(1, n, greet, 0)
+    for other in (mate, twin):
+        pl.semaphore_signal(barrier, inc=1, device_id=other, device_id_type=MESH)
+    pl.semaphore_wait(barrier, n + 1)
+    for fetch in fetches:
+        fetch.wait()
+    count, seq, width = d_proj.shape
+    half, model = resid.shape
+    early, event, finish = reducer(
+        n, pos, core, nexts, mate, (lefts, d_proj, grads, *refs[34:]), lambda m: m // 2
+    )
+    for m in range(count):
+        early(m, 0)
+    for m in range(count):
+        event(m)
+    theirs = pl.ds(pl.multiple_of((1 - lane) * half, half), half)
+    ours = pl.ds(pl.multiple_of(lane * half, half), half)
+    deep = first_block.shape[1]
+    turns = model // deep
+
+    def stream(source, offset, block, sem):
+        def fetch(i):
+            return pltpu.make_async_copy(
+                source.at[pl.ds(pl.multiple_of(offset + i * deep, deep), deep)], block.at[i % 2], sem.at[i % 2]
+            )
+
+        return fetch
+
+    first_fetch = stream(qkv_weight, 0, first_block, first_sem)
+    second_fetch = stream(weights, 2 * model, second_block, second_sem)
+    first_fetch(0).start()
+
+    def narrow(which, fetch, block, rows_of, every, base):
+        def one(i, carry):
+            @pl.when(i < turns - 1)
+            def _():
+                fetch(i + 1).start()
+
+            fetch(i).wait()
+            there = pl.ds(pl.multiple_of(i * deep, deep), deep)
+            for rows, target in ((theirs, part), (ours, own)):
+                total = None
+                for left, start in rows_of(rows):
+                    gained = tail_product(left, block[i % 2, :, pl.ds(start, left.shape[1])])
+                    total = gained if total is None else total + gained
+                target[which, :, there] = total.astype(target.dtype)
+
+            @pl.when(i % every == every - 1)
+            def _():
+                event(base + i // every)
+
+            return carry
+
+        lax.fori_loop(0, turns, one, 0)
+
+    narrow(
+        0, first_fetch, first_block,
+        lambda rows: [(d_proj[0, rows, :], 0), (d_proj[1, rows, :], width)], 4, count,
+    )
+    sends = [remote(part.at[i], peer.at[i], swap_sem.at[i, 0], swap_sem.at[i, 1], twin) for i in range(2)]
+    sends[0].start()
+    second_fetch(0).start()
+    done = count + turns // 4
+    narrow(1, second_fetch, second_block, lambda rows: [(acts[rows, :], 0)], 2, done)
+    sends[1].start()
+    done = done + turns // 2
+
+    def events(number):
+        nonlocal done
+        for e in range(done, done + number):
+            event(e)
+        done = done + number
+
+    events(4)
+    sends[0].wait_recv()
+    strip = 32
+
+    def norm_strip(i, carry):
+        there = pl.ds(pl.multiple_of(i * strip, strip), strip)
+        incoming = own[0, there, :] + peer[0, there, :].astype(jnp.float32)
+        values = tokens[there, :].astype(jnp.float32)
+        inverse = row_scale(values)
+        normed = values * inverse
+        scaled = incoming * attn_gain[...]
+        change = d_resid[there, :] + inverse * (
+            scaled - normed * jnp.mean(scaled * normed, axis=-1, keepdims=True)
+        )
+        input_grad[there, :] = change.astype(jnp.bfloat16)
+        total = jnp.sum(incoming * normed, axis=0, keepdims=True)
+
+        @pl.when(i == 0)
+        def _():
+            attn_sum[...] = total
+
+        @pl.when(i > 0)
+        def _():
+            attn_sum[...] += total
+
+        return carry
+
+    lax.fori_loop(0, half // strip, norm_strip, 0)
+    events(1)
+    dp = 2 * n
+    share, head_share = model // dp, 2 * HD // dp
+    table[...] = jnp.zeros_like(table)
+    for d in range(dp):
+        start = d * share // 128 * 128
+        row = d * head_share // HD
+        table[d, 0:1, :] = attn_sum[:, start : start + 128]
+        table[d, 1:2, :] = mlp_sum[:, start : start + 128]
+        table[d, 2:3, :] = qk_sum[row : row + 1, :]
+    for i, partner in enumerate((twin, mate)):
+        trade = remote(table, others.at[i], trade_sem.at[i, 0], trade_sem.at[i, 1], partner)
+        trade.start()
+        events(1)
+        trade.wait()
+        table[...] += others[i]
+
+    def mail(o, target):
+        return remote(table.at[target], inbox.at[o], post_sem.at[o], mail_sem.at[o], at((pos + o) % n, core, n))
+
+    def post(o, carry):
+        mail(o, chip_at((pos + o) % n, n) * 2 + core).start()
+        return carry
+
+    lax.fori_loop(1, n, post, 0)
+    events(3)
+    sends[1].wait_recv()
+
+    def last_strip(i, carry):
+        there = pl.ds(pl.multiple_of(i * strip, strip), strip)
+        result[there, :] = (
+            resid[there, :] + (own[1, there, :] + peer[1, there, :].astype(jnp.float32))
+        ).astype(jnp.bfloat16)
+        return carry
+
+    lax.fori_loop(0, half // strip, last_strip, 0)
+    gain_out[...] = table[me]
+
+    def collect(o, carry):
+        mail(o, 0).wait_recv()
+        gain_out[...] += inbox[o]
+        return carry
+
+    lax.fori_loop(1, n, collect, 0)
+
+    def rest(e, carry):
+        event(e)
+        return carry
+
+    lax.fori_loop(done, count * n, rest, 0)
+    finish()
+    for send in sends:
+        send.wait_send()
+
+    def sent(o, carry):
+        mail(o, 0).wait_send()
+        return carry
+
+    lax.fori_loop(1, n, sent, 0)
+
+
+def closing_block(
+    flipped, d_flip, d_proj, qkv_weight, weights, act, tokens, resid, d_resid, attn_gain, mlp_sum, qk_sum, dp
+):
+    n = dp // 2
+    count, seq, width = d_proj.shape
+    half, model = resid.shape
+    hidden = act.shape[2]
+    rows = model // dp
+    deep = 256
+    low, dma, vmem = jnp.bfloat16, pltpu.SemaphoreType.DMA, pltpu.VMEM
+    shape = jax.ShapeDtypeStruct
+    place = lambda kind: pl.BlockSpec(memory_space=kind)
+    hbm = pltpu.HBM
+    return pl.pallas_call(
+        functools.partial(closing_kernel, n),
+        out_shape=[
+            shape((count, rows, width), jnp.float32),
+            shape((half, model), low),
+            shape((half, model), low),
+            shape((8, 128), jnp.float32),
+        ],
+        in_specs=[place(k) for k in (hbm, hbm, vmem, hbm, hbm, hbm, *[vmem] * 6)],
+        out_specs=[place(hbm), place(vmem), place(vmem), place(vmem)],
+        scratch_shapes=[
+            vmem((2, model, seq), low),
+            vmem((seq, hidden), low),
+            vmem((2, deep, qkv_weight.shape[1]), low),
+            vmem((2, deep, hidden), low),
+            vmem((2, half, model), jnp.float32),
+            vmem((2, half, model), low),
+            vmem((2, half, model), low),
+            vmem((1, model), jnp.float32),
+            vmem((dp, 8, 128), jnp.float32),
+            vmem((2, dp, 8, 128), jnp.float32),
+            vmem((n, 8, 128), jnp.float32),
+            dma((2, 2)),
+            dma((3,)),
+            dma((2,)),
+            dma((2,)),
+            dma((2, 2)),
+            dma((n,)),
+            dma((n,)),
+            *reduce_scratch(n, count, rows, width // 2),
+        ],
+        compiler_params=pltpu.CompilerParams(
+            collective_id=3, has_side_effects=True, vmem_limit_bytes=67043328
+        ),
+    )(flipped, d_flip, d_proj, qkv_weight, weights, act, tokens, resid, d_resid, attn_gain, mlp_sum, qk_sum)
 
 
 def on_device(
@@ -1036,10 +1320,7 @@
     cotangent,
 ):
     dp = lax.axis_size("dp")
-    input_rows = tokens.astype(jnp.float32)
-    model = input_rows.shape[1]
-    inverse_one = norm_rows(input_rows)
-    normed_one = input_rows * inverse_one
+    model = tokens.shape[1]
     gain_row = jnp.concatenate(
         [
             jnp.pad(g.astype(jnp.float32), (0, 128 - g.shape[0]))
@@ -1069,11 +1350,12 @@
     pair = jnp.stack([query_gain, key_gain])
     signed = jnp.concatenate([-sine_table[:, : HD // 2], sine_table[:, HD // 2 :]], axis=1)
     rope_tab = jnp.stack([cosine_table, signed])
-    weights, attn_rows, resid, full_two, act = forward_block(
+    weights, attn_rows, resid, flipped, act = forward_block(
         jnp.stack([w_gate, w_up, w_down.T]),
         projected,
         out_weight,
         tokens,
+        full_one,
         full_cot,
         rope_tab,
         seg_ids[0],
@@ -1083,18 +1365,12 @@
         kv_heads,
         dp,
     )
-    mlp_branch = lax.psum_scatter(
-        tail_product(act[2], weights[2 * model :]).astype(jnp.bfloat16),
-        "tensor",
-        scatter_dimension=0,
-        tiled=True,
-    ).astype(jnp.float32)
-    result_rows = (resid + mlp_branch).astype(jnp.bfloat16)
-    grads, d_projected, full_resid, d_resid, mlp_gain_part, qk_part = backward_block(
-        jnp.stack([full_two.T, full_cot.T]),
+    grads, d_projected, d_flip, d_resid, mlp_sum, qk_sum = backward_block(
+        flipped,
         act,
         weights,
         projected,
+        attn_rows,
         out_weight,
         cotangent,
         resid,
@@ -1107,24 +1383,20 @@
         dp,
     )
     grad_gate, grad_up, grad_down = grads[0], grads[1], grads[2]
-    mlp_gain_part = mlp_gain_part[0]
-    query_gain_part, key_gain_part = qk_part[0], qk_part[1]
-    grad_qkv, grad_out = reduce_grads(
-        [full_one.T, full_resid.T], [d_projected, attn_rows], [(0, 0), (1, 1)], dp, 3
-    )
-    d_normed_one = lax.psum_scatter(
-        tail_product(d_projected, qkv_weight).astype(jnp.bfloat16),
-        "tensor",
-        scatter_dimension=0,
-        tiled=True,
-    ).astype(jnp.float32)
-    attn_gain_part = jnp.sum(d_normed_one * normed_one, axis=0)
-    input_grad = (d_resid + norm_back(d_normed_one * attn_gain, normed_one, inverse_one)).astype(
-        jnp.bfloat16
-    )
-    gain_sums = lax.psum(
-        jnp.concatenate([attn_gain_part, mlp_gain_part, query_gain_part, key_gain_part]),
-        ("dp", "tensor"),
+    late_grads, result_rows, input_grad, gain_sums = closing_block(
+        flipped,
+        d_flip,
+        d_projected,
+        qkv_weight,
+        weights,
+        act,
+        tokens,
+        resid,
+        d_resid,
+        attn_gain[None, :],
+        mlp_sum,
+        qk_sum,
+        dp,
     )
     me = lax.axis_index("dp")
     share = model // dp
@@ -1132,16 +1404,16 @@
     return (
         result_rows,
         input_grad,
-        grad_qkv[:, :q_width],
-        grad_qkv[:, q_width : q_width + kv_width],
-        grad_qkv[:, q_width + kv_width :],
-        grad_out.T,
+        late_grads[0],
+        late_grads[1, :, :kv_width],
+        late_grads[1, :, kv_width:],
+        late_grads[2].T,
         grad_gate,
         grad_up,
         grad_down.T,
-        lax.dynamic_slice(gain_sums, (me * share,), (share,)),
-        lax.dynamic_slice(gain_sums, (model + me * share,), (share,)),
-        lax.dynamic_slice(gain_sums, (2 * model + me * qk_share,), (qk_share,)),
+        lax.dynamic_slice(gain_sums, (0, me * share % 128), (1, share))[0],
+        lax.dynamic_slice(gain_sums, (1, me * share % 128), (1, share))[0],
+        lax.dynamic_slice(gain_sums, (2, me * qk_share % HD), (1, qk_share))[0],
     )
 
 

time: 694 us -> 616 us (0.89)
  blocking collectives: 38.8 us -> 0 us
  Pallas kernels: 543 us -> 565 us
  matrix products: 31.7 us -> 10.1 us
  local copies, waits for them, and re-layouts: 35.7 us -> 21.2 us
  between operations: 14.7 us -> 1.25 us
  other arithmetic: 20.2 us -> 9.84 us
    psum x1 -> x0, blocking collectives: 38.8 us -> none  [on_device(): lax.psum(jnp.concatenate([attn_gain_part, mlp_gain_part, query_gain_part,...]
    dot_general x2 -> x0, matrix products: 21.9 us -> none  [tail_product(): lax.dot_general(left, right, (((1,), (1,)), ((), ())), preferred_element_...]
    pallas_call x1, Pallas kernels: 69.5 us -> 91 us  [closing_block(): pl.pallas_call(functools.partial(closing_kernel, n), out_shape=[shape((co...]
    pallas_call x4 -> x0, local copies, waits for them, and re-layouts: 15 us -> none  [the longest x2 6.77 us: gather_weights(): pl.pallas_call(functools.partial(gather_kernel, n, tuple(parts), count, l...]
  transfers between devices with their start and end apart: 2 -> 0, of which waited for: 0 -> 0; matrix products, arithmetic and copies ran while one was open for 5% -> 0% of each run, Pallas kernels for 10% -> 0%
where the time goes in v3:
time: 616 us; the launch traced here: 607 us
  Pallas kernels  565 us (92%)
  local copies, waits for them, and re-layouts  21.2 us (3%)
  matrix products  10.1 us (2%)
  other arithmetic  9.84 us (2%)
    pallas_call x1, Pallas kernels, forward_block(): pl.pallas_call(functools.partial(forward_kernel, n, (q_heads, kv_heads, s...  204 us
    pallas_call x1, Pallas kernels, backward_block(): pl.pallas_call(functools.partial(backward_kernel, n, (q_heads, kv_heads,...  198 us
    pallas_call x1, Pallas kernels, closing_block(): pl.pallas_call(functools.partial(closing_kernel, n), out_shape=[shape((co...  91 us
    pallas_call x1, Pallas kernels, gather_weights(): pl.pallas_call(functools.partial(gather_kernel, n, tuple(parts), count, l...  71.4 us

profile of v3, /device:TPU:0, one launch (start us, length us, event | category | flops | bytes accessed | tf_op | source)
XLA Modules:
  0.0 606.9 jit_solution(16044523700594247658)
XLA Ops:
  0.6 1.9 pad_maximum_fusion.1.refs_0_
  2.6 1.8 copy.37
  4.4 0.7 fusion.6
  5.1 0.6 broadcast_in_dim.2.refs_2_
  5.7 71.4 %shard_map.220 = (bf16[2048,2048]{1,0:T(8,128)(2,1)}, bf16[2048,1024]{1,0:T(8,128)(2,1)}, f32[256,384]{1,0:T(8,128)}, bf16[512,2048]{1,0:T(8,128)(2,1)}, bf16[512,2048]{1,0:T(8,128)(2,1)}) custom-call(bf16[128,2048]{1,0:T(8,128)(2,1)} %pad_maximum_fusion.1.refs_0_, bf16[128,1024]{1,0:T(8,128)(2,1)} %bitcast.46, f32[16,384]{1,0:T(8,128)} %broadcast_in_dim.2.refs_2_, ...), custom_call_target="tpu_custom_call" | custom-call | tf_op jit(solution)/shard_map/pallas_call | solution.py:144
  77.0 0.0 copy-start
  77.1 1.3 reshape.57
  78.4 0.6 slice_bitcast_fusion.11
  79.0 2.1 fusion
  81.1 0.0 copy-done
  81.1 0.5 fusion.2.refs_4_
  81.6 0.0 copy-start.1
  81.6 0.0 copy-start.7
  81.7 10.1 %fusion.7.refs_1_.refs_3_ = f32[512,2048]{1,0:T(8,128)} fusion(bf16[512,2048]{1,0:T(8,128)(2,1)S(1)} %fusion.2.refs_4_, bf16[2048,2048]{1,0:T(8,128)(2,1)} %get-tuple-element.34.refs_3_), kind=kOutput, calls=%fused_computation.37 | convolution fusion | flops 4294967296 | bytes 14680064 | tf_op jit(solution)/shard_map/dot_general | solution.py:302
  91.8 0.0 copy-done.1
  91.8 0.0 copy-start.6
  91.8 0.0 copy-done.7
  91.8 0.2 convert_reduce_fusion
  92.0 0.0 copy-start.4
  92.1 0.0 copy-start.5
  92.1 1.0 multiply_cosine_fusion
  93.1 0.2 maximum_bitcast_fusion
  93.3 0.8 pad_maximum_fusion.2.refs_6_.refs_8_
  94.1 0.1 stack.37
  94.2 0.1 stack.38
  94.3 0.6 pad_maximum_fusion.3.refs_9_.refs_11_
  94.9 0.9 copy.38.refs_7_.refs_9_
  95.7 0.0 copy-done.6
  95.7 0.3 copy.36
  96.0 0.0 copy-done.4
  96.0 0.0 copy-done.5
  96.0 1.7 pad_maximum_fusion.refs_0_
  97.8 204.3 %shard_map.221 = (bf16[6144,3072]{1,0:T(8,128)(2,1)}, bf16[512,1024]{1,0:T(8,128)(2,1)}, f32[256,2048]{1,0:T(8,128)}, bf16[3,2048,512]{2,1,0:T(8,128)(2,1)}, bf16[3,512,3072]{2,1,0:T(8,128)(2,1)}) custom-call(bf16[3,128,3072]{2,1,0:T(8,128)(2,1)} %pad_maximum_fusion.refs_0_, f32[512,2048]{1,0:T(8,128)} %fusion.7.refs_1_.refs_3_, ...), custom_call_target="tpu_custom_call" | custom-call | tf_op jit(solution)/shard_map/pallas_call | solution.py:665
  302.1 197.8 %shard_map.222 = (f32[3,128,3072]{2,1,0:T(8,128)}, bf16[3,512,1024]{2,1,0:T(8,128)(2,1)}, bf16[2048,512]{1,0:T(8,128)(2,1)}, f32[256,2048]{1,0:T(8,128)}, f32[1,2048]{1,0:T(1,128)}, /*index=5*/f32[8,128]{1,0:T(8,128)}) custom-call(bf16[3,2048,512]{2,1,0:T(8,128)(2,1)} %get-tuple-element.37.refs_0_, bf16[3,512,3072]{2,1,0:T(8,128)(2,1)} %get-tuple-element.38.refs_1_.refs_5_, ...), custom_call_target="tpu_custom_call" | custom-call | tf_op jit(solution)/shard_map/pallas_call | solution.py:1029
  499.9 4.5 slice_bitcast_fusion
  504.4 1.6 copy.41
  506.0 91.0 %shard_map.223 = (f32[3,128,1024]{2,1,0:T(8,128)}, bf16[256,2048]{1,0:T(8,128)(2,1)}, bf16[256,2048]{1,0:T(8,128)(2,1)}, f32[8,128]{1,0:T(8,128)}) custom-call(bf16[3,2048,512]{2,1,0:T(8,128)(2,1)} %get-tuple-element.37.refs_0_, bf16[2048,512]{1,0:T(8,128)(2,1)} %get-tuple-element.42.refs_1_, bf16[3,512,1024]{2,1,0:T(8,128)(2,1)} %get-tuple-element.43.refs_2_, ...), custom_call_target="tpu_custom_call" | custom-call | tf_op jit(solution)/shard_map/pallas_call | solution.py:1270
  597.0 0.0 copy-start.3
  597.0 2.2 slice_bitcast_fusion.3
  599.2 0.0 copy-start.2
  599.2 1.0 copy.40
  600.2 1.9 slice_bitcast_fusion.5
  602.1 1.2 dynamic-slice_bitcast_fusion
  603.3 1.3 slice_bitcast_fusion.9
  604.5 0.0 copy-done.3
  604.5 1.0 copy.44
  605.5 0.0 copy-done.2
  605.5 1.0 copy.45
  (5 shorter events, 0.1 us)
Async XLA Ops:
  77.0 4.0 copy-start
  81.6 10.1 %copy-start.1 = (bf16[512,2048]{1,0:T(8,128)(2,1)}, bf16[512,2048]{1,0:T(8,128)(2,1)S(1)}, u32[]{:S(2)}) copy-start(bf16[512,2048]{1,0:T(8,128)(2,1)S(1)} %fusion.2.refs_4_) | copy-start | bytes 6291460
  81.6 10.1 %copy-start.7 = (s32[1,512]{1,0:T(1,128)S(1)}, s32[1,512]{1,0:T(1,128)}, u32[]{:S(2)}) copy-start(s32[1,512]{1,0:T(1,128)} %refs_10_.1) | copy-start | bytes 6148
  91.8 4.0 copy-start.6
  92.0 4.0 copy-start.4
  92.1 4.0 copy-start.5
  597.0 7.5 %copy-start.3 = (bf16[256,2048]{1,0:T(8,128)(2,1)S(1)}, bf16[256,2048]{1,0:T(8,128)(2,1)}, u32[]{:S(2)}) copy-start(bf16[256,2048]{1,0:T(8,128)(2,1)} %get-tuple-element.119) | copy-start | bytes 3145732
  599.2 6.3 %copy-start.2 = (bf16[256,2048]{1,0:T(8,128)(2,1)S(1)}, bf16[256,2048]{1,0:T(8,128)(2,1)}, u32[]{:S(2)}) copy-start(bf16[256,2048]{1,0:T(8,128)(2,1)} %get-tuple-element.120) | copy-start | bytes 3145732

commit v4 on v3

--- a/solution.py
+++ b/solution.py
@@ -42,260 +42,6 @@
     return pltpu.make_async_remote_copy(
         src_ref=src, dst_ref=dst, send_sem=send, recv_sem=recv, device_id=peer, device_id_type=MESH
     )
-
-
-def gather_kernel(n, parts, count, swaps, *refs):
-    shards = refs[:count]
-    halves = refs[count : count + swaps]
-    fulls = refs[count + swaps : 2 * count + swaps]
-    wholes = refs[2 * count + swaps : 2 * (count + swaps)]
-    own_sem, send_sem, recv_sem, give_sem, take_sem, swap_sem = refs[2 * (count + swaps) :]
-    pos, core = ring_place(n)
-    lane = lax.axis_index("tensor")
-    nexts = (at((pos + 1) % n, core, n), at((pos + n - 1) % n, core, n))
-    mate = at(pos, 1 - core, n)
-    twin = (lax.axis_index("dp"), 1 - lane)
-    meet((*nexts, mate, twin))
-    messages = [(w, part) for w in range(count) for part in range(parts[w])]
-
-    def sizes(w):
-        rows = shards[w].shape[0]
-        return rows, rows // 2, rows // 2 // parts[w]
-
-    def spot(w, owner, who, side, part):
-        rows, half, piece = sizes(w)
-        start = (chip_at(owner, n) * 2 + who) * rows + (side * half + part * piece)
-        return fulls[w].at[pl.ds(pl.multiple_of(start, piece), piece)]
-
-    def shard_of(w, who):
-        rows = shards[w].shape[0]
-        return fulls[w].at[pl.ds(pl.multiple_of((chip_at(pos, n) * 2 + who) * rows, rows), rows)]
-
-    def swap_spot(s, which):
-        rows = halves[s].shape[0]
-        return wholes[s].at[pl.ds(pl.multiple_of(which * rows, rows), rows)]
-
-    for k, (w, part) in enumerate(messages):
-        rows, half, piece = sizes(w)
-        for side in range(2):
-            src = shards[w].at[pl.ds(side * half + part * piece, piece)]
-            remote(
-                src, spot(w, pos, core, side, part), send_sem.at[k, side, 0], recv_sem.at[k, side, 0], nexts[side]
-            ).start()
-    for s in range(swaps):
-        remote(halves[s], swap_spot(s, lane), swap_sem.at[s, 0], swap_sem.at[s, 1], twin).start()
-        pltpu.make_async_copy(halves[s], swap_spot(s, lane), own_sem.at[count + s]).start()
-    for w in range(count):
-        remote(shards[w], shard_of(w, core), give_sem.at[w, 0, n - 1], take_sem.at[w, 0, n - 1], mate).start()
-        pltpu.make_async_copy(shards[w], shard_of(w, core), own_sem.at[w]).start()
-
-    def owner_of(side, step):
-        if side == 0:
-            return (pos - 1 - step + 2 * n) % n
-        return (pos + 1 + step) % n
-
-    def step_body(step, carry):
-        for k, (w, part) in enumerate(messages):
-            for side in range(2):
-                block = spot(w, owner_of(side, step), core, side, part)
-                remote(block, block, send_sem.at[k, side, step], recv_sem.at[k, side, step], nexts[side]).wait_recv()
-
-                @pl.when(step < n - 2)
-                def _():
-                    remote(
-                        block, block, send_sem.at[k, side, step + 1], recv_sem.at[k, side, step + 1], nexts[side]
-                    ).start()
-
-                remote(block, block, give_sem.at[k, side, step], take_sem.at[k, side, step], mate).start()
-        return carry
-
-    lax.fori_loop(0, n - 1, step_body, 0)
-
-    def drain(step, carry):
-        for k, (w, part) in enumerate(messages):
-            for side in range(2):
-                owner = owner_of(side, step)
-                block = spot(w, owner, core, side, part)
-                theirs = spot(w, owner, 1 - core, side, part)
-                remote(block, block, send_sem.at[k, side, step], recv_sem.at[k, side, step], nexts[side]).wait_send()
-                given = remote(block, theirs, give_sem.at[k, side, step], take_sem.at[k, side, step], mate)
-                given.wait_send()
-                given.wait_recv()
-        return carry
-
-    lax.fori_loop(0, n - 1, drain, 0)
-    for w in range(count):
-        pltpu.make_async_copy(shards[w], shard_of(w, core), own_sem.at[w]).wait()
-        given = remote(shards[w], shard_of(w, 1 - core), give_sem.at[w, 0, n - 1], take_sem.at[w, 0, n - 1], mate)
-        given.wait_send()
-        given.wait_recv()
-    for s in range(swaps):
-        pltpu.make_async_copy(halves[s], swap_spot(s, lane), own_sem.at[count + s]).wait()
-        other = remote(halves[s], swap_spot(s, 1 - lane), swap_sem.at[s, 0], swap_sem.at[s, 1], twin)
-        other.wait_send()
-        other.wait_recv()
-
-
-def gather_weights(shards, swaps, parts, dp, collective_id):
-    n = dp // 2
-    count = len(shards)
-    msgs = sum(parts)
-    dma = pltpu.SemaphoreType.DMA
-    outs = pl.pallas_call(
-        functools.partial(gather_kernel, n, tuple(parts), count, len(swaps)),
-        out_shape=[
-            *[jax.ShapeDtypeStruct((s.shape[0] * dp, s.shape[1]), s.dtype) for s in shards],
-            *[jax.ShapeDtypeStruct((s.shape[0] * 2, s.shape[1]), s.dtype) for s in swaps],
-        ],
-        in_specs=[pl.BlockSpec(memory_space=pltpu.VMEM)] * (count + len(swaps)),
-        out_specs=[pl.BlockSpec(memory_space=pltpu.HBM)] * (count + len(swaps)),
-        scratch_shapes=[
-            dma((count + len(swaps),)),
-            dma((msgs, 2, n - 1)),
-            dma((msgs, 2, n - 1)),
-            dma((msgs, 2, n)),
-            dma((msgs, 2, n)),
-            dma((max(1, len(swaps)), 2)),
-        ],
-        compiler_params=pltpu.CompilerParams(collective_id=collective_id, has_side_effects=True),
-    )(*shards, *swaps)
-    return outs[:count], outs[count:]
-
-
-def reduce_kernel(n, pairs, *refs):
-    n_left = 1 + max(p[0] for p in pairs)
-    n_right = 1 + max(p[1] for p in pairs)
-    count = len(pairs)
-    lefts = refs[:n_left]
-    rights = refs[n_left : n_left + n_right]
-    outs = refs[n_left + n_right : n_left + n_right + count]
-    rest = refs[n_left + n_right + count :]
-    mine, give, take, ship, land = (rest[i * count : (i + 1) * count] for i in range(5))
-    term, give_sem, take_sem, ship_sem, land_sem = rest[5 * count :]
-    pos, core = ring_place(n)
-    nexts = (at((pos + 1) % n, core, n), at((pos + n - 1) % n, core, n))
-    mate = at(pos, 1 - core, n)
-    meet((*nexts, mate))
-    rows = outs[0].shape[0]
-
-    def owner_of(side, step):
-        if side == 0:
-            return (pos - 1 - step + 2 * n) % n
-        return (pos + 1 + step) % n
-
-    def early(m, side, step):
-        left, right = pairs[m]
-        wide = outs[m].shape[1] // 2
-        slot = step % 2
-        start = pl.multiple_of(chip_at(owner_of(side, step), n) * 2 * rows, 2 * rows)
-        part = term.at[:, pl.ds(0, wide)]
-        part[...] = jnp.dot(
-            lefts[left][pl.ds(start, 2 * rows), :],
-            rights[right][:, pl.ds(side * wide, wide)],
-            preferred_element_type=jnp.float32,
-        )
-        other = pl.ds(pl.multiple_of((1 - core) * rows, rows), rows)
-        same = pl.ds(pl.multiple_of(core * rows, rows), rows)
-        given = remote(
-            give[m].at[side, slot], take[m].at[side, slot],
-            give_sem.at[m, side, slot], take_sem.at[m, side, slot], mate,
-        )
-
-        @pl.when(step >= 2)
-        def _():
-            given.wait_send()
-
-        give[m][side, slot] = part[other, :].astype(jnp.bfloat16)
-        given.start()
-        mine[m][side] = part[same, :]
-
-    def shipped(m, side, step):
-        return remote(
-            ship[m].at[side, step % 2], land[m].at[side, step],
-            ship_sem.at[m, side, step % 2], land_sem.at[m, side, step], nexts[side],
-        )
-
-    def local_sum(m, side, step):
-        slot = step % 2
-        remote(
-            give[m].at[side, slot], take[m].at[side, slot],
-            give_sem.at[m, side, slot], take_sem.at[m, side, slot], mate,
-        ).wait_recv()
-        return mine[m][side] + take[m][side, slot].astype(jnp.float32)
-
-    for m in range(count):
-        for side in range(2):
-            early(m, side, 0)
-    for m in range(count):
-        for side in range(2):
-            total = local_sum(m, side, 0)
-            ship[m][side, 0] = total.astype(jnp.bfloat16)
-            shipped(m, side, 0).start()
-            early(m, side, 1)
-
-    def step_body(step, carry):
-        for m in range(count):
-            for side in range(2):
-                total = local_sum(m, side, step)
-                shipped(m, side, step - 1).wait_recv()
-                total = total + land[m][side, step - 1].astype(jnp.float32)
-
-                @pl.when(step >= 2)
-                def _():
-                    shipped(m, side, step - 2).wait_send()
-
-                ship[m][side, step % 2] = total.astype(jnp.bfloat16)
-                shipped(m, side, step).start()
-                early(m, side, step + 1)
-        return carry
-
-    lax.fori_loop(1, n - 1, step_body, 0)
-    last = n - 1
-    for m in range(count):
-        wide = outs[m].shape[1] // 2
-        for side in range(2):
-            total = local_sum(m, side, last)
-            shipped(m, side, last - 1).wait_recv()
-            outs[m][:, pl.ds(side * wide, wide)] = total + land[m][side, last - 1].astype(jnp.float32)
-    for m in range(count):
-        for side in range(2):
-            shipped(m, side, last - 1).wait_send()
-            if last >= 2:
-                shipped(m, side, last - 2).wait_send()
-            for slot in range(2):
-                remote(
-                    give[m].at[side, slot], take[m].at[side, slot],
-                    give_sem.at[m, side, slot], take_sem.at[m, side, slot], mate,
-                ).wait_send()
-
-
-def reduce_grads(lefts, rights, pairs, dp, collective_id):
-    n = dp // 2
-    count = len(pairs)
-    rows = lefts[0].shape[0] // dp
-    wides = [rights[r].shape[1] // 2 for _, r in pairs]
-    low = jnp.bfloat16
-    return pl.pallas_call(
-        functools.partial(reduce_kernel, n, tuple(pairs)),
-        out_shape=[jax.ShapeDtypeStruct((rows, 2 * w), jnp.float32) for w in wides],
-        in_specs=[pl.BlockSpec(memory_space=pltpu.VMEM)] * (len(lefts) + len(rights)),
-        out_specs=[pl.BlockSpec(memory_space=pltpu.VMEM)] * count,
-        scratch_shapes=[
-            *[pltpu.VMEM((2, rows, w), jnp.float32) for w in wides],
-            *[pltpu.VMEM((2, 2, rows, w), low) for w in wides],
-            *[pltpu.VMEM((2, 2, rows, w), low) for w in wides],
-            *[pltpu.VMEM((2, 2, rows, w), low) for w in wides],
-            *[pltpu.VMEM((2, n - 1, rows, w), low) for w in wides],
-            pltpu.VMEM((2 * rows, max(wides)), jnp.float32),
-            pltpu.SemaphoreType.DMA((count, 2, 2)),
-            pltpu.SemaphoreType.DMA((count, 2, 2)),
-            pltpu.SemaphoreType.DMA((count, 2, 2)),
-            pltpu.SemaphoreType.DMA((count, 2, n - 1)),
-        ],
-        compiler_params=pltpu.CompilerParams(
-            collective_id=collective_id, has_side_effects=True, vmem_limit_bytes=67043328
-        ),
-    )(*lefts, *rights)
 
 
 def product(left, right):
@@ -435,21 +181,25 @@
 
 def forward_kernel(n, dims, *refs):
     (
-        shards, qkv, out_weight, tokens, full_one, cot_full, tab, seg_col, seg_row, gains, mlp_gain,
-        weights, attn, resid, flipped, act,
-        full_two, kept, part, peer, acc, blocks, stage,
-        own_sem, send_sem, recv_sem, give_sem, take_sem, swap_sem, load_sem, stage_sem,
+        mixed, ffn_shards, tile, tokens, cot, tab, seg_col, seg_row,
+        weights, qkv_out, attn, resid, flipped, act, attn_gain, mlp_gain, gains,
+        full_rows, cot_full, full_two, out_weight, columns, box, kept, part, peer, acc, blocks, stage,
+        own_sem, send_sem, recv_sem, give_sem, take_sem, swap_sem, load_sem, stage_sem, column_sem, tile_sem,
     ) = refs
     q_heads, kv_heads, seq, block = dims
     pos, core = ring_place(n)
+    me = lax.axis_index("dp")
     lane = lax.axis_index("tensor")
     nexts = (at((pos + 1) % n, core, n), at((pos + n - 1) % n, core, n))
     mate = at(pos, 1 - core, n)
-    twin = (lax.axis_index("dp"), 1 - lane)
-    count, rows, width = shards.shape
+    twin = (me, 1 - lane)
+    count, rows, width = ffn_shards.shape
     wide = width // 2
+    narrow = wide // 2
     model = 2 * n * rows
     half = seq // 2
+    theirs = pl.ds(pl.multiple_of((1 - lane) * half, half), half)
+    ours = pl.ds(pl.multiple_of(lane * half, half), half)
     meet((*nexts, mate, twin))
 
     def owner_of(side, step):
@@ -457,63 +207,175 @@
             return (pos - step + 2 * n) % n
         return (pos + step) % n
 
-    def spot(w, chip, who, side):
-        start = w * model + (chip * 2 + who) * rows
-        return weights.at[pl.ds(pl.multiple_of(start, rows), rows), pl.ds(side * wide, wide)]
-
-    def hop(w, side, step):
-        here = spot(w, chip_at(owner_of(side, step), n), core, side)
-        return remote(here, here, send_sem.at[w, side, step], recv_sem.at[w, side, step], nexts[side])
-
-    def first_hop(w, side):
-        return remote(
-            shards.at[w, :, pl.ds(side * wide, wide)],
-            spot(w, chip_at(pos, n), core, side),
-            send_sem.at[w, side, 1], recv_sem.at[w, side, 1], nexts[side],
-        )
-
-    def onward(w, side, step):
-        here = spot(w, chip_at(owner_of(side, step), n), core, side)
-        return remote(here, here, send_sem.at[w, side, step + 1], recv_sem.at[w, side, step + 1], nexts[side])
-
-    def hand(w, side, step, who):
-        here = spot(w, chip_at(owner_of(side, step), n), who, side)
-        return remote(here, here, give_sem.at[w, side, step], take_sem.at[w, side, step], mate)
-
-    def hand_own(w, side, who):
-        return remote(
-            shards.at[w, :, pl.ds(side * wide, wide)],
-            spot(w, chip_at(pos, n), who, side),
-            give_sem.at[w, side, 0], take_sem.at[w, side, 0], mate,
-        )
-
-    def keep_own(w, side):
-        return pltpu.make_async_copy(
-            shards.at[w, :, pl.ds(side * wide, wide)], spot(w, chip_at(pos, n), core, side), own_sem.at[w, side]
-        )
-
+    def small(sub, side):
+        return (sub, 0, pl.ds(side * wide + sub * narrow, narrow), mixed)
+
+    def large(w, side):
+        return (w + 2, (w + 1) * model, pl.ds(side * wide, wide), None if not isinstance(w, int) else ffn_shards.at[w])
+
+    def spot(message, chip, who):
+        start = message[1] + (chip * 2 + who) * rows
+        return weights.at[pl.ds(pl.multiple_of(start, rows), rows), message[2]]
+
+    def hop(message, side, step):
+        k = message[0]
+        here = spot(message, chip_at(owner_of(side, step - 1), n), core)
+        return remote(here, here, send_sem.at[k, side, step], recv_sem.at[k, side, step], nexts[side])
+
+    def arrived(message, side, step):
+        k = message[0]
+        here = spot(message, chip_at(owner_of(side, step), n), core)
+        return remote(here, here, send_sem.at[k, side, step], recv_sem.at[k, side, step], nexts[side])
+
+    def hand(message, side, step, who):
+        k = message[0]
+        here = spot(message, chip_at(owner_of(side, step), n), who)
+        return remote(here, here, give_sem.at[k, side, step], take_sem.at[k, side, step], mate)
+
+    def begin(message, side):
+        k = message[0]
+        source = message[3].at[:, message[2]]
+        here = spot(message, chip_at(pos, n), core)
+        remote(source, here, send_sem.at[k, side, 1], recv_sem.at[k, side, 1], nexts[side]).start()
+        remote(source, here, give_sem.at[k, side, 0], take_sem.at[k, side, 0], mate).start()
+        pltpu.make_async_copy(source, here, own_sem.at[k, side]).start()
+
+    def keep_own(message, side):
+        here = spot(message, chip_at(pos, n), core)
+        return pltpu.make_async_copy(here, here, own_sem.at[message[0], side])
+
+    def tile_hop(step, owner):
+        place = chip_at(owner, n) * 2 + core
+        return remote(box.at[place], box.at[place], tile_sem.at[0, step], tile_sem.at[1, step], nexts[0])
+
+    def tile_hand(step, who):
+        place = chip_at(owner_of(0, step), n) * 2 + who
+        return remote(box.at[place], box.at[place], tile_sem.at[2, step], tile_sem.at[3, step], mate)
+
+    box[me] = tile[...]
+    swaps = [
+        remote(source, target.at[ours], swap_sem.at[i, 0], swap_sem.at[i, 1], twin)
+        for i, (source, target) in enumerate(((tokens, full_rows), (cot, cot_full)))
+    ]
+    remote(tile, box.at[me], tile_sem.at[0, 1], tile_sem.at[1, 1], nexts[0]).start()
+    remote(tile, box.at[me], tile_sem.at[2, 0], tile_sem.at[3, 0], mate).start()
+    for sub in range(2):
+        for side in range(2):
+            begin(small(sub, side), side)
+    for swap in swaps:
+        swap.start()
+    full_rows[ours, :] = tokens[...]
+    cot_full[ours, :] = cot[...]
+
+    def pass_on(message, side, step):
+        arrived(message, side, step).wait_recv()
+
+        @pl.when(step < n - 1)
+        def _():
+            hop(message, side, step + 1).start()
+
+        hand(message, side, step, core).start()
+
+    def pass_tile(step):
+        tile_hop(step, owner_of(0, step)).wait_recv()
+
+        @pl.when(step < n - 1)
+        def _():
+            tile_hop(step + 1, owner_of(0, step)).start()
+
+        tile_hand(step, core).start()
+
+    def mixed_step(step, carry):
+        pass_tile(step)
+        for sub in range(2):
+            for side in range(2):
+                pass_on(small(sub, side), side, step)
+        return carry
+
+    lax.fori_loop(1, n - 1, mixed_step, 0)
+    pass_tile(n - 1)
     for w in range(count):
         for side in range(2):
-            first_hop(w, side).start()
-    for w in range(count):
-        for side in range(2):
-            hand_own(w, side, core).start()
-            keep_own(w, side).start()
+            begin(large(w, side), side)
+        if w < 2:
+            for side in range(2):
+                pass_on(small(w, side), side, n - 1)
 
     def service(event):
         step, w = event // count + 1, event % count
         for side in range(2):
-            hop(w, side, step).wait_recv()
-
-            @pl.when(step < n - 1)
-            def _():
-                onward(w, side, step).start()
-
-            hand(w, side, step, core).start()
+            pass_on(large(w, side), side, step)
+
+    def gathered(step, carry):
+        for sub in range(2):
+            for side in range(2):
+                hand(small(sub, side), side, step, 1 - core).wait_recv()
+        tile_hand(step, 1 - core).wait_recv()
+        return carry
+
+    lax.fori_loop(0, n, gathered, 0)
+    for sub in range(2):
+        for side in range(2):
+            keep_own(small(sub, side), side).wait()
+    q_wide = (q_heads + 2 * kv_heads) * HD
+    fetch_out = pltpu.make_async_copy(
+        weights.at[pl.ds(0, model), pl.ds(q_wide, width - q_wide)], out_weight, load_sem.at[0]
+    )
+    turns = q_wide // columns.shape[2]
+    deep = columns.shape[2]
+
+    def fetch_columns(i):
+        return pltpu.make_async_copy(
+            weights.at[pl.ds(0, model), pl.ds(pl.multiple_of(i * deep, deep), deep)],
+            columns.at[i % 2], column_sem.at[i % 2],
+        )
+
+    fetch_columns(0).start()
+    fetch_out.start()
+    dp = 2 * n
+    share, head_share = model // dp, 2 * HD // dp
+    for first, target, per in ((0, attn_gain, share), (1, mlp_gain, share)):
+        for s in range(model // 128):
+            owners = [d for d in range(dp) if d * per // 128 == s]
+            total = box[owners[0], first : first + 1, :]
+            for d in owners[1:]:
+                total = total + box[d, first : first + 1, :]
+            target[:, s * 128 : (s + 1) * 128] = total
+    for s in range(2):
+        owners = [d for d in range(dp) if d * head_share // HD == s]
+        total = box[owners[0], 2:3, :]
+        for d in owners[1:]:
+            total = total + box[d, 2:3, :]
+        gains[s : s + 1, :] = total
+    swaps[0].wait_recv()
+    strip = 32
+
+    def norm_strip(i, carry):
+        there = pl.ds(pl.multiple_of(i * strip, strip), strip)
+        values = full_rows[there, :].astype(jnp.float32)
+        full_two[there, :] = (values * row_scale(values) * attn_gain[...]).astype(jnp.bfloat16)
+        return carry
+
+    lax.fori_loop(0, seq // strip, norm_strip, 0)
+    qkv = acc.at[count - 1]
+
+    def project(i, carry):
+        @pl.when(i < turns - 1)
+        def _():
+            fetch_columns(i + 1).start()
+
+        fetch_columns(i).wait()
+        qkv[:, pl.ds(pl.multiple_of(i * deep, deep), deep)] = product(full_two[...], columns[i % 2])
+        return carry
+
+    lax.fori_loop(0, turns, project, 0)
+    save_qkv = pltpu.make_async_copy(qkv.at[:, pl.ds(0, q_wide)], qkv_out, load_sem.at[1])
+    save_qkv.start()
+    service(0)
 
     def load(job, side):
         step, w = job // count, job % count
-        start = w * model + chip_at(owner_of(side, step), n) * 2 * rows
+        start = (w + 1) * model + chip_at(owner_of(side, step), n) * 2 * rows
         return pltpu.make_async_copy(
             weights.at[pl.ds(pl.multiple_of(start, 2 * rows), 2 * rows), pl.ds(side * wide, wide)],
             blocks.at[side], load_sem.at[side],
@@ -522,14 +384,11 @@
     def work(job):
         step, w = job // count, job % count
         for side in range(2):
-            @pl.when(step > 0)
-            def _():
-                hand(w, side, step, 1 - core).wait_recv()
+            hand(large(w, side), side, step, 1 - core).wait_recv()
 
             @pl.when(step == 0)
             def _():
-                hand_own(w, side, 1 - core).wait_recv()
-                keep_own(w, side).wait()
+                keep_own(large(w, side), side).wait()
 
             load(job, side).start()
         for side in range(2):
@@ -537,11 +396,11 @@
             chip = chip_at(owner_of(side, step), n)
 
             def with_left(left):
-                tile = wide // 3
+                tile_width = wide // 3
 
                 def one(i, carry):
-                    there = pl.ds(pl.multiple_of(side * wide + i * tile, tile), tile)
-                    gained = product(left, blocks[side, :, pl.ds(pl.multiple_of(i * tile, tile), tile)])
+                    there = pl.ds(pl.multiple_of(side * wide + i * tile_width, tile_width), tile_width)
+                    gained = product(left, blocks[side, :, pl.ds(pl.multiple_of(i * tile_width, tile_width), tile_width)])
 
                     @pl.when(step == 0)
                     def _():
@@ -555,11 +414,11 @@
 
                 lax.fori_loop(0, 3, one, 0)
 
-            @pl.when(w < 2)
+            @pl.when(w < count - 1)
             def _():
                 with_left(block_columns(full_two, chip, 2 * rows))
 
-            @pl.when(w == 2)
+            @pl.when(w == count - 1)
             def _():
                 with_left(block_columns(cot_full, chip, 2 * rows))
 
@@ -575,35 +434,35 @@
 
         lax.fori_loop(first, last, one, 0)
 
+    flip(full_two, 2)
     attend(0, kv_heads // 2)
-    service(0)
+    service(1)
     attend(kv_heads // 2, kv_heads)
-    service(1)
-    theirs = pl.ds(pl.multiple_of((1 - lane) * half, half), half)
-    ours = pl.ds(pl.multiple_of(lane * half, half), half)
+    service(2)
+    fetch_out.wait()
     part[...] = tail_product(attn[theirs, :], out_weight[...]).astype(jnp.bfloat16)
-    send_part = remote(part, peer, swap_sem.at[0, 0], swap_sem.at[0, 1], twin)
+    swaps[1].wait_recv()
+    send_part = remote(part, peer, swap_sem.at[2, 0], swap_sem.at[2, 1], twin)
     send_part.start()
     resid[...] = tokens[...].astype(jnp.float32) + tail_product(attn[ours, :], out_weight[...])
-    service(2)
-    flip(full_one, 2)
     service(3)
+    service(4)
     flip(cot_full, 1)
-    for event in range(4, 6):
-        service(event)
+    service(5)
     send_part.wait_recv()
     summed = resid[...] + peer[...].astype(jnp.float32)
     resid[...] = summed
     send_part.wait_send()
     part[...] = (summed * row_scale(summed) * mlp_gain[...]).astype(jnp.bfloat16)
-    send_two = remote(part, full_two.at[ours], swap_sem.at[1, 0], swap_sem.at[1, 1], twin)
+    send_two = remote(part, full_two.at[ours], swap_sem.at[3, 0], swap_sem.at[3, 1], twin)
     send_two.start()
     full_two[ours, :] = part[...]
     ready = 9
     for event in range(6, ready):
         service(event)
-    remote(part, full_two.at[theirs], swap_sem.at[1, 0], swap_sem.at[1, 1], twin).wait_recv()
+    remote(part, full_two.at[theirs], swap_sem.at[3, 0], swap_sem.at[3, 1], twin).wait_recv()
     flip(full_two, 0)
+    save_qkv.wait()
 
     def both(i, carry):
         service(ready + i)
@@ -623,9 +482,6 @@
         return carry
 
     lax.fori_loop(0, count * (n - 1) - ready, both, 0)
-    send_two.wait_send()
-
-    strip = 32
 
     def finish(i, carry):
         there = pl.ds(pl.multiple_of(i * strip, strip), strip)
@@ -642,61 +498,75 @@
     lax.fori_loop(0, seq // strip, finish, 0)
 
     def drain(step, carry):
-        for w in range(count):
-            for side in range(2):
-                hop(w, side, step).wait_send()
-                hand(w, side, step, core).wait_send()
+        for side in range(2):
+            for message in [small(sub, side) for sub in range(2)] + [large(w, side) for w in range(count)]:
+                hop(message, side, step).wait_send()
+                hand(message, side, step, core).wait_send()
+        tile_hop(step, owner_of(0, step)).wait_send()
+        tile_hand(step, core).wait_send()
         return carry
 
     lax.fori_loop(1, n, drain, 0)
-    for w in range(count):
-        for side in range(2):
-            hand_own(w, side, core).wait_send()
-
-
-def forward_block(shards, qkv, out_weight, tokens, full_one, cot_full, tab, segments, gains, mlp_gain, q_heads, kv_heads, dp):
+    for side in range(2):
+        for message in [small(sub, side) for sub in range(2)] + [large(w, side) for w in range(count)]:
+            hand(message, side, 0, core).wait_send()
+    tile_hand(0, core).wait_send()
+    for swap in (*swaps, send_two):
+        swap.wait_send()
+
+
+def forward_block(mixed, ffn_shards, tile, tokens, cot, tab, segments, q_heads, kv_heads, dp):
     n = dp // 2
-    count, rows, width = shards.shape
-    seq, model = cot_full.shape
-    half = seq // 2
-    low, dma, vmem = jnp.bfloat16, pltpu.SemaphoreType.DMA, pltpu.VMEM
+    count, rows, width = ffn_shards.shape
+    half, model = tokens.shape
+    seq = 2 * half
+    q_wide = (q_heads + 2 * kv_heads) * HD
+    low, dma, vmem, hbm = jnp.bfloat16, pltpu.SemaphoreType.DMA, pltpu.VMEM, pltpu.HBM
     shape = jax.ShapeDtypeStruct
     place = lambda kind: pl.BlockSpec(memory_space=kind)
     return pl.pallas_call(
         functools.partial(forward_kernel, n, (q_heads, kv_heads, seq, seq // 2)),
         out_shape=[
-            shape((count * model, width), low),
+            shape(((count + 1) * model, width), low),
+            shape((seq, q_wide), jnp.float32),
             shape((seq, q_heads * HD), low),
             shape((half, model), jnp.float32),
             shape((3, model, seq), low),
             shape((count, seq, width), low),
+            shape((1, model), jnp.float32),
+            shape((1, model), jnp.float32),
+            shape((2, HD), jnp.float32),
         ],
-        in_specs=[place(vmem)] * 11,
-        out_specs=[place(pltpu.HBM), place(vmem), place(vmem), place(pltpu.HBM), place(vmem)],
+        in_specs=[place(vmem)] * 8,
+        out_specs=[place(k) for k in (hbm, hbm, vmem, vmem, hbm, vmem, vmem, vmem, vmem)],
         scratch_shapes=[
             vmem((seq, model), low),
+            vmem((seq, model), low),
+            vmem((seq, model), low),
+            vmem((model, width - q_wide), low),
+            vmem((2, model, 256), low),
+            vmem((dp, 8, 128), jnp.float32),
             vmem((2, seq, HD), low),
             vmem((half, model), low),
             vmem((half, model), low),
             vmem((count, seq, width), jnp.float32),
             vmem((2, 2 * rows, width // 2), low),
             vmem((2, 256, seq), low),
-            dma((count, 2)),
-            dma((count, 2, n)),
-            dma((count, 2, n)),
-            dma((count, 2, n)),
-            dma((count, 2, n)),
-            dma((2, 2)),
+            dma((count + 2, 2)),
+            dma((count + 2, 2, n)),
+            dma((count + 2, 2, n)),
+            dma((count + 2, 2, n)),
+            dma((count + 2, 2, n)),
+            dma((4, 2)),
             dma((2,)),
             dma((2,)),
+            dma((2,)),
+            dma((4, n)),
         ],
         compiler_params=pltpu.CompilerParams(
             collective_id=1, has_side_effects=True, vmem_limit_bytes=67043328
         ),
-    )(
-        shards, qkv, out_weight, tokens, full_one, cot_full, tab,
-        segments.reshape(seq, 1), segments.reshape(1, seq), gains, mlp_gain,
-    )
+    )(mixed, ffn_shards, tile, tokens, cot, tab, segments.reshape(seq, 1), segments.reshape(1, seq))
 
 
 SLOTS = 3
@@ -866,9 +736,9 @@
 
 def backward_kernel(n, dims, *refs):
     (
-        flipped, act, weights, qkv, attn, out_weight, cot, resid, tab, seg_col, seg_row, gains, mlp_gain,
+        flipped, act, weights, qkv, attn, cot, resid, tab, seg_col, seg_row, gains, mlp_gain,
         grads, d_proj, d_flip, d_resid, mlp_sum, qk_sum,
-        lefts, d_full, gate_block, up_block, own, part, peer, d_attn, heads, kept, stage,
+        lefts, out_weight, d_full, gate_block, up_block, own, part, peer, d_attn, heads, kept, stage,
         swap_sem, load_sem, head_sem, left_sem, stage_sem,
     ) = refs[:35]
     q_heads, kv_heads, seq, block = dims
@@ -881,8 +751,13 @@
     fetch_lefts.start()
     fetch_attn = pltpu.make_async_copy(attn, d_proj.at[2], left_sem.at[1])
     fetch_attn.start()
+    q_wide = qkv.shape[1]
+    fetch_out = pltpu.make_async_copy(
+        weights.at[pl.ds(0, out_weight.shape[0]), pl.ds(q_wide, out_weight.shape[1])], out_weight, left_sem.at[2]
+    )
     meet((*nexts, mate, twin))
     fetch_lefts.wait()
+    fetch_out.start()
     fetch_attn.wait()
     count = act.shape[0]
     model = resid.shape[1]
@@ -902,7 +777,7 @@
 
     def fetch(i, which):
         target = (gate_block, up_block)[which]
-        start = which * model + i * deep
+        start = (which + 1) * model + i * deep
         return pltpu.make_async_copy(
             weights.at[pl.ds(pl.multiple_of(start, deep), deep), :], target, load_sem.at[which]
         )
@@ -972,6 +847,7 @@
     send = remote(part, d_full.at[ours], swap_sem.at[1, 0], swap_sem.at[1, 1], twin)
     send.start()
     d_full[ours, :] = part[...]
+    fetch_out.wait()
     columns = out_weight.shape[1]
     quarter = columns // 4
 
@@ -1016,7 +892,7 @@
 
 
 def backward_block(
-    flipped, act, weights, qkv, attn, out_weight, cot, resid, tab, segments, gains, mlp_gain, q_heads, kv_heads, dp
+    flipped, act, weights, qkv, attn, cot, resid, tab, segments, gains, mlp_gain, q_heads, kv_heads, dp
 ):
     n = dp // 2
     count, seq, width = act.shape
@@ -1036,10 +912,11 @@
             shape((1, model), jnp.float32),
             shape((8, HD), jnp.float32),
         ],
-        in_specs=[place(pltpu.HBM), place(vmem)] + [place(pltpu.HBM)] * 3 + [place(vmem)] * 8,
+        in_specs=[place(pltpu.HBM), place(vmem)] + [place(pltpu.HBM)] * 3 + [place(vmem)] * 7,
         out_specs=[place(pltpu.HBM), place(vmem), place(pltpu.HBM)] + [place(vmem)] * 3,
         scratch_shapes=[
             vmem((2, model, seq), low),
+            vmem((model, q_heads * HD), low),
             vmem((seq, model), low),
             vmem((deep, width), low),
             vmem((deep, width), low),
@@ -1053,7 +930,7 @@
             dma((2, 2)),
             dma((2,)),
             dma((q_heads // kv_heads + 2,)),
-            dma((2,)),
+            dma((3,)),
             dma((2,)),
             *reduce_scratch(n, count, rows, width // 2),
         ],
@@ -1061,18 +938,18 @@
             collective_id=2, has_side_effects=True, vmem_limit_bytes=67043328
         ),
     )(
-        flipped, act, weights, qkv, attn, out_weight, cot, resid, tab,
+        flipped, act, weights, qkv, attn, cot, resid, tab,
         segments.reshape(seq, 1), segments.reshape(1, seq), gains, mlp_gain,
     )
 
 
 def closing_kernel(n, *refs):
     (
-        flipped, d_flip, d_proj, qkv_weight, weights, act, tokens, resid, d_resid, attn_gain, mlp_sum, qk_sum,
+        flipped, d_flip, d_proj, weights, act, tokens, resid, d_resid, attn_gain, mlp_sum, qk_sum,
         grads, result, input_grad, gain_out,
         lefts, acts, first_block, second_block, own, part, peer, attn_sum, table, others, inbox,
         swap_sem, load_sem, first_sem, second_sem, trade_sem, post_sem, mail_sem,
-    ) = refs[:34]
+    ) = refs[:33]
     pos, core = ring_place(n)
     me = lax.axis_index("dp")
     lane = lax.axis_index("tensor")
@@ -1101,7 +978,7 @@
     count, seq, width = d_proj.shape
     half, model = resid.shape
     early, event, finish = reducer(
-        n, pos, core, nexts, mate, (lefts, d_proj, grads, *refs[34:]), lambda m: m // 2
+        n, pos, core, nexts, mate, (lefts, d_proj, grads, *refs[33:]), lambda m: m // 2
     )
     for m in range(count):
         early(m, 0)
@@ -1115,13 +992,13 @@
     def stream(source, offset, block, sem):
         def fetch(i):
             return pltpu.make_async_copy(
-                source.at[pl.ds(pl.multiple_of(offset + i * deep, deep), deep)], block.at[i % 2], sem.at[i % 2]
+                source.at[pl.ds(pl.multiple_of(offset + i * deep, deep), deep), pl.ds(0, block.shape[2])], block.at[i % 2], sem.at[i % 2]
             )
 
         return fetch
 
-    first_fetch = stream(qkv_weight, 0, first_block, first_sem)
-    second_fetch = stream(weights, 2 * model, second_block, second_sem)
+    first_fetch = stream(weights, 0, first_block, first_sem)
+    second_fetch = stream(weights, 3 * model, second_block, second_sem)
     first_fetch(0).start()
 
     def narrow(which, fetch, block, rows_of, every, base):
@@ -1255,7 +1132,7 @@
 
 
 def closing_block(
-    flipped, d_flip, d_proj, qkv_weight, weights, act, tokens, resid, d_resid, attn_gain, mlp_sum, qk_sum, dp
+    flipped, d_flip, d_proj, weights, act, tokens, resid, d_resid, attn_gain, mlp_sum, qk_sum, dp
 ):
     n = dp // 2
     count, seq, width = d_proj.shape
@@ -1275,12 +1152,12 @@
             shape((half, model), low),
             shape((8, 128), jnp.float32),
         ],
-        in_specs=[place(k) for k in (hbm, hbm, vmem, hbm, hbm, hbm, *[vmem] * 6)],
+        in_specs=[place(k) for k in (hbm, hbm, vmem, hbm, hbm, *[vmem] * 6)],
         out_specs=[place(hbm), place(vmem), place(vmem), place(vmem)],
         scratch_shapes=[
             vmem((2, model, seq), low),
             vmem((seq, hidden), low),
-            vmem((2, deep, qkv_weight.shape[1]), low),
+            vmem((2, deep, 2 * width), low),
             vmem((2, deep, hidden), low),
             vmem((2, half, model), jnp.float32),
             vmem((2, half, model), low),
@@ -1301,7 +1178,7 @@
         compiler_params=pltpu.CompilerParams(
             collective_id=3, has_side_effects=True, vmem_limit_bytes=67043328
         ),
-    )(flipped, d_flip, d_proj, qkv_weight, weights, act, tokens, resid, d_resid, attn_gain, mlp_sum, qk_sum)
+    )(flipped, d_flip, d_proj, weights, act, tokens, resid, d_resid, attn_gain, mlp_sum, qk_sum)
 
 
 def on_device(
@@ -1321,46 +1198,26 @@
 ):
     dp = lax.axis_size("dp")
     model = tokens.shape[1]
-    gain_row = jnp.concatenate(
-        [
-            jnp.pad(g.astype(jnp.float32), (0, 128 - g.shape[0]))
-            for g in (gain_attn, gain_mlp, gain_qk)
-        ]
-    )
-    gain_shard = jnp.broadcast_to(gain_row[None, :], (16, gain_row.shape[0]))
-    shard_qkv = jnp.concatenate([w_query, w_key, w_value], axis=1)
-    (qkv_weight, out_weight, gain_all), (full_rows, full_cot) = gather_weights(
-        [shard_qkv, w_output.T, gain_shard], [tokens, cotangent], [2, 1, 1], dp, 0
-    )
-    gain_all = gain_all.reshape(dp, 16, 3, 128)[:, 0]
-    attn_gain = gain_all[:, 0, : gain_attn.shape[0]].reshape(-1)
-    full_rows = full_rows.astype(jnp.float32)
-    full_one = (full_rows * norm_rows(full_rows) * attn_gain).astype(jnp.bfloat16)
-    mlp_gain = gain_all[:, 1, : gain_mlp.shape[0]].reshape(-1)
-    qk_gain = gain_all[:, 2, : gain_qk.shape[0]].reshape(-1)
-    query_gain = qk_gain[:HD]
-    key_gain = qk_gain[HD:]
-    cosine_table, sine_table, _ = tables(seg_ids[0])
-    seq_len = full_one.shape[0]
+    me = lax.axis_index("dp")
+    tile = jnp.zeros((8, 128), jnp.float32)
+    for row, gain in enumerate((gain_attn, gain_mlp, gain_qk)):
+        spot = me * gain.shape[0] % 128 if gain.shape[0] % 128 else 0
+        tile = lax.dynamic_update_slice(tile, gain.astype(jnp.float32)[None, :], (row, spot))
     q_width = w_query.shape[1]
     kv_width = w_key.shape[1]
     q_heads = q_width // HD
     kv_heads = kv_width // HD
-    projected = product(full_one, qkv_weight)
-    pair = jnp.stack([query_gain, key_gain])
+    cosine_table, sine_table, _ = tables(seg_ids[0])
     signed = jnp.concatenate([-sine_table[:, : HD // 2], sine_table[:, HD // 2 :]], axis=1)
     rope_tab = jnp.stack([cosine_table, signed])
-    weights, attn_rows, resid, flipped, act = forward_block(
+    weights, projected, attn_rows, resid, flipped, act, attn_gain, mlp_gain, pair = forward_block(
+        jnp.concatenate([w_query, w_key, w_value, w_output.T], axis=1),
         jnp.stack([w_gate, w_up, w_down.T]),
-        projected,
-        out_weight,
+        tile,
         tokens,
-        full_one,
-        full_cot,
+        cotangent,
         rope_tab,
         seg_ids[0],
-        pair,
-        mlp_gain[None, :],
         q_heads,
         kv_heads,
         dp,
@@ -1371,13 +1228,12 @@
         weights,
         projected,
         attn_rows,
-        out_weight,
         cotangent,
         resid,
         rope_tab,
         seg_ids[0],
         pair,
-        mlp_gain[None, :],
+        mlp_gain,
         q_heads,
         kv_heads,
         dp,
@@ -1387,18 +1243,16 @@
         flipped,
         d_flip,
         d_projected,
-        qkv_weight,
         weights,
         act,
         tokens,
         resid,
         d_resid,
-        attn_gain[None, :],
+        attn_gain,
         mlp_sum,
         qk_sum,
         dp,
     )
-    me = lax.axis_index("dp")
     share = model // dp
     qk_share = 2 * HD // dp
     return (

time: 616 us -> 591 us (0.959)
  Pallas kernels: 565 us -> 552 us
  matrix products: 10.1 us -> 0 us
    pallas_call x1 -> x0, Pallas kernels: 71.4 us -> none  [gather_weights(): pl.pallas_call(functools.partial(gather_kernel, n, tuple(parts), count, l...]
    pallas_call x1, Pallas kernels: 204 us -> 263 us  [forward_block(): pl.pallas_call(functools.partial(forward_kernel, n, (q_heads, kv_heads, s...]
    dot_general x1 -> x0, matrix products: 10.1 us -> none  [product(): return jnp.dot(left, right, preferred_element_type=jnp.float32)]
where the time goes in v4:
time: 591 us; the launch traced here: 582 us
  Pallas kernels  552 us (93%)
  local copies, waits for them, and re-layouts  20.2 us (3%)
  other arithmetic  8.73 us (1%)
    pallas_call x1, Pallas kernels, forward_block(): pl.pallas_call(functools.partial(forward_kernel, n, (q_heads, kv_heads, s...  263 us
    pallas_call x1, Pallas kernels, backward_block(): pl.pallas_call(functools.partial(backward_kernel, n, (q_heads, kv_heads,...  196 us
    pallas_call x1, Pallas kernels, closing_block(): pl.pallas_call(functools.partial(closing_kernel, n), out_shape=[shape((co...  92 us

profile of v4, /device:TPU:0, one launch (start us, length us, event | category | flops | bytes accessed | tf_op | source)
XLA Modules:
  0.0 581.8 jit_solution(8955945878223616789)
XLA Ops:
  0.7 0.7 bitcast_convert_fusion.1
  1.3 0.7 bitcast_convert_fusion
  2.0 1.0 convert_reduce_fusion
  3.0 0.7 pad_convert_fusion
  3.7 0.2 dynamic_update_slice.14.refs_2_
  3.9 0.0 copy-start.5
  3.9 0.6 copy-done.5
  4.5 1.5 copy.37.refs_6_.refs_8_
  6.0 1.1 copy.35
  7.1 2.0 pad_maximum_fusion.1.refs_0_
  9.1 0.0 copy-start.4
  9.1 1.0 multiply_cosine_fusion
  10.1 0.2 maximum_bitcast_fusion
  10.3 0.0 copy-start.2
  10.3 0.0 copy-start.3
  10.4 0.8 pad_maximum_fusion.2.refs_5_.refs_7_
  11.2 0.0 copy-done.4
  11.2 0.3 copy.36
  11.5 0.2 copy-done.2
  11.7 0.2 copy-done.3
  11.9 1.7 pad_maximum_fusion.refs_1_
  13.6 263.4 %shard_map.220 = (bf16[8192,3072]{1,0:T(8,128)(2,1)}, f32[512,2048]{1,0:T(8,128)}, bf16[512,1024]{1,0:T(8,128)(2,1)}, f32[256,2048]{1,0:T(8,128)}, bf16[3,2048,5...) custom-call(bf16[128,3072]{1,0:T(8,128)(2,1)} %pad_maximum_fusion.1., ...), custom_call_target="tpu_custom_call" | custom-call | tf_op jit(solution)/shard_map/pallas_call | solution.py:527
  277.0 196.3 %shard_map.221 = (f32[3,128,3072]{2,1,0:T(8,128)}, bf16[3,512,1024]{2,1,0:T(8,128)(2,1)}, bf16[2048,512]{1,0:T(8,128)(2,1)}, f32[256,2048]{1,0:T(8,128)}, f32[1,2048]{1,0:T(1,128)}, /*index=5*/f32[8,128]{1,0:T(8,128)}) custom-call(bf16[3,2048,512]{2,1,0:T(8,128)(2,1)} %get-tuple-element.31.refs_0_, bf16[3,512,3072]{2,1,0:T(8,128)(2,1)} %get-tuple-element.32.refs_1_.refs_4_, ...), custom_call_target="tpu_custom_call" | custom-call | tf_op jit(solution)/shard_map/pallas_call | solution.py:905
  473.2 92.0 %shard_map.222 = (f32[3,128,1024]{2,1,0:T(8,128)}, bf16[256,2048]{1,0:T(8,128)(2,1)}, bf16[256,2048]{1,0:T(8,128)(2,1)}, f32[8,128]{1,0:T(8,128)}) custom-call(bf16[3,2048,512]{2,1,0:T(8,128)(2,1)} %get-tuple-element.31.refs_0_, bf16[2048,512]{1,0:T(8,128)(2,1)} %get-tuple-element.39.refs_1_, bf16[3,512,1024]{2,1,0:T(8,128)(2,1)} %get-tuple-element.40.refs_2_, ...), custom_call_target="tpu_custom_call" | custom-call | tf_op jit(solution)/shard_map/pallas_call | solution.py:1147
  565.2 1.3 dynamic-slice_bitcast_fusion
  566.5 1.3 slice_bitcast_fusion.7
  567.8 1.9 slice_bitcast_fusion.5
  569.6 2.1 slice_bitcast_fusion.3
  571.7 1.0 copy.39
  572.7 4.5 slice_bitcast_fusion
  577.2 0.0 copy-start.1
  577.2 1.6 copy.40
  578.8 0.0 copy-done.1
  578.8 0.0 copy-start
  578.8 1.0 copy.45
  579.8 0.6 copy-done
  580.4 1.0 copy.46
  (3 shorter events, 0.0 us)
Async XLA Ops:
  3.9 0.6 copy-start.5
  9.1 2.1 copy-start.4
  10.3 1.3 copy-start.2
  10.3 1.6 copy-start.3
  577.2 1.6 copy-start.1
  578.8 1.6 copy-start

commit v5 on v4

--- a/solution.py
+++ b/solution.py
@@ -595,7 +595,7 @@
             width = first + block
             exps = exp_block(query[first:width], keys[:width], seg_col, seg_row, first)
             probs = exps / jnp.sum(exps, axis=-1, keepdims=True)
-            incoming = d_attn[first:width, head_at(head)]
+            incoming = d_attn[first:width, head_at(r)]
             d_probs = tail_product(incoming, values[:width])
             delta = jnp.sum(probs * d_probs, axis=-1, keepdims=True)
             d_scores = (probs * (d_probs - delta)).astype(low)
@@ -617,11 +617,13 @@
     d_proj[1, :, head_at(kv_heads + group)] = kept[2].astype(low)
 
 
-def reducer(n, pos, core, nexts, mate, refs, left_of):
-    lefts, rights, out, mine, term, give, take, ship, land, give_sem, take_sem, ship_sem, land_sem, free_sem, out_sem = refs
+def reducer(n, pos, core, nexts, mate, rights, outs, fetch_left, scratch, stage_of):
+    lefts, mine, term, give, take, ship, land, give_sem, take_sem, ship_sem, land_sem, free_sem, out_sem = scratch
+    before, sends_before, sends_total = stage_of
     count = rights.shape[0]
     wide = rights.shape[2] // 2
-    rows = out.shape[1]
+    rows = outs[0].shape[0]
+    span = pl.ds(0, wide)
 
     def owner_of(side, step):
         if side == 0:
@@ -629,27 +631,34 @@
         return (pos + 1 + step) % n
 
     def given(m, side, step):
+        slot = (before + step) % 2
         return remote(
-            give.at[m, side], take.at[m, side, step % 2],
-            give_sem.at[m, side], take_sem.at[m, side, step % 2], mate,
+            give.at[m, side, :, span], take.at[m, side, slot, :, span],
+            give_sem.at[m, side], take_sem.at[m, side, slot], mate,
         )
 
     def shipped(m, side, step):
+        slot = (sends_before + step) % SLOTS
         return remote(
-            ship.at[m, side], land.at[m, side, step % SLOTS],
-            ship_sem.at[m, side], land_sem.at[m, side, step % SLOTS], nexts[side],
+            ship.at[m, side, :, span], land.at[m, side, slot, :, span],
+            ship_sem.at[m, side], land_sem.at[m, side, slot], nexts[side],
         )
+
+    def fetch(m, step):
+        for side in range(2):
+            start = pl.multiple_of(chip_at(owner_of(side, step), n) * 2 * rows, 2 * rows)
+            fetch_left(m, side, pl.ds(start, 2 * rows))
 
     def early(m, step):
         for side in range(2):
-            start = pl.multiple_of(chip_at(owner_of(side, step), n) * 2 * rows, 2 * rows)
-            left = lefts[left_of(m), pl.ds(start, 2 * rows), :]
+            fetch_left(m, side, None)
+        for side in range(2):
             tile = min(512, wide)
 
             def one(i, carry):
                 there = pl.multiple_of(i * tile, tile)
                 term[:, pl.ds(there, tile)] = product(
-                    left, rights[m, :, pl.ds(pl.multiple_of(side * wide + there, tile), tile)]
+                    lefts[side], rights[m, :, pl.ds(pl.multiple_of(side * wide + there, tile), tile)]
                 )
                 return carry
 
@@ -659,27 +668,33 @@
             def _():
                 given(m, side, step - 1).wait_send()
 
-            give[m, side] = term[pl.ds(pl.multiple_of((1 - core) * rows, rows), rows), :].astype(jnp.bfloat16)
+            other = term[pl.ds(pl.multiple_of((1 - core) * rows, rows), rows), span]
+            give[m, side, :, span] = other.astype(jnp.bfloat16)
             given(m, side, step).start()
-            mine[m, side] = term[pl.ds(pl.multiple_of(core * rows, rows), rows), :]
+            mine[m, side, :, span] = term[pl.ds(pl.multiple_of(core * rows, rows), rows), span]
 
     def event(e):
         step, m = e // count, e % count
+
+        @pl.when(step < n - 1)
+        def _():
+            fetch(m, step + 1)
+
         for side in range(2):
             given(m, side, step).wait_recv()
+            near = take[m, side, (before + step) % 2, :, span].astype(jnp.float32)
 
             @pl.when(step == 0)
             def _():
-                mine[m, side] += take[m, side, 0].astype(jnp.float32)
+                mine[m, side, :, span] += near
 
             @pl.when(step > 0)
             def _():
                 shipped(m, side, step - 1).wait_recv()
-                mine[m, side] += take[m, side, step % 2].astype(jnp.float32) + land[
-                    m, side, (step - 1) % SLOTS
-                ].astype(jnp.float32)
-
-                @pl.when(step - 1 + SLOTS <= n - 2)
+                far = land[m, side, (sends_before + step - 1) % SLOTS, :, span].astype(jnp.float32)
+                mine[m, side, :, span] += near + far
+
+                @pl.when(sends_before + step - 1 + SLOTS < sends_total)
                 def _():
                     pl.semaphore_signal(
                         free_sem.at[m, side], inc=1, device_id=nexts[1 - side], device_id_type=MESH
@@ -689,118 +704,146 @@
 
             @pl.when(step < n - 1)
             def _():
-                @pl.when(step >= SLOTS)
+                @pl.when(sends_before + step >= SLOTS)
                 def _():
                     pl.semaphore_wait(free_sem.at[m, side], 1)
 
-                ship[m, side] = mine[m, side].astype(jnp.bfloat16)
+                ship[m, side, :, span] = mine[m, side, :, span].astype(jnp.bfloat16)
                 shipped(m, side, step).start()
 
             @pl.when(step == n - 1)
             def _():
-                written(m, side).start()
+                for i in range(count):
+                    @pl.when(m == i)
+                    def _():
+                        written(m, side, i).start()
 
         @pl.when(step < n - 1)
         def _():
             early(m, step + 1)
 
-    def written(m, side):
-        return pltpu.make_async_copy(mine.at[m, side], out.at[m, :, pl.ds(side * wide, wide)], out_sem.at[m, side])
-
-    def finish():
-        for m in range(count):
-            for side in range(2):
-                given(m, side, n - 1).wait_send()
-                written(m, side).wait()
-
-    return early, event, finish
-
-
-def reduce_scratch(n, count, rows, wide):
-    low, dma, vmem = jnp.bfloat16, pltpu.SemaphoreType.DMA, pltpu.VMEM
-    return [
-        vmem((count, 2, rows, wide), jnp.float32),
-        vmem((2 * rows, wide), jnp.float32),
-        vmem((count, 2, rows, wide), low),
-        vmem((count, 2, 2, rows, wide), low),
-        vmem((count, 2, rows, wide), low),
-        vmem((count, 2, SLOTS, rows, wide), low),
-        dma((count, 2)),
-        dma((count, 2, 2)),
-        dma((count, 2)),
-        dma((count, 2, SLOTS)),
-        pltpu.SemaphoreType.REGULAR((count, 2)),
-        dma((count, 2)),
-    ]
+    def written(m, side, i):
+        return pltpu.make_async_copy(
+            mine.at[m, side, :, span], outs[i].at[:, pl.ds(side * wide, wide)], out_sem.at[m, side]
+        )
+
+    def begin(m):
+        fetch(m, 0)
+        early(m, 0)
+
+    def finish(m):
+        for side in range(2):
+            given(m, side, n - 1).wait_send()
+            written(m, side, m).wait()
+
+    return begin, event, finish
 
 
 def backward_kernel(n, dims, *refs):
     (
-        flipped, act, weights, qkv, attn, cot, resid, tab, seg_col, seg_row, gains, mlp_gain,
-        grads, d_proj, d_flip, d_resid, mlp_sum, qk_sum,
-        lefts, out_weight, d_full, gate_block, up_block, own, part, peer, d_attn, heads, kept, stage,
-        swap_sem, load_sem, head_sem, left_sem, stage_sem,
-    ) = refs[:35]
+        flipped, act, weights, qkv, attn, cot, tokens, resid, tab, seg_col, seg_row, gains, attn_gain, mlp_gain,
+        grad_gate, grad_up, grad_down, grad_query, grad_pair, grad_out, result, input_grad, gain_out, d_flip,
+        d_proj, d_full, d_resid, blocks, columns, own, part, peer, d_attn, heads, kept, stage,
+        attn_sum, mlp_sum, qk_sum, table, others, inbox,
+        swap_sem, load_sem, head_sem, attn_sem, stage_sem, column_sem, trade_sem, post_sem, mail_sem, left_sem,
+        *scratch,
+    ) = refs
     q_heads, kv_heads, seq, block = dims
     pos, core = ring_place(n)
+    me = lax.axis_index("dp")
     lane = lax.axis_index("tensor")
     nexts = (at((pos + 1) % n, core, n), at((pos + n - 1) % n, core, n))
     mate = at(pos, 1 - core, n)
-    twin = (lax.axis_index("dp"), 1 - lane)
-    fetch_lefts = pltpu.make_async_copy(flipped.at[pl.ds(0, 2)], lefts, left_sem.at[0])
-    fetch_lefts.start()
-    fetch_attn = pltpu.make_async_copy(attn, d_proj.at[2], left_sem.at[1])
+    twin = (me, 1 - lane)
+    fetch_attn = pltpu.make_async_copy(attn, d_proj.at[2], attn_sem.at[0])
     fetch_attn.start()
+    barrier = pltpu.get_barrier_semaphore()
+
+    def greet(o, carry):
+        pl.semaphore_signal(barrier, inc=1, device_id=at((pos + o) % n, core, n), device_id_type=MESH)
+        return carry
+
+    lax.fori_loop(1, n, greet, 0)
+    for other in (mate, twin):
+        pl.semaphore_signal(barrier, inc=1, device_id=other, device_id_type=MESH)
+    pl.semaphore_wait(barrier, n + 1)
+    count, _, hidden = act.shape
+    half, model = resid.shape
     q_wide = qkv.shape[1]
-    fetch_out = pltpu.make_async_copy(
-        weights.at[pl.ds(0, out_weight.shape[0]), pl.ds(q_wide, out_weight.shape[1])], out_weight, left_sem.at[2]
-    )
-    meet((*nexts, mate, twin))
-    fetch_lefts.wait()
-    fetch_out.start()
-    fetch_attn.wait()
-    count = act.shape[0]
-    model = resid.shape[1]
-    half = seq // 2
-    early, event, finish = reducer(
-        n, pos, core, nexts, mate, (lefts, act, grads, *refs[35:]), lambda m: m // 2
-    )
+    per_group = q_heads // kv_heads
+    lefts = scratch[0]
+
+    def from_flipped(first):
+        def fetch_left(m, side, there):
+            if there is None:
+                pltpu.make_async_copy(
+                    flipped.at[0, pl.ds(0, lefts.shape[1])], lefts.at[side], left_sem.at[side]
+                ).wait()
+            elif first == 0:
+                pltpu.make_async_copy(flipped.at[m // 2, there], lefts.at[side], left_sem.at[side]).start()
+            else:
+                @pl.when(m < 2)
+                def _():
+                    pltpu.make_async_copy(flipped.at[2, there], lefts.at[side], left_sem.at[side]).start()
+
+                @pl.when(m == 2)
+                def _():
+                    pltpu.make_async_copy(d_flip.at[there], lefts.at[side], left_sem.at[side]).start()
+
+        return fetch_left
+
+    links = (n, pos, core, nexts, mate)
+    begin, event, finish = reducer(
+        *links, act, (grad_gate, grad_up, grad_down), from_flipped(0), scratch, (0, 0, 2 * (n - 1))
+    )
+    late_begin, late_event, late_finish = reducer(
+        *links, d_proj, (grad_query, grad_pair, grad_out), from_flipped(2), scratch, (n, n - 1, 2 * (n - 1))
+    )
+    deep = blocks.shape[1]
+    turns = model // deep
+
+    def fetch(which, i, slot, width):
+        start = which * model + i * deep
+        return pltpu.make_async_copy(
+            weights.at[pl.ds(pl.multiple_of(start, deep), deep), pl.ds(0, width)],
+            blocks.at[slot, :, pl.ds(0, width)], load_sem.at[slot],
+        )
+
     for m in range(count):
-        early(m, 0)
+        begin(m)
+    fetch(1, 0, 0, hidden).start()
+    fetch(2, 0, 1, hidden).start()
     for m in range(count):
         event(m)
-
     theirs = pl.ds(pl.multiple_of((1 - lane) * half, half), half)
     ours = pl.ds(pl.multiple_of(lane * half, half), half)
-    deep = gate_block.shape[0]
-    turns = model // deep
-
-    def fetch(i, which):
-        target = (gate_block, up_block)[which]
-        start = (which + 1) * model + i * deep
-        return pltpu.make_async_copy(
-            weights.at[pl.ds(pl.multiple_of(start, deep), deep), :], target, load_sem.at[which]
-        )
-
-    fetch(0, 0).start()
-    fetch(0, 1).start()
-
-    def narrow(i, carry):
+    done = count
+
+    def events(number):
+        nonlocal done
+        for e in range(done, done + number):
+            event(e)
+        done = done + number
+
+    def send_part(slot, target, i):
+        return remote(part.at[slot], target, swap_sem.at[i, 0], swap_sem.at[i, 1], twin)
+
+    def dn_two(i, carry):
         there = pl.ds(pl.multiple_of(i * deep, deep), deep)
-        for which, target in enumerate((gate_block, up_block)):
-            fetch(i, which).wait()
-            other = tail_product(act[which, theirs, :], target[...])
-            same = tail_product(act[which, ours, :], target[...])
+        for which in range(2):
+            fetch(which + 1, i, which, hidden).wait()
+            other = tail_product(act[which, theirs, :], blocks[which])
+            same = tail_product(act[which, ours, :], blocks[which])
             if which == 0:
                 own[:, there] = same
                 d_resid[:, there] = other
             else:
                 own[:, there] += same
-                part[:, there] = (d_resid[:, there] + other).astype(jnp.bfloat16)
+                part[0, :, there] = (d_resid[:, there] + other).astype(jnp.bfloat16)
 
             @pl.when(i < turns - 1)
             def _():
-                fetch(i + 1, which).start()
+                fetch(which + 1, i + 1, which, hidden).start()
 
         @pl.when(i % 3 == 2)
         def _():
@@ -808,62 +851,92 @@
 
         return carry
 
-    lax.fori_loop(0, turns, narrow, 0)
-    done = count + turns // 3
-    send = remote(part, peer, swap_sem.at[0, 0], swap_sem.at[0, 1], twin)
-    send.start()
-    for e in range(done, done + 3):
-        event(e)
-    done = done + 3
-    send.wait_recv()
-    send.wait_send()
+    lax.fori_loop(0, turns, dn_two, 0)
+    done = done + turns // 3
+    sends = [send_part(0, peer.at[0], 0)]
+    sends[0].start()
+    fetch(3, 0, 0, hidden).start()
+    events(3)
+    sends[0].wait_recv()
+    sends[0].wait_send()
     strip = 32
 
-    def norm_strip(i, carry):
+    def over_strips(body):
+        lax.fori_loop(0, half // strip, body, 0)
+
+    def gather_sum(target, i, total):
+        @pl.when(i == 0)
+        def _():
+            target[...] = total
+
+        @pl.when(i > 0)
+        def _():
+            target[...] += total
+
+    def norm_two(i, carry):
         there = pl.ds(pl.multiple_of(i * strip, strip), strip)
-        incoming = own[there, :] + peer[there, :].astype(jnp.float32)
-        hidden = resid[there, :]
-        inverse = row_scale(hidden)
-        normed = hidden * inverse
+        incoming = own[there, :] + peer[0, there, :].astype(jnp.float32)
+        values = resid[there, :]
+        inverse = row_scale(values)
+        normed = values * inverse
         scaled = incoming * mlp_gain[...]
         change = cot[there, :].astype(jnp.float32) + inverse * (
             scaled - normed * jnp.mean(scaled * normed, axis=-1, keepdims=True)
         )
         d_resid[there, :] = change
-        part[there, :] = change.astype(jnp.bfloat16)
-        total = jnp.sum(incoming * normed, axis=0, keepdims=True)
-
-        @pl.when(i == 0)
-        def _():
-            mlp_sum[...] = total
-
-        @pl.when(i > 0)
-        def _():
-            mlp_sum[...] += total
-
-        return carry
-
-    lax.fori_loop(0, half // strip, norm_strip, 0)
-    send = remote(part, d_full.at[ours], swap_sem.at[1, 0], swap_sem.at[1, 1], twin)
-    send.start()
-    d_full[ours, :] = part[...]
-    fetch_out.wait()
-    columns = out_weight.shape[1]
-    quarter = columns // 4
-
-    for e in range(done, done + 3):
-        event(e)
-    done = done + 3
-    remote(part, d_full.at[theirs], swap_sem.at[1, 0], swap_sem.at[1, 1], twin).wait_recv()
-    send.wait_send()
-    for i in range(4):
-        there = pl.ds(i * quarter, quarter)
-        d_attn[:, there] = product(d_full[...], out_weight[:, there]).astype(jnp.bfloat16)
-    event(done)
-    done = done + 1
+        part[0, there, :] = change.astype(jnp.bfloat16)
+        gather_sum(mlp_sum, i, jnp.sum(incoming * normed, axis=0, keepdims=True))
+        return carry
+
+    over_strips(norm_two)
+    sends.append(send_part(0, d_full.at[ours], 1))
+    sends[1].start()
+    d_full[ours, :] = part[0]
+
+    def narrow(which, width, slot, base, rows_of):
+        def one(i, carry):
+            @pl.when(i < turns - 1)
+            def _():
+                fetch(which, i + 1, (i + 1) % 2, width).start()
+
+            fetch(which, i, i % 2, width).wait()
+            there = pl.ds(pl.multiple_of(i * deep, deep), deep)
+            for rows, mine in ((theirs, False), (ours, True)):
+                total = None
+                for left, start in rows_of(rows):
+                    gained = tail_product(left, blocks[i % 2, :, pl.ds(start, left.shape[1])])
+                    total = gained if total is None else total + gained
+                if mine:
+                    own[:, there] = total
+                else:
+                    part[slot, :, there] = total.astype(jnp.bfloat16)
+
+            @pl.when(i % 4 == 3)
+            def _():
+                event(base + i // 4)
+
+            return carry
+
+        lax.fori_loop(0, turns, one, 0)
+
+    narrow(3, hidden, 1, done, lambda rows: [(act[2, rows, :], 0)])
+    done = done + turns // 4
+    sends.append(send_part(1, peer.at[1], 2))
+    sends[2].start()
+    group_wide = per_group * HD
+
+    def fetch_columns(g):
+        return pltpu.make_async_copy(
+            weights.at[pl.ds(0, model), pl.ds(pl.multiple_of(q_wide + g * group_wide, group_wide), group_wide)],
+            columns.at[g % 2], column_sem.at[g % 2],
+        )
+
+    fetch_columns(0).start()
+    events(1)
+    remote(part.at[0], d_full.at[theirs], swap_sem.at[1, 0], swap_sem.at[1, 1], twin).wait_recv()
     flip_into(d_full, d_flip, stage, stage_sem)
-    per_group = q_heads // kv_heads
     qk_sum[...] = jnp.zeros_like(qk_sum)
+    fetch_attn.wait()
 
     def group_step(group, carry):
         places = [group * per_group + r for r in range(per_group)]
@@ -874,6 +947,13 @@
         ]
         for copy in copies:
             copy.start()
+
+        @pl.when(group < kv_heads - 1)
+        def _():
+            fetch_columns(group + 1).start()
+
+        fetch_columns(group).wait()
+        d_attn[...] = product(d_full[...], columns[group % 2]).astype(jnp.bfloat16)
         for copy in copies:
             copy.wait()
         attend_back(group, dims, heads, tab, seg_col, seg_row, gains, d_attn, d_proj, qk_sum, kept)
@@ -882,173 +962,30 @@
 
     lax.fori_loop(0, kv_heads, group_step, 0)
     done = done + kv_heads
-
-    def rest(e, carry):
-        event(e)
-        return carry
-
-    lax.fori_loop(done, count * n, rest, 0)
-    finish()
-
-
-def backward_block(
-    flipped, act, weights, qkv, attn, cot, resid, tab, segments, gains, mlp_gain, q_heads, kv_heads, dp
-):
-    n = dp // 2
-    count, seq, width = act.shape
-    half, model = resid.shape
-    rows = model // dp
-    low, dma, vmem = jnp.bfloat16, pltpu.SemaphoreType.DMA, pltpu.VMEM
-    shape = jax.ShapeDtypeStruct
-    place = lambda kind: pl.BlockSpec(memory_space=kind)
-    deep = 256
-    return pl.pallas_call(
-        functools.partial(backward_kernel, n, (q_heads, kv_heads, seq, seq // 2)),
-        out_shape=[
-            shape((count, rows, width), jnp.float32),
-            shape((3, seq, q_heads * HD), low),
-            shape((model, seq), low),
-            shape((half, model), jnp.float32),
-            shape((1, model), jnp.float32),
-            shape((8, HD), jnp.float32),
-        ],
-        in_specs=[place(pltpu.HBM), place(vmem)] + [place(pltpu.HBM)] * 3 + [place(vmem)] * 7,
-        out_specs=[place(pltpu.HBM), place(vmem), place(pltpu.HBM)] + [place(vmem)] * 3,
-        scratch_shapes=[
-            vmem((2, model, seq), low),
-            vmem((model, q_heads * HD), low),
-            vmem((seq, model), low),
-            vmem((deep, width), low),
-            vmem((deep, width), low),
-            vmem((half, model), jnp.float32),
-            vmem((half, model), low),
-            vmem((half, model), low),
-            vmem((seq, q_heads * HD), low),
-            vmem((q_heads // kv_heads + 2, seq, HD), jnp.float32),
-            vmem((3, seq, HD), jnp.float32),
-            vmem((2, 256, seq), low),
-            dma((2, 2)),
-            dma((2,)),
-            dma((q_heads // kv_heads + 2,)),
-            dma((3,)),
-            dma((2,)),
-            *reduce_scratch(n, count, rows, width // 2),
-        ],
-        compiler_params=pltpu.CompilerParams(
-            collective_id=2, has_side_effects=True, vmem_limit_bytes=67043328
-        ),
-    )(
-        flipped, act, weights, qkv, attn, cot, resid, tab,
-        segments.reshape(seq, 1), segments.reshape(1, seq), gains, mlp_gain,
-    )
-
-
-def closing_kernel(n, *refs):
-    (
-        flipped, d_flip, d_proj, weights, act, tokens, resid, d_resid, attn_gain, mlp_sum, qk_sum,
-        grads, result, input_grad, gain_out,
-        lefts, acts, first_block, second_block, own, part, peer, attn_sum, table, others, inbox,
-        swap_sem, load_sem, first_sem, second_sem, trade_sem, post_sem, mail_sem,
-    ) = refs[:33]
-    pos, core = ring_place(n)
-    me = lax.axis_index("dp")
-    lane = lax.axis_index("tensor")
-    nexts = (at((pos + 1) % n, core, n), at((pos + n - 1) % n, core, n))
-    mate = at(pos, 1 - core, n)
-    twin = (me, 1 - lane)
-    fetches = [
-        pltpu.make_async_copy(flipped.at[2], lefts.at[0], load_sem.at[0]),
-        pltpu.make_async_copy(d_flip, lefts.at[1], load_sem.at[1]),
-        pltpu.make_async_copy(act.at[2], acts, load_sem.at[2]),
-    ]
-    for fetch in fetches:
-        fetch.start()
-    barrier = pltpu.get_barrier_semaphore()
-
-    def greet(o, carry):
-        pl.semaphore_signal(barrier, inc=1, device_id=at((pos + o) % n, core, n), device_id_type=MESH)
-        return carry
-
-    lax.fori_loop(1, n, greet, 0)
-    for other in (mate, twin):
-        pl.semaphore_signal(barrier, inc=1, device_id=other, device_id_type=MESH)
-    pl.semaphore_wait(barrier, n + 1)
-    for fetch in fetches:
-        fetch.wait()
-    count, seq, width = d_proj.shape
-    half, model = resid.shape
-    early, event, finish = reducer(
-        n, pos, core, nexts, mate, (lefts, d_proj, grads, *refs[33:]), lambda m: m // 2
-    )
-    for m in range(count):
-        early(m, 0)
-    for m in range(count):
-        event(m)
-    theirs = pl.ds(pl.multiple_of((1 - lane) * half, half), half)
-    ours = pl.ds(pl.multiple_of(lane * half, half), half)
-    deep = first_block.shape[1]
-    turns = model // deep
-
-    def stream(source, offset, block, sem):
-        def fetch(i):
-            return pltpu.make_async_copy(
-                source.at[pl.ds(pl.multiple_of(offset + i * deep, deep), deep), pl.ds(0, block.shape[2])], block.at[i % 2], sem.at[i % 2]
-            )
-
-        return fetch
-
-    first_fetch = stream(weights, 0, first_block, first_sem)
-    second_fetch = stream(weights, 3 * model, second_block, second_sem)
-    first_fetch(0).start()
-
-    def narrow(which, fetch, block, rows_of, every, base):
-        def one(i, carry):
-            @pl.when(i < turns - 1)
-            def _():
-                fetch(i + 1).start()
-
-            fetch(i).wait()
-            there = pl.ds(pl.multiple_of(i * deep, deep), deep)
-            for rows, target in ((theirs, part), (ours, own)):
-                total = None
-                for left, start in rows_of(rows):
-                    gained = tail_product(left, block[i % 2, :, pl.ds(start, left.shape[1])])
-                    total = gained if total is None else total + gained
-                target[which, :, there] = total.astype(target.dtype)
-
-            @pl.when(i % every == every - 1)
-            def _():
-                event(base + i // every)
-
-            return carry
-
-        lax.fori_loop(0, turns, one, 0)
-
-    narrow(
-        0, first_fetch, first_block,
-        lambda rows: [(d_proj[0, rows, :], 0), (d_proj[1, rows, :], width)], 4, count,
-    )
-    sends = [remote(part.at[i], peer.at[i], swap_sem.at[i, 0], swap_sem.at[i, 1], twin) for i in range(2)]
-    sends[0].start()
-    second_fetch(0).start()
-    done = count + turns // 4
-    narrow(1, second_fetch, second_block, lambda rows: [(acts[rows, :], 0)], 2, done)
-    sends[1].start()
-    done = done + turns // 2
-
-    def events(number):
-        nonlocal done
-        for e in range(done, done + number):
-            event(e)
-        done = done + number
-
-    events(4)
-    sends[0].wait_recv()
-    strip = 32
-
-    def norm_strip(i, carry):
+    sends[2].wait_recv()
+
+    def last_strip(i, carry):
         there = pl.ds(pl.multiple_of(i * strip, strip), strip)
-        incoming = own[0, there, :] + peer[0, there, :].astype(jnp.float32)
+        result[there, :] = (
+            resid[there, :] + (own[there, :] + peer[1, there, :].astype(jnp.float32))
+        ).astype(jnp.bfloat16)
+        return carry
+
+    over_strips(last_strip)
+    fetch(0, 0, 0, q_wide).start()
+    sends[1].wait_send()
+    events(1)
+    width = d_proj.shape[2]
+    narrow(0, q_wide, 0, done, lambda rows: [(d_proj[0, rows, :], 0), (d_proj[1, rows, :], width)])
+    done = done + turns // 4
+    sends.append(send_part(0, peer.at[0], 3))
+    sends[3].start()
+    events(1)
+    sends[3].wait_recv()
+
+    def norm_one(i, carry):
+        there = pl.ds(pl.multiple_of(i * strip, strip), strip)
+        incoming = own[there, :] + peer[0, there, :].astype(jnp.float32)
         values = tokens[there, :].astype(jnp.float32)
         inverse = row_scale(values)
         normed = values * inverse
@@ -1057,20 +994,10 @@
             scaled - normed * jnp.mean(scaled * normed, axis=-1, keepdims=True)
         )
         input_grad[there, :] = change.astype(jnp.bfloat16)
-        total = jnp.sum(incoming * normed, axis=0, keepdims=True)
-
-        @pl.when(i == 0)
-        def _():
-            attn_sum[...] = total
-
-        @pl.when(i > 0)
-        def _():
-            attn_sum[...] += total
-
-        return carry
-
-    lax.fori_loop(0, half // strip, norm_strip, 0)
-    events(1)
+        gather_sum(attn_sum, i, jnp.sum(incoming * normed, axis=0, keepdims=True))
+        return carry
+
+    over_strips(norm_one)
     dp = 2 * n
     share, head_share = model // dp, 2 * HD // dp
     table[...] = jnp.zeros_like(table)
@@ -1095,17 +1022,18 @@
         return carry
 
     lax.fori_loop(1, n, post, 0)
-    events(3)
-    sends[1].wait_recv()
-
-    def last_strip(i, carry):
-        there = pl.ds(pl.multiple_of(i * strip, strip), strip)
-        result[there, :] = (
-            resid[there, :] + (own[1, there, :] + peer[1, there, :].astype(jnp.float32))
-        ).astype(jnp.bfloat16)
-        return carry
-
-    lax.fori_loop(0, half // strip, last_strip, 0)
+
+    def rest(e, carry):
+        event(e)
+        return carry
+
+    last = count * (n - 1)
+    lax.fori_loop(done, last, rest, 0)
+    for m in range(count):
+        event(last + m)
+        finish(m)
+        late_begin(m)
+        late_event(m)
     gain_out[...] = table[me]
 
     def collect(o, carry):
@@ -1115,14 +1043,15 @@
 
     lax.fori_loop(1, n, collect, 0)
 
-    def rest(e, carry):
-        event(e)
-        return carry
-
-    lax.fori_loop(done, count * n, rest, 0)
-    finish()
-    for send in sends:
-        send.wait_send()
+    def late_rest(e, carry):
+        late_event(e)
+        return carry
+
+    lax.fori_loop(count, count * n, late_rest, 0)
+    for m in range(count):
+        late_finish(m)
+    sends[2].wait_send()
+    sends[3].wait_send()
 
     def sent(o, carry):
         mail(o, 0).wait_send()
@@ -1131,54 +1060,82 @@
     lax.fori_loop(1, n, sent, 0)
 
 
-def closing_block(
-    flipped, d_flip, d_proj, weights, act, tokens, resid, d_resid, attn_gain, mlp_sum, qk_sum, dp
+def backward_block(
+    flipped, act, weights, qkv, attn, cot, tokens, resid, tab, segments, gains, attn_gain, mlp_gain,
+    q_heads, kv_heads, dp,
 ):
     n = dp // 2
-    count, seq, width = d_proj.shape
+    count, seq, hidden = act.shape
     half, model = resid.shape
-    hidden = act.shape[2]
     rows = model // dp
-    deep = 256
-    low, dma, vmem = jnp.bfloat16, pltpu.SemaphoreType.DMA, pltpu.VMEM
+    wide = hidden // 2
+    width = q_heads * HD
+    low, full, dma, vmem, hbm = jnp.bfloat16, jnp.float32, pltpu.SemaphoreType.DMA, pltpu.VMEM, pltpu.HBM
     shape = jax.ShapeDtypeStruct
     place = lambda kind: pl.BlockSpec(memory_space=kind)
-    hbm = pltpu.HBM
+    per_group = q_heads // kv_heads
     return pl.pallas_call(
-        functools.partial(closing_kernel, n),
+        functools.partial(backward_kernel, n, (q_heads, kv_heads, seq, seq // 2)),
         out_shape=[
-            shape((count, rows, width), jnp.float32),
+            *[shape((rows, hidden), full)] * 3,
+            *[shape((rows, width), full)] * 3,
             shape((half, model), low),
             shape((half, model), low),
-            shape((8, 128), jnp.float32),
+            shape((8, 128), full),
+            shape((model, seq), low),
         ],
-        in_specs=[place(k) for k in (hbm, hbm, vmem, hbm, hbm, *[vmem] * 6)],
-        out_specs=[place(hbm), place(vmem), place(vmem), place(vmem)],
+        in_specs=[place(k) for k in (hbm, vmem, hbm, hbm, hbm, *[vmem] * 9)],
+        out_specs=[place(k) for k in (*[hbm] * 6, vmem, vmem, vmem, hbm)],
         scratch_shapes=[
-            vmem((2, model, seq), low),
-            vmem((seq, hidden), low),
-            vmem((2, deep, 2 * width), low),
-            vmem((2, deep, hidden), low),
-            vmem((2, half, model), jnp.float32),
+            vmem((3, seq, width), low),
+            vmem((seq, model), low),
+            vmem((half, model), full),
+            vmem((2, 256, hidden), low),
+            vmem((2, model, per_group * HD), low),
+            vmem((half, model), full),
             vmem((2, half, model), low),
             vmem((2, half, model), low),
-            vmem((1, model), jnp.float32),
-            vmem((dp, 8, 128), jnp.float32),
-            vmem((2, dp, 8, 128), jnp.float32),
-            vmem((n, 8, 128), jnp.float32),
-            dma((2, 2)),
-            dma((3,)),
+            vmem((seq, per_group * HD), low),
+            vmem((per_group + 2, seq, HD), full),
+            vmem((3, seq, HD), full),
+            vmem((2, 256, seq), low),
+            vmem((1, model), full),
+            vmem((1, model), full),
+            vmem((8, HD), full),
+            vmem((dp, 8, 128), full),
+            vmem((2, dp, 8, 128), full),
+            vmem((n, 8, 128), full),
+            dma((4, 2)),
+            dma((2,)),
+            dma((per_group + 2,)),
+            dma((1,)),
             dma((2,)),
             dma((2,)),
             dma((2, 2)),
             dma((n,)),
             dma((n,)),
-            *reduce_scratch(n, count, rows, width // 2),
+            dma((2,)),
+            vmem((2, 2 * rows, seq), low),
+            vmem((count, 2, rows, wide), full),
+            vmem((2 * rows, wide), full),
+            vmem((count, 2, rows, wide), low),
+            vmem((count, 2, 2, rows, wide), low),
+            vmem((count, 2, rows, wide), low),
+            vmem((count, 2, SLOTS, rows, wide), low),
+            dma((count, 2)),
+            dma((count, 2, 2)),
+            dma((count, 2)),
+            dma((count, 2, SLOTS)),
+            pltpu.SemaphoreType.REGULAR((count, 2)),
+            dma((count, 2)),
         ],
         compiler_params=pltpu.CompilerParams(
-            collective_id=3, has_side_effects=True, vmem_limit_bytes=67043328
+            collective_id=2, has_side_effects=True, vmem_limit_bytes=67043328
         ),
-    )(flipped, d_flip, d_proj, weights, act, tokens, resid, d_resid, attn_gain, mlp_sum, qk_sum)
+    )(
+        flipped, act, weights, qkv, attn, cot, tokens, resid, tab,
+        segments.reshape(seq, 1), segments.reshape(1, seq), gains, attn_gain, mlp_gain,
+    )
 
 
 def on_device(
@@ -1222,35 +1179,24 @@
         kv_heads,
         dp,
     )
-    grads, d_projected, d_flip, d_resid, mlp_sum, qk_sum = backward_block(
+    (
+        grad_gate, grad_up, grad_down, grad_query, grad_pair, grad_out, result_rows, input_grad, gain_sums, _,
+    ) = backward_block(
         flipped,
         act,
         weights,
         projected,
         attn_rows,
         cotangent,
+        tokens,
         resid,
         rope_tab,
         seg_ids[0],
         pair,
+        attn_gain,
         mlp_gain,
         q_heads,
         kv_heads,
-        dp,
-    )
-    grad_gate, grad_up, grad_down = grads[0], grads[1], grads[2]
-    late_grads, result_rows, input_grad, gain_sums = closing_block(
-        flipped,
-        d_flip,
-        d_projected,
-        weights,
-        act,
-        tokens,
-        resid,
-        d_resid,
-        attn_gain,
-        mlp_sum,
-        qk_sum,
         dp,
     )
     share = model // dp
@@ -1258,10 +1204,10 @@
     return (
         result_rows,
         input_grad,
-        late_grads[0],
-        late_grads[1, :, :kv_width],
-        late_grads[1, :, kv_width:],
-        late_grads[2].T,
+        grad_query,
+        grad_pair[:, :kv_width],
+        grad_pair[:, kv_width:],
+        grad_out.T,
         grad_gate,
         grad_up,
         grad_down.T,

time: 591 us -> 562 us (0.951)
  Pallas kernels: 552 us -> 523 us
    pallas_call x1 -> x0, Pallas kernels: 92 us -> none  [closing_block(): pl.pallas_call(functools.partial(closing_kernel, n), out_shape=[shape((co...]
    pallas_call x1, Pallas kernels: 196 us -> 260 us  [backward_block(): pl.pallas_call(functools.partial(backward_kernel, n, (q_heads, kv_heads,...]
    transpose x2 -> x0, local copies, waits for them, and re-layouts: 6.55 us -> none  [the longest x1 4.47 us: on_device(): return (result_rows, input_grad, late_grads[0], late_grads[1, :, :kv_widt...]
    unnamed x18 -> x29, local copies, waits for them, and re-layouts: 7.57 us -> 12.9 us
where the time goes in v5:
time: 562 us; the launch traced here: 552 us
  Pallas kernels  523 us (93%)
  local copies, waits for them, and re-layouts  19.2 us (3%)
  other arithmetic  8.75 us (2%)
    pallas_call x1, Pallas kernels, forward_block(): pl.pallas_call(functools.partial(forward_kernel, n, (q_heads, kv_heads, s...  263 us
    pallas_call x1, Pallas kernels, backward_block(): pl.pallas_call(functools.partial(backward_kernel, n, (q_heads, kv_heads,...  260 us
    unnamed x29, local copies, waits for them, and re-layouts  12.9 us

profile of v5, /device:TPU:0, one launch (start us, length us, event | category | flops | bytes accessed | tf_op | source)
XLA Modules:
  0.0 552.1 jit_solution(17739191371309141711)
XLA Ops:
  0.7 0.7 bitcast_convert_fusion.1
  1.3 0.7 bitcast_convert_fusion
  2.0 1.0 convert_reduce_fusion
  3.0 0.7 pad_convert_fusion
  3.7 0.2 dynamic_update_slice.14.refs_2_
  3.9 0.0 copy-start.9
  3.9 0.6 copy-done.9
  4.5 1.5 copy.37.refs_6_.refs_9_
  6.0 1.1 copy.35
  7.1 2.0 pad_maximum_fusion.1.refs_0_
  9.1 0.0 copy-start.7
  9.1 1.0 multiply_cosine_fusion
  10.1 0.2 maximum_bitcast_fusion
  10.3 0.0 copy-start.5
  10.3 0.0 copy-start.6
  10.4 0.8 pad_maximum_fusion.2.refs_5_.refs_8_
  11.2 0.0 copy-done.7
  11.2 0.3 copy.36
  11.5 0.2 copy-done.5
  11.7 0.2 copy-done.6
  11.9 1.7 pad_maximum_fusion.refs_1_
  13.6 263.4 %shard_map.220 = (bf16[8192,3072]{1,0:T(8,128)(2,1)}, f32[512,2048]{1,0:T(8,128)}, bf16[512,1024]{1,0:T(8,128)(2,1)}, f32[256,2048]{1,0:T(8,128)}, bf16[3,2048,5...) custom-call(bf16[128,3072]{1,0:T(8,128)(2,1)} %pad_maximum_fusion.1., ...), custom_call_target="tpu_custom_call" | custom-call | tf_op jit(solution)/shard_map/pallas_call | solution.py:527
  277.0 259.6 %shard_map.221 = (f32[128,3072]{1,0:T(8,128)}, f32[128,3072]{1,0:T(8,128)}, f32[128,3072]{1,0:T(8,128)}, f32[128,1024]{1,0:T(8,128)}, f32[128,1024]{1,0:T(8,128)...) custom-call(bf16[3,2048,512]{2,1,0:T(8,128)(2,1)} %get-tuple-element, ...), custom_call_target="tpu_custom_call" | custom-call | tf_op jit(solution)/shard_map/pallas_call | solution.py:1077
  536.6 0.0 copy-start.2
  536.6 1.4 dynamic-slice_bitcast_fusion
  538.0 1.3 slice_bitcast_fusion
  539.3 2.0 copy.39
  541.3 1.9 fusion.1
  543.2 0.0 copy-done.2
  543.2 0.0 copy-start.4
  543.2 1.6 copy.40
  544.8 0.0 copy-done.4
  544.8 0.0 copy-start.3
  544.8 1.0 copy.48
  545.8 0.6 copy-done.3
  546.4 0.0 copy-start.8
  546.4 0.0 copy-start.1
  546.4 1.0 copy.49
  547.4 0.4 copy-done.8
  547.8 0.8 copy.50
  548.6 0.0 copy-done.1
  548.6 0.0 copy-start
  548.6 1.1 copy.51
  549.7 0.8 copy-done
  550.5 1.1 copy.52
  (3 shorter events, 0.0 us)
Async XLA Ops:
  3.9 0.6 copy-start.9
  9.1 2.1 copy-start.7
  10.3 1.3 copy-start.5
  10.3 1.6 copy-start.6
  536.6 6.5 %copy-start.2 = (f32[128,3072]{1,0:T(8,128)S(1)}, f32[128,3072]{1,0:T(8,128)}, u32[]{:S(2)}) copy-start(f32[128,3072]{1,0:T(8,128)} %get-tuple-element.46) | copy-start | bytes 4718596
  543.2 1.6 copy-start.4
  544.8 1.6 copy-start.3
  546.4 1.4 copy-start.8
  546.4 2.2 copy-start.1
  548.6 2.0 copy-start

commit v6 on v5

--- a/solution.py
+++ b/solution.py
@@ -1,6 +1,7 @@
 import functools
 import jax
 import jax.numpy as jnp
+import numpy as np
 from jax import lax
 from jax.experimental import pallas as pl
 from jax.experimental.pallas import tpu as pltpu
@@ -58,43 +59,6 @@
     return lax.dot_general(
         left, right, (((1,), (1,)), ((), ())), preferred_element_type=jnp.float32
     )
-
-
-def norm_rows(values):
-    return lax.rsqrt(jnp.mean(values * values, axis=-1, keepdims=True) + epsilon)
-
-
-def norm_back(incoming, normed, inverse):
-    return inverse * (incoming - normed * jnp.mean(incoming * normed, axis=-1, keepdims=True))
-
-
-def rotate(values, cosine_table, sine_table):
-    half_width = values.shape[-1] // 2
-    turned = jnp.concatenate([-values[..., half_width:], values[..., :half_width]], axis=-1)
-    return values * cosine_table + turned * sine_table
-
-
-def rotate_back(incoming, cosine_table, sine_table):
-    half_width = incoming.shape[-1] // 2
-    scaled = incoming * sine_table
-    return incoming * cosine_table + jnp.concatenate(
-        [scaled[..., half_width:], -scaled[..., :half_width]], axis=-1
-    )
-
-
-def tables(segments):
-    seq_len = segments.shape[0]
-    token_index = jnp.arange(seq_len, dtype=jnp.int32)
-    doc_start = jnp.sum((segments[None, :] < segments[:, None]).astype(jnp.int32), axis=1)
-    doc_pos = (token_index - doc_start).astype(jnp.float32)
-    frequency = rope_base ** (-jnp.arange(0, HD, 2).astype(jnp.float32) / HD)
-    angles = doc_pos[:, None] * frequency[None, :]
-    cosine_table = jnp.concatenate([jnp.cos(angles), jnp.cos(angles)], axis=1)
-    sine_table = jnp.concatenate([jnp.sin(angles), jnp.sin(angles)], axis=1)
-    allowed = (segments[:, None] == segments[None, :]) & (
-        token_index[None, :] <= token_index[:, None]
-    )
-    return (cosine_table, sine_table, allowed)
 
 
 def turn(values):
@@ -181,8 +145,9 @@
 
 def forward_kernel(n, dims, *refs):
     (
-        mixed, ffn_shards, tile, tokens, cot, tab, seg_col, seg_row,
-        weights, qkv_out, attn, resid, flipped, act, attn_gain, mlp_gain, gains,
+        query_shard, key_shard, value_shard, out_shard, gate_shard, up_shard, down_shard,
+        tokens, cot, frequency, seg_row, attn_share, mlp_share, qk_share,
+        weights, qkv_out, attn, resid, flipped, act, attn_gain, mlp_gain, gains, tab, seg_col,
         full_rows, cot_full, full_two, out_weight, columns, box, kept, part, peer, acc, blocks, stage,
         own_sem, send_sem, recv_sem, give_sem, take_sem, swap_sem, load_sem, stage_sem, column_sem, tile_sem,
     ) = refs
@@ -193,13 +158,22 @@
     nexts = (at((pos + 1) % n, core, n), at((pos + n - 1) % n, core, n))
     mate = at(pos, 1 - core, n)
     twin = (me, 1 - lane)
-    count, rows, width = ffn_shards.shape
+    ffn_shards = (gate_shard, up_shard, down_shard)
+    count = len(ffn_shards)
+    rows, width = gate_shard.shape
     wide = width // 2
-    narrow = wide // 2
+    q_span, kv_span = query_shard.shape[1], key_shard.shape[1]
     model = 2 * n * rows
     half = seq // 2
     theirs = pl.ds(pl.multiple_of((1 - lane) * half, half), half)
     ours = pl.ds(pl.multiple_of(lane * half, half), half)
+    tile = box.at[me]
+    tile[...] = jnp.zeros(tile.shape, jnp.float32)
+    for i, gain in enumerate((attn_share, mlp_share, qk_share)):
+        size = gain.shape[1]
+        tile[i : i + 1, 0:size] = gain[...].astype(jnp.float32)
+        if size % 128:
+            tile[i : i + 1, :] = pltpu.roll(tile[i : i + 1, :], me * size % 128, 1)
     meet((*nexts, mate, twin))
 
     def owner_of(side, step):
@@ -208,10 +182,16 @@
         return (pos + step) % n
 
     def small(sub, side):
-        return (sub, 0, pl.ds(side * wide + sub * narrow, narrow), mixed)
+        start, source = (
+            ((0, query_shard), (q_span + 2 * kv_span, out_shard)),
+            ((q_span, key_shard), (q_span + kv_span, value_shard)),
+        )[sub][side]
+        return (sub, 0, pl.ds(start, source.shape[1]), source)
 
     def large(w, side):
-        return (w + 2, (w + 1) * model, pl.ds(side * wide, wide), None if not isinstance(w, int) else ffn_shards.at[w])
+        columns = pl.ds(side * wide, wide)
+        source = ffn_shards[w].at[:, columns] if isinstance(w, int) else None
+        return (w + 2, (w + 1) * model, columns, source)
 
     def spot(message, chip, who):
         start = message[1] + (chip * 2 + who) * rows
@@ -234,7 +214,7 @@
 
     def begin(message, side):
         k = message[0]
-        source = message[3].at[:, message[2]]
+        source = message[3]
         here = spot(message, chip_at(pos, n), core)
         remote(source, here, send_sem.at[k, side, 1], recv_sem.at[k, side, 1], nexts[side]).start()
         remote(source, here, give_sem.at[k, side, 0], take_sem.at[k, side, 0], mate).start()
@@ -252,7 +232,6 @@
         place = chip_at(owner_of(0, step), n) * 2 + who
         return remote(box.at[place], box.at[place], tile_sem.at[2, step], tile_sem.at[3, step], mate)
 
-    box[me] = tile[...]
     swaps = [
         remote(source, target.at[ours], swap_sem.at[i, 0], swap_sem.at[i, 1], twin)
         for i, (source, target) in enumerate(((tokens, full_rows), (cot, cot_full)))
@@ -292,7 +271,22 @@
                 pass_on(small(sub, side), side, step)
         return carry
 
-    lax.fori_loop(1, n - 1, mixed_step, 0)
+    def mixed_steps(first, last):
+        lax.fori_loop(first, last, mixed_step, 0)
+
+    mixed_steps(1, 3)
+    row = lax.broadcasted_iota(jnp.int32, (seq, seq), 0)
+    column = lax.broadcasted_iota(jnp.int32, (seq, seq), 1)
+    ids = jnp.broadcast_to(seg_row[...], (seq, seq)).astype(jnp.float32)
+    own_id = jnp.sum(jnp.where(row == column, ids, 0.0), axis=1, keepdims=True)
+    doc_start = jnp.sum(jnp.where(ids < own_id, 1.0, 0.0), axis=1, keepdims=True)
+    place = lax.broadcasted_iota(jnp.int32, (seq, 1), 0).astype(jnp.float32)
+    seg_col[...] = own_id.astype(jnp.int32)
+    angles = (place - doc_start) * frequency[...]
+    tab[0] = jnp.cos(angles)
+    sign = jnp.where(lax.broadcasted_iota(jnp.int32, angles.shape, 1) < HD // 2, -1.0, 1.0)
+    tab[1] = jnp.sin(angles) * sign
+    mixed_steps(3, n - 1)
     pass_tile(n - 1)
     for w in range(count):
         for side in range(2):
@@ -305,6 +299,13 @@
         step, w = event // count + 1, event % count
         for side in range(2):
             pass_on(large(w, side), side, step)
+
+    def services(first, last):
+        def one(event, carry):
+            service(event)
+            return carry
+
+        lax.fori_loop(first, last, one, 0)
 
     def gathered(step, carry):
         for sub in range(2):
@@ -373,8 +374,7 @@
     save_qkv.start()
     service(0)
 
-    def load(job, side):
-        step, w = job // count, job % count
+    def load(step, w, side):
         start = (w + 1) * model + chip_at(owner_of(side, step), n) * 2 * rows
         return pltpu.make_async_copy(
             weights.at[pl.ds(pl.multiple_of(start, 2 * rows), 2 * rows), pl.ds(side * wide, wide)],
@@ -390,9 +390,9 @@
             def _():
                 keep_own(large(w, side), side).wait()
 
-            load(job, side).start()
+            load(step, w, side).start()
         for side in range(2):
-            load(job, side).wait()
+            load(step, w, side).wait()
             chip = chip_at(owner_of(side, step), n)
 
             def with_left(left):
@@ -427,26 +427,27 @@
 
     groups = (qkv, tab, seg_col, seg_row, gains, attn, kept)
 
-    def attend(first, last):
+    def attend():
         def one(group, carry):
             attend_group(group, dims, *groups)
+
+            @pl.when(group % (kv_heads // 2) == kv_heads // 2 - 1)
+            def _():
+                service(1 + group // (kv_heads // 2))
+
             return carry
 
-        lax.fori_loop(first, last, one, 0)
+        lax.fori_loop(0, kv_heads, one, 0)
 
     flip(full_two, 2)
-    attend(0, kv_heads // 2)
-    service(1)
-    attend(kv_heads // 2, kv_heads)
-    service(2)
+    attend()
     fetch_out.wait()
     part[...] = tail_product(attn[theirs, :], out_weight[...]).astype(jnp.bfloat16)
     swaps[1].wait_recv()
     send_part = remote(part, peer, swap_sem.at[2, 0], swap_sem.at[2, 1], twin)
     send_part.start()
     resid[...] = tokens[...].astype(jnp.float32) + tail_product(attn[ours, :], out_weight[...])
-    service(3)
-    service(4)
+    services(3, 5)
     flip(cot_full, 1)
     service(5)
     send_part.wait_recv()
@@ -458,27 +459,25 @@
     send_two.start()
     full_two[ours, :] = part[...]
     ready = 9
-    for event in range(6, ready):
-        service(event)
+    services(6, ready)
     remote(part, full_two.at[theirs], swap_sem.at[3, 0], swap_sem.at[3, 1], twin).wait_recv()
     flip(full_two, 0)
     save_qkv.wait()
 
+    def works(first, last):
+        def one(job, carry):
+            work(job)
+            return carry
+
+        lax.fori_loop(first, last, one, 0)
+
+    pairs = ready + 3
+
     def both(i, carry):
         service(ready + i)
-
-        @pl.when(i < ready + 3)
-        def _():
-            def one(q, carry):
-                work(2 * i + q)
-                return carry
-
-            lax.fori_loop(0, 2, one, 0)
-
-        @pl.when(i >= ready + 3)
-        def _():
-            work(ready + 3 + i)
-
+        several = 1 - jnp.minimum(i // pairs, 1)
+        first = several * 2 * i + (1 - several) * (pairs + i)
+        works(first, first + 1 + several)
         return carry
 
     lax.fori_loop(0, count * (n - 1) - ready, both, 0)
@@ -515,41 +514,44 @@
         swap.wait_send()
 
 
-def forward_block(mixed, ffn_shards, tile, tokens, cot, tab, segments, q_heads, kv_heads, dp):
+def forward_block(shards, tokens, cot, frequency, seg_row, shares, q_heads, kv_heads, dp):
     n = dp // 2
-    count, rows, width = ffn_shards.shape
+    rows, width = shards[-1].shape
+    count = 3
     half, model = tokens.shape
     seq = 2 * half
     q_wide = (q_heads + 2 * kv_heads) * HD
-    low, dma, vmem, hbm = jnp.bfloat16, pltpu.SemaphoreType.DMA, pltpu.VMEM, pltpu.HBM
+    low, full, dma, vmem, hbm = jnp.bfloat16, jnp.float32, pltpu.SemaphoreType.DMA, pltpu.VMEM, pltpu.HBM
     shape = jax.ShapeDtypeStruct
     place = lambda kind: pl.BlockSpec(memory_space=kind)
     return pl.pallas_call(
         functools.partial(forward_kernel, n, (q_heads, kv_heads, seq, seq // 2)),
         out_shape=[
             shape(((count + 1) * model, width), low),
-            shape((seq, q_wide), jnp.float32),
+            shape((seq, q_wide), full),
             shape((seq, q_heads * HD), low),
-            shape((half, model), jnp.float32),
+            shape((half, model), full),
             shape((3, model, seq), low),
             shape((count, seq, width), low),
-            shape((1, model), jnp.float32),
-            shape((1, model), jnp.float32),
-            shape((2, HD), jnp.float32),
+            shape((1, model), full),
+            shape((1, model), full),
+            shape((2, HD), full),
+            shape((2, seq, HD), full),
+            shape((seq, 1), jnp.int32),
         ],
-        in_specs=[place(vmem)] * 8,
-        out_specs=[place(k) for k in (hbm, hbm, vmem, vmem, hbm, vmem, vmem, vmem, vmem)],
+        in_specs=[place(vmem)] * 14,
+        out_specs=[place(k) for k in (hbm, hbm, vmem, vmem, hbm, *[vmem] * 6)],
         scratch_shapes=[
             vmem((seq, model), low),
             vmem((seq, model), low),
             vmem((seq, model), low),
             vmem((model, width - q_wide), low),
             vmem((2, model, 256), low),
-            vmem((dp, 8, 128), jnp.float32),
+            vmem((dp, 8, 128), full),
             vmem((2, seq, HD), low),
             vmem((half, model), low),
             vmem((half, model), low),
-            vmem((count, seq, width), jnp.float32),
+            vmem((count, seq, width), full),
             vmem((2, 2 * rows, width // 2), low),
             vmem((2, 256, seq), low),
             dma((count + 2, 2)),
@@ -566,7 +568,7 @@
         compiler_params=pltpu.CompilerParams(
             collective_id=1, has_side_effects=True, vmem_limit_bytes=67043328
         ),
-    )(mixed, ffn_shards, tile, tokens, cot, tab, segments.reshape(seq, 1), segments.reshape(1, seq))
+    )(*shards, tokens, cot, frequency, seg_row, *shares)
 
 
 SLOTS = 3
@@ -734,7 +736,7 @@
     def finish(m):
         for side in range(2):
             given(m, side, n - 1).wait_send()
-            written(m, side, m).wait()
+            written(m, side, 0).wait()
 
     return begin, event, finish
 
@@ -809,20 +811,28 @@
             blocks.at[slot, :, pl.ds(0, width)], load_sem.at[slot],
         )
 
-    for m in range(count):
+    def first_m(m, carry):
         begin(m)
+        return carry
+
+    lax.fori_loop(0, count, first_m, 0)
     fetch(1, 0, 0, hidden).start()
     fetch(2, 0, 1, hidden).start()
-    for m in range(count):
-        event(m)
+    def run(first, last):
+        def one(e, carry):
+            event(e)
+            return carry
+
+        lax.fori_loop(first, last, one, 0)
+
+    run(0, count)
     theirs = pl.ds(pl.multiple_of((1 - lane) * half, half), half)
     ours = pl.ds(pl.multiple_of(lane * half, half), half)
     done = count
 
     def events(number):
         nonlocal done
-        for e in range(done, done + number):
-            event(e)
+        run(done, done + number)
         done = done + number
 
     def send_part(slot, target, i):
@@ -1007,12 +1017,17 @@
         table[d, 0:1, :] = attn_sum[:, start : start + 128]
         table[d, 1:2, :] = mlp_sum[:, start : start + 128]
         table[d, 2:3, :] = qk_sum[row : row + 1, :]
-    for i, partner in enumerate((twin, mate)):
-        trade = remote(table, others.at[i], trade_sem.at[i, 0], trade_sem.at[i, 1], partner)
-        trade.start()
-        events(1)
-        trade.wait()
+    def trade(i, carry):
+        partner = ((1 - i) * me + i * mate[0], (1 - i) * twin[1] + i * lane)
+        swap = remote(table, others.at[i], trade_sem.at[i, 0], trade_sem.at[i, 1], partner)
+        swap.start()
+        event(done + i)
+        swap.wait()
         table[...] += others[i]
+        return carry
+
+    lax.fori_loop(0, 2, trade, 0)
+    done = done + 2
 
     def mail(o, target):
         return remote(table.at[target], inbox.at[o], post_sem.at[o], mail_sem.at[o], at((pos + o) % n, core, n))
@@ -1023,17 +1038,17 @@
 
     lax.fori_loop(1, n, post, 0)
 
-    def rest(e, carry):
-        event(e)
-        return carry
-
     last = count * (n - 1)
-    lax.fori_loop(done, last, rest, 0)
-    for m in range(count):
+    run(done, last)
+
+    def hand_over(m, carry):
         event(last + m)
         finish(m)
         late_begin(m)
         late_event(m)
+        return carry
+
+    lax.fori_loop(0, count, hand_over, 0)
     gain_out[...] = table[me]
 
     def collect(o, carry):
@@ -1061,7 +1076,7 @@
 
 
 def backward_block(
-    flipped, act, weights, qkv, attn, cot, tokens, resid, tab, segments, gains, attn_gain, mlp_gain,
+    flipped, act, weights, qkv, attn, cot, tokens, resid, tab, seg_col, seg_row, gains, attn_gain, mlp_gain,
     q_heads, kv_heads, dp,
 ):
     n = dp // 2
@@ -1133,9 +1148,63 @@
             collective_id=2, has_side_effects=True, vmem_limit_bytes=67043328
         ),
     )(
-        flipped, act, weights, qkv, attn, cot, tokens, resid, tab,
-        segments.reshape(seq, 1), segments.reshape(1, seq), gains, attn_gain, mlp_gain,
+        flipped, act, weights, qkv, attn, cot, tokens, resid, tab, seg_col, seg_row, gains, attn_gain, mlp_gain,
     )
+
+
+def finishing_kernel(dp, *refs):
+    gains = refs[0]
+    sources, outs = refs[1:9], refs[9:21]
+    bufs, turned, in_sem, out_sem = refs[21:29], refs[29:31], refs[31], refs[32]
+    loads = [pltpu.make_async_copy(source, buf, in_sem.at[i]) for i, (source, buf) in enumerate(zip(sources, bufs))]
+    for load in loads:
+        load.start()
+    half = outs[3].shape[1]
+    stores = [None] * 9
+
+    def store(i, buf, out):
+        stores[i] = pltpu.make_async_copy(buf, out, out_sem.at[i])
+        stores[i].start()
+
+    for i, (which, out) in enumerate(((6, 0), (7, 1), (3, 2), (0, 6), (1, 7))):
+        loads[which].wait()
+        store(i, bufs[which], outs[out])
+    loads[4].wait()
+    store(5, bufs[4].at[:, pl.ds(0, half)], outs[3])
+    store(6, bufs[4].at[:, pl.ds(half, half)], outs[4])
+    for i, (which, out) in enumerate(((2, 8), (5, 5))):
+        loads[which].wait()
+        turned[i][...] = bufs[which][...].T
+        store(7 + i, turned[i], outs[out])
+    me = lax.axis_index("dp")
+    for row in range(3):
+        target = outs[9 + row]
+        size = target.shape[1]
+        line = gains[row : row + 1, :]
+        if size % 128:
+            line = pltpu.roll(line, (128 - me * size % 128) % 128, 1)
+        target[...] = line[:, :size]
+    for copy in stores:
+        copy.wait()
+
+
+def finishing_block(gains, arrays, shapes, dp):
+    full, dma, vmem, hbm = jnp.float32, pltpu.SemaphoreType.DMA, pltpu.VMEM, pltpu.HBM
+    place = lambda kind: pl.BlockSpec(memory_space=kind)
+    return pl.pallas_call(
+        functools.partial(finishing_kernel, dp),
+        out_shape=shapes,
+        in_specs=[place(vmem)] + [place(hbm)] * 8,
+        out_specs=[place(hbm)] * 9 + [place(vmem)] * 3,
+        scratch_shapes=[
+            *[vmem(a.shape, a.dtype) for a in arrays],
+            vmem(arrays[2].shape[::-1], full),
+            vmem(arrays[5].shape[::-1], full),
+            dma((8,)),
+            dma((9,)),
+        ],
+        compiler_params=pltpu.CompilerParams(vmem_limit_bytes=67043328),
+    )(gains, *arrays)
 
 
 def on_device(
@@ -1154,27 +1223,19 @@
     cotangent,
 ):
     dp = lax.axis_size("dp")
-    model = tokens.shape[1]
-    me = lax.axis_index("dp")
-    tile = jnp.zeros((8, 128), jnp.float32)
-    for row, gain in enumerate((gain_attn, gain_mlp, gain_qk)):
-        spot = me * gain.shape[0] % 128 if gain.shape[0] % 128 else 0
-        tile = lax.dynamic_update_slice(tile, gain.astype(jnp.float32)[None, :], (row, spot))
-    q_width = w_query.shape[1]
-    kv_width = w_key.shape[1]
-    q_heads = q_width // HD
-    kv_heads = kv_width // HD
-    cosine_table, sine_table, _ = tables(seg_ids[0])
-    signed = jnp.concatenate([-sine_table[:, : HD // 2], sine_table[:, HD // 2 :]], axis=1)
-    rope_tab = jnp.stack([cosine_table, signed])
-    weights, projected, attn_rows, resid, flipped, act, attn_gain, mlp_gain, pair = forward_block(
-        jnp.concatenate([w_query, w_key, w_value, w_output.T], axis=1),
-        jnp.stack([w_gate, w_up, w_down.T]),
-        tile,
+    q_heads = w_query.shape[1] // HD
+    kv_heads = w_key.shape[1] // HD
+    places = np.arange(HD) % (HD // 2) * 2
+    frequency = jnp.asarray((rope_base ** (-places / HD)).astype(np.float32)[None, :])
+    (
+        weights, projected, attn_rows, resid, flipped, act, attn_gain, mlp_gain, pair, rope_tab, seg_col,
+    ) = forward_block(
+        (w_query, w_key, w_value, w_output.T, w_gate, w_up, w_down.T),
         tokens,
         cotangent,
-        rope_tab,
-        seg_ids[0],
+        frequency,
+        seg_ids,
+        [g[None, :] for g in (gain_attn, gain_mlp, gain_qk)],
         q_heads,
         kv_heads,
         dp,
@@ -1191,7 +1252,8 @@
         tokens,
         resid,
         rope_tab,
-        seg_ids[0],
+        seg_col,
+        seg_ids,
         pair,
         attn_gain,
         mlp_gain,
@@ -1199,22 +1261,20 @@
         kv_heads,
         dp,
     )
-    share = model // dp
-    qk_share = 2 * HD // dp
-    return (
-        result_rows,
-        input_grad,
-        grad_query,
-        grad_pair[:, :kv_width],
-        grad_pair[:, kv_width:],
-        grad_out.T,
-        grad_gate,
-        grad_up,
-        grad_down.T,
-        lax.dynamic_slice(gain_sums, (0, me * share % 128), (1, share))[0],
-        lax.dynamic_slice(gain_sums, (1, me * share % 128), (1, share))[0],
-        lax.dynamic_slice(gain_sums, (2, me * qk_share % HD), (1, qk_share))[0],
+    full = jnp.float32
+    shapes = [jax.ShapeDtypeStruct(tokens.shape, jnp.bfloat16)] * 2
+    shapes += [
+        jax.ShapeDtypeStruct(w.shape, full)
+        for w in (w_query, w_key, w_value, w_output, w_gate, w_up, w_down)
+    ]
+    shapes += [jax.ShapeDtypeStruct((1, g.shape[0]), full) for g in (gain_attn, gain_mlp, gain_qk)]
+    outs = finishing_block(
+        gain_sums,
+        [grad_gate, grad_up, grad_down, grad_query, grad_pair, grad_out, result_rows, input_grad],
+        shapes,
+        dp,
     )
+    return (*outs[:9], *(g.reshape(-1) for g in outs[9:]))
 
 
 def solution(mesh):

time: 562 us -> 538 us (0.957); the launches traced: 552 us -> 536 us
  local copies, waits for them, and re-layouts: 19.2 us -> 4.08 us
  other arithmetic: 8.75 us -> 0 us
  Pallas kernels: 523 us -> 531 us
    unnamed x29 -> x2, local copies, waits for them, and re-layouts: 12.9 us -> 4.08 us
    pallas_call x0 -> x1, Pallas kernels: none -> 7.73 us  [finishing_block(): pl.pallas_call(functools.partial(finishing_kernel, dp), out_shape=shapes,...]
where the time goes in v6:
time: 538 us; the launch traced here: 536 us
  Pallas kernels  531 us (99%)
    pallas_call x1, Pallas kernels, forward_block(): pl.pallas_call(functools.partial(forward_kernel, n, (q_heads, kv_heads, s...  264 us
    pallas_call x1, Pallas kernels, backward_block(): pl.pallas_call(functools.partial(backward_kernel, n, (q_heads, kv_heads,...  259 us

profile of v6, /device:TPU:0, one launch (start us, length us, event | category | flops | bytes accessed | tf_op | source)
XLA Modules:
  0.0 536.0 jit_solution(12817624495862961399)
XLA Ops:
  0.6 1.8 copy.26
  2.4 2.3 copy.27
  4.7 264.3 %shard_map.229 = (bf16[8192,3072]{1,0:T(8,128)(2,1)}, f32[512,2048]{1,0:T(8,128)}, bf16[512,1024]{1,0:T(8,128)(2,1)}, f32[256,2048]{1,0:T(8,128)}, bf16[3,2048,5...) custom-call(bf16[128,1024]{1,0:T(8,128)(2,1)} %refs_0_.1, ...), custom_call_target="tpu_custom_call" | custom-call | tf_op jit(solution)/shard_map/pallas_call | solution.py:527
  269.1 259.0 %shard_map.230 = (f32[128,3072]{1,0:T(8,128)}, f32[128,3072]{1,0:T(8,128)}, f32[128,3072]{1,0:T(8,128)}, f32[128,1024]{1,0:T(8,128)}, f32[128,1024]{1,0:T(8,128)...) custom-call(bf16[3,2048,512]{2,1,0:T(8,128)(2,1)} %get-tuple-element, ...), custom_call_target="tpu_custom_call" | custom-call | tf_op jit(solution)/shard_map/pallas_call | solution.py:1092
  528.1 7.7 %shard_map.231 = (bf16[256,2048]{1,0:T(8,128)(2,1)}, bf16[256,2048]{1,0:T(8,128)(2,1)}, f32[128,1024]{1,0:T(8,128)}, f32[128,512]{1,0:T(8,128)}, f32[128,512]{1,...) custom-call(f32[8,128]{1,0:T(8,128)} %get-tuple-element.55.refs_0_, ...), custom_call_target="tpu_custom_call" | custom-call | tf_op jit(solution)/shard_map/pallas_call | solution.py:1194

commit v7 on v6

--- a/solution.py
+++ b/solution.py
@@ -118,6 +118,10 @@
     for i in range(1, fold):
         picked = jnp.where(index % fold == i, tile[:, i * width : (i + 1) * width], picked)
     return picked
+
+
+HALFWAY = 6
+READY = 9
 
 
 def flip_into(source, target, stage, stage_sem):
@@ -238,9 +242,8 @@
     ]
     remote(tile, box.at[me], tile_sem.at[0, 1], tile_sem.at[1, 1], nexts[0]).start()
     remote(tile, box.at[me], tile_sem.at[2, 0], tile_sem.at[3, 0], mate).start()
-    for sub in range(2):
-        for side in range(2):
-            begin(small(sub, side), side)
+    for side in range(2):
+        begin(small(0, side), side)
     for swap in swaps:
         swap.start()
     full_rows[ours, :] = tokens[...]
@@ -274,7 +277,6 @@
     def mixed_steps(first, last):
         lax.fori_loop(first, last, mixed_step, 0)
 
-    mixed_steps(1, 3)
     row = lax.broadcasted_iota(jnp.int32, (seq, seq), 0)
     column = lax.broadcasted_iota(jnp.int32, (seq, seq), 1)
     ids = jnp.broadcast_to(seg_row[...], (seq, seq)).astype(jnp.float32)
@@ -286,14 +288,16 @@
     tab[0] = jnp.cos(angles)
     sign = jnp.where(lax.broadcasted_iota(jnp.int32, angles.shape, 1) < HD // 2, -1.0, 1.0)
     tab[1] = jnp.sin(angles) * sign
-    mixed_steps(3, n - 1)
+    for side in range(2):
+        begin(small(1, side), side)
+    mixed_steps(1, n - 1)
     pass_tile(n - 1)
-    for w in range(count):
-        for side in range(2):
-            begin(large(w, side), side)
-        if w < 2:
-            for side in range(2):
-                pass_on(small(w, side), side, n - 1)
+    for side in range(2):
+        pass_on(small(0, side), side, n - 1)
+    for side in range(2):
+        begin(large(0, side), side)
+    for side in range(2):
+        pass_on(small(1, side), side, n - 1)
 
     def service(event):
         step, w = event // count + 1, event % count
@@ -320,7 +324,7 @@
             keep_own(small(sub, side), side).wait()
     q_wide = (q_heads + 2 * kv_heads) * HD
     fetch_out = pltpu.make_async_copy(
-        weights.at[pl.ds(0, model), pl.ds(q_wide, width - q_wide)], out_weight, load_sem.at[0]
+        weights.at[pl.ds(0, model), pl.ds(q_wide, width - q_wide)], out_weight, load_sem.at[0, 0]
     )
     turns = q_wide // columns.shape[2]
     deep = columns.shape[2]
@@ -358,6 +362,8 @@
         return carry
 
     lax.fori_loop(0, seq // strip, norm_strip, 0)
+    for side in range(2):
+        begin(large(1, side), side)
     qkv = acc.at[count - 1]
 
     def project(i, carry):
@@ -370,29 +376,35 @@
         return carry
 
     lax.fori_loop(0, turns, project, 0)
-    save_qkv = pltpu.make_async_copy(qkv.at[:, pl.ds(0, q_wide)], qkv_out, load_sem.at[1])
+    save_qkv = pltpu.make_async_copy(qkv.at[:, pl.ds(0, q_wide)], qkv_out, load_sem.at[0, 1])
     save_qkv.start()
+    for side in range(2):
+        begin(large(2, side), side)
     service(0)
 
-    def load(step, w, side):
+    def load(job, side):
+        step, w = job // count, job % count
         start = (w + 1) * model + chip_at(owner_of(side, step), n) * 2 * rows
         return pltpu.make_async_copy(
             weights.at[pl.ds(pl.multiple_of(start, 2 * rows), 2 * rows), pl.ds(side * wide, wide)],
-            blocks.at[side], load_sem.at[side],
+            blocks.at[job % 2, side], load_sem.at[job % 2, side],
         )
+
+    def prepare(job):
+        step, w = job // count, job % count
+        for side in range(2):
+            hand(large(w, side), side, step, 1 - core).wait_recv()
+
+            @pl.when(step == 0)
+            def _():
+                keep_own(large(w, side), side).wait()
+
+            load(job, side).start()
 
     def work(job):
         step, w = job // count, job % count
         for side in range(2):
-            hand(large(w, side), side, step, 1 - core).wait_recv()
-
-            @pl.when(step == 0)
-            def _():
-                keep_own(large(w, side), side).wait()
-
-            load(step, w, side).start()
-        for side in range(2):
-            load(step, w, side).wait()
+            load(job, side).wait()
             chip = chip_at(owner_of(side, step), n)
 
             def with_left(left):
@@ -400,7 +412,9 @@
 
                 def one(i, carry):
                     there = pl.ds(pl.multiple_of(side * wide + i * tile_width, tile_width), tile_width)
-                    gained = product(left, blocks[side, :, pl.ds(pl.multiple_of(i * tile_width, tile_width), tile_width)])
+                    gained = product(
+                        left, blocks[job % 2, side, :, pl.ds(pl.multiple_of(i * tile_width, tile_width), tile_width)]
+                    )
 
                     @pl.when(step == 0)
                     def _():
@@ -449,7 +463,7 @@
     resid[...] = tokens[...].astype(jnp.float32) + tail_product(attn[ours, :], out_weight[...])
     services(3, 5)
     flip(cot_full, 1)
-    service(5)
+    services(5, HALFWAY)
     send_part.wait_recv()
     summed = resid[...] + peer[...].astype(jnp.float32)
     resid[...] = summed
@@ -458,43 +472,67 @@
     send_two = remote(part, full_two.at[ours], swap_sem.at[3, 0], swap_sem.at[3, 1], twin)
     send_two.start()
     full_two[ours, :] = part[...]
-    ready = 9
-    services(6, ready)
+    ready = READY
+    services(HALFWAY, ready)
     remote(part, full_two.at[theirs], swap_sem.at[3, 0], swap_sem.at[3, 1], twin).wait_recv()
     flip(full_two, 0)
     save_qkv.wait()
 
-    def works(first, last):
+    jobs, turns_left = count * n, count * (n - 1) - ready
+    most = 2 if 2 * (turns_left - 1) >= jobs - 2 else 3
+
+    def done_before(i):
+        return jnp.minimum(jnp.minimum(most * i, i + ready + count), jobs - 2)
+
+    def both(i, carry):
+        service(ready + i)
+        first, last = done_before(i), done_before(i + 1)
+
         def one(job, carry):
+            @pl.when((job == first) & ((i == 0) | (job == i + ready + count)))
+            def _():
+                prepare(job)
+
+            @pl.when(job + 1 <= i + ready + count)
+            def _():
+                prepare(job + 1)
+
             work(job)
             return carry
 
         lax.fori_loop(first, last, one, 0)
-
-    pairs = ready + 3
-
-    def both(i, carry):
-        service(ready + i)
-        several = 1 - jnp.minimum(i // pairs, 1)
-        first = several * 2 * i + (1 - several) * (pairs + i)
-        works(first, first + 1 + several)
-        return carry
-
-    lax.fori_loop(0, count * (n - 1) - ready, both, 0)
-
-    def finish(i, carry):
+        return carry
+
+    lax.fori_loop(0, turns_left - 1, both, 0)
+    full_turn = next(i for i in range(turns_left) if min(most * (i + 1), i + 1 + ready + count) > jobs - 3)
+    if jobs - 2 > full_turn + ready + count:
+        prepare(jobs - 2)
+    work(jobs - 2)
+
+    def partly(i, carry):
         there = pl.ds(pl.multiple_of(i * strip, strip), strip)
         gate = acc[0, there, :]
         up = acc[1, there, :]
-        d_act = acc[2, there, :]
         sig = 1.0 / (1.0 + jnp.exp(-gate))
         silu = gate * sig
-        act[0, there, :] = (d_act * up * sig * (1.0 + gate * (1.0 - sig))).astype(jnp.bfloat16)
-        act[1, there, :] = (d_act * silu).astype(jnp.bfloat16)
+        acc[0, there, :] = up * sig * (1.0 + gate * (1.0 - sig))
+        acc[1, there, :] = silu
         act[2, there, :] = (silu * up).astype(jnp.bfloat16)
         return carry
 
-    lax.fori_loop(0, seq // strip, finish, 0)
+    lax.fori_loop(0, seq // strip, partly, 0)
+    service(count * (n - 1) - 1)
+    prepare(jobs - 1)
+    work(jobs - 1)
+
+    def complete(i, carry):
+        there = pl.ds(pl.multiple_of(i * strip, strip), strip)
+        d_act = acc[2, there, :]
+        act[0, there, :] = (d_act * acc[0, there, :]).astype(jnp.bfloat16)
+        act[1, there, :] = (d_act * acc[1, there, :]).astype(jnp.bfloat16)
+        return carry
+
+    lax.fori_loop(0, seq // strip, complete, 0)
 
     def drain(step, carry):
         for side in range(2):
@@ -552,7 +590,7 @@
             vmem((half, model), low),
             vmem((half, model), low),
             vmem((count, seq, width), full),
-            vmem((2, 2 * rows, width // 2), low),
+            vmem((2, 2, 2 * rows, width // 2), low),
             vmem((2, 256, seq), low),
             dma((count + 2, 2)),
             dma((count + 2, 2, n)),
@@ -560,7 +598,7 @@
             dma((count + 2, 2, n)),
             dma((count + 2, 2, n)),
             dma((4, 2)),
-            dma((2,)),
+            dma((2, 2)),
             dma((2,)),
             dma((2,)),
             dma((4, n)),
@@ -855,18 +893,18 @@
             def _():
                 fetch(which + 1, i + 1, which, hidden).start()
 
-        @pl.when(i % 3 == 2)
+        @pl.when(i % 4 == 3)
         def _():
-            event(count + i // 3)
+            event(count + i // 4)
 
         return carry
 
     lax.fori_loop(0, turns, dn_two, 0)
-    done = done + turns // 3
+    done = done + turns // 4
     sends = [send_part(0, peer.at[0], 0)]
     sends[0].start()
     fetch(3, 0, 0, hidden).start()
-    events(3)
+    events(4)
     sends[0].wait_recv()
     sends[0].wait_send()
     strip = 32
@@ -903,7 +941,7 @@
     sends[1].start()
     d_full[ours, :] = part[0]
 
-    def narrow(which, width, slot, base, rows_of):
+    def narrow(which, width, slot, base, every, rows_of):
         def one(i, carry):
             @pl.when(i < turns - 1)
             def _():
@@ -921,15 +959,15 @@
                 else:
                     part[slot, :, there] = total.astype(jnp.bfloat16)
 
-            @pl.when(i % 4 == 3)
+            @pl.when(i % every == every - 1)
             def _():
-                event(base + i // 4)
+                event(base + i // every)
 
             return carry
 
         lax.fori_loop(0, turns, one, 0)
 
-    narrow(3, hidden, 1, done, lambda rows: [(act[2, rows, :], 0)])
+    narrow(3, hidden, 1, done, 4, lambda rows: [(act[2, rows, :], 0)])
     done = done + turns // 4
     sends.append(send_part(1, peer.at[1], 2))
     sends[2].start()
@@ -986,11 +1024,11 @@
     sends[1].wait_send()
     events(1)
     width = d_proj.shape[2]
-    narrow(0, q_wide, 0, done, lambda rows: [(d_proj[0, rows, :], 0), (d_proj[1, rows, :], width)])
-    done = done + turns // 4
+    narrow(0, q_wide, 0, done, 8, lambda rows: [(d_proj[0, rows, :], 0), (d_proj[1, rows, :], width)])
+    done = done + turns // 8
     sends.append(send_part(0, peer.at[0], 3))
     sends[3].start()
-    events(1)
+    events(3)
     sends[3].wait_recv()
 
     def norm_one(i, carry):
@@ -1021,13 +1059,11 @@
         partner = ((1 - i) * me + i * mate[0], (1 - i) * twin[1] + i * lane)
         swap = remote(table, others.at[i], trade_sem.at[i, 0], trade_sem.at[i, 1], partner)
         swap.start()
-        event(done + i)
         swap.wait()
         table[...] += others[i]
         return carry
 
     lax.fori_loop(0, 2, trade, 0)
-    done = done + 2
 
     def mail(o, target):
         return remote(table.at[target], inbox.at[o], post_sem.at[o], mail_sem.at[o], at((pos + o) % n, core, n))

time: 538 us -> 534 us (level)
  no operation moved by 1% of the time
where the time goes in v7:
time: 534 us; the launch traced here: 533 us
  Pallas kernels  528 us (99%)
    pallas_call x1, Pallas kernels, backward_block(): pl.pallas_call(functools.partial(backward_kernel, n, (q_heads, kv_heads,...  260 us
    pallas_call x1, Pallas kernels, forward_block(): pl.pallas_call(functools.partial(forward_kernel, n, (q_heads, kv_heads, s...  260 us

profile of v7, /device:TPU:0, one launch (start us, length us, event | category | flops | bytes accessed | tf_op | source)
XLA Modules:
  0.0 533.0 jit_solution(17403709074408662886)
XLA Ops:
  0.6 1.8 copy.26
  2.4 2.3 copy.27
  4.7 259.9 %shard_map.229 = (bf16[8192,3072]{1,0:T(8,128)(2,1)}, f32[512,2048]{1,0:T(8,128)}, bf16[512,1024]{1,0:T(8,128)(2,1)}, f32[256,2048]{1,0:T(8,128)}, bf16[3,2048,5...) custom-call(bf16[128,1024]{1,0:T(8,128)(2,1)} %refs_0_.1, ...), custom_call_target="tpu_custom_call" | custom-call | tf_op jit(solution)/shard_map/pallas_call | solution.py:565
  264.6 260.4 %shard_map.230 = (f32[128,3072]{1,0:T(8,128)}, f32[128,3072]{1,0:T(8,128)}, f32[128,3072]{1,0:T(8,128)}, f32[128,1024]{1,0:T(8,128)}, f32[128,1024]{1,0:T(8,128)...) custom-call(bf16[3,2048,512]{2,1,0:T(8,128)(2,1)} %get-tuple-element, ...), custom_call_target="tpu_custom_call" | custom-call | tf_op jit(solution)/shard_map/pallas_call | solution.py:1128
  525.0 7.7 %shard_map.231 = (bf16[256,2048]{1,0:T(8,128)(2,1)}, bf16[256,2048]{1,0:T(8,128)(2,1)}, f32[128,1024]{1,0:T(8,128)}, f32[128,512]{1,0:T(8,128)}, f32[128,512]{1,...) custom-call(f32[8,128]{1,0:T(8,128)} %get-tuple-element.55.refs_0_, ...), custom_call_target="tpu_custom_call" | custom-call | tf_op jit(solution)/shard_map/pallas_call | solution.py:1230

commit v8 on v7

--- a/solution.py
+++ b/solution.py
@@ -149,11 +149,11 @@
 
 def forward_kernel(n, dims, *refs):
     (
-        query_shard, key_shard, value_shard, out_shard, gate_shard, up_shard, down_shard,
+        query_shard, key_shard, value_shard, out_shard, gate_shard, up_shard, down_given,
         tokens, cot, frequency, seg_row, attn_share, mlp_share, qk_share,
         weights, qkv_out, attn, resid, flipped, act, attn_gain, mlp_gain, gains, tab, seg_col,
         full_rows, cot_full, full_two, out_weight, columns, box, kept, part, peer, acc, blocks, stage,
-        own_sem, send_sem, recv_sem, give_sem, take_sem, swap_sem, load_sem, stage_sem, column_sem, tile_sem,
+        own_sem, send_sem, recv_sem, give_sem, take_sem, swap_sem, load_sem, stage_sem, column_sem, tile_sem, down_shard,
     ) = refs
     q_heads, kv_heads, seq, block = dims
     pos, core = ring_place(n)
@@ -284,6 +284,8 @@
     doc_start = jnp.sum(jnp.where(ids < own_id, 1.0, 0.0), axis=1, keepdims=True)
     place = lax.broadcasted_iota(jnp.int32, (seq, 1), 0).astype(jnp.float32)
     seg_col[...] = own_id.astype(jnp.int32)
+    for i in range(0, width, 512):
+        down_shard[:, i : i + 512] = down_given[i : i + 512, :].T
     angles = (place - doc_start) * frequency[...]
     tab[0] = jnp.cos(angles)
     sign = jnp.where(lax.broadcasted_iota(jnp.int32, angles.shape, 1) < HD // 2, -1.0, 1.0)
@@ -554,7 +556,7 @@
 
 def forward_block(shards, tokens, cot, frequency, seg_row, shares, q_heads, kv_heads, dp):
     n = dp // 2
-    rows, width = shards[-1].shape
+    rows, width = shards[-2].shape
     count = 3
     half, model = tokens.shape
     seq = 2 * half
@@ -602,6 +604,7 @@
             dma((2,)),
             dma((2,)),
             dma((4, n)),
+            vmem((rows, width), low),
         ],
         compiler_params=pltpu.CompilerParams(
             collective_id=1, has_side_effects=True, vmem_limit_bytes=67043328
@@ -1193,8 +1196,8 @@
     sources, outs = refs[1:9], refs[9:21]
     bufs, turned, in_sem, out_sem = refs[21:29], refs[29:31], refs[31], refs[32]
     loads = [pltpu.make_async_copy(source, buf, in_sem.at[i]) for i, (source, buf) in enumerate(zip(sources, bufs))]
-    for load in loads:
-        load.start()
+    for i in (2, 6, 7, 5, 3, 4, 0, 1):
+        loads[i].start()
     half = outs[3].shape[1]
     stores = [None] * 9
 
@@ -1202,16 +1205,22 @@
         stores[i] = pltpu.make_async_copy(buf, out, out_sem.at[i])
         stores[i].start()
 
-    for i, (which, out) in enumerate(((6, 0), (7, 1), (3, 2), (0, 6), (1, 7))):
+    def turn_over(i, which, out):
+        loads[which].wait()
+        turned[i][...] = bufs[which][...].T
+        store(7 + i, turned[i], outs[out])
+
+    turn_over(0, 2, 8)
+    for i, (which, out) in enumerate(((6, 0), (7, 1))):
         loads[which].wait()
         store(i, bufs[which], outs[out])
+    turn_over(1, 5, 5)
+    for i, (which, out) in enumerate(((3, 2), (0, 6), (1, 7))):
+        loads[which].wait()
+        store(2 + i, bufs[which], outs[out])
     loads[4].wait()
     store(5, bufs[4].at[:, pl.ds(0, half)], outs[3])
     store(6, bufs[4].at[:, pl.ds(half, half)], outs[4])
-    for i, (which, out) in enumerate(((2, 8), (5, 5))):
-        loads[which].wait()
-        turned[i][...] = bufs[which][...].T
-        store(7 + i, turned[i], outs[out])
     me = lax.axis_index("dp")
     for row in range(3):
         target = outs[9 + row]
@@ -1266,7 +1275,7 @@
     (
         weights, projected, attn_rows, resid, flipped, act, attn_gain, mlp_gain, pair, rope_tab, seg_col,
     ) = forward_block(
-        (w_query, w_key, w_value, w_output.T, w_gate, w_up, w_down.T),
+        (w_query, w_key, w_value, w_output.T, w_gate, w_up, w_down),
         tokens,
         cotangent,
         frequency,

time: 534 us -> 532 us (level)
  no operation moved by 1% of the time
where the time goes in v8:
time: 532 us; the launch traced here: 530 us
  Pallas kernels  528 us (99%)
    pallas_call x1, Pallas kernels, backward_block(): pl.pallas_call(functools.partial(backward_kernel, n, (q_heads, kv_heads,...  260 us
    pallas_call x1, Pallas kernels, forward_block(): pl.pallas_call(functools.partial(forward_kernel, n, (q_heads, kv_heads, s...  260 us

profile of v8, /device:TPU:0, one launch (start us, length us, event | category | flops | bytes accessed | tf_op | source)
XLA Modules:
  0.0 530.5 jit_solution(7418084872178235591)
XLA Ops:
  0.6 1.8 copy.26
  2.4 259.9 %shard_map.229 = (bf16[8192,3072]{1,0:T(8,128)(2,1)}, f32[512,2048]{1,0:T(8,128)}, bf16[512,1024]{1,0:T(8,128)(2,1)}, f32[256,2048]{1,0:T(8,128)}, bf16[3,2048,5...) custom-call(bf16[128,1024]{1,0:T(8,128)(2,1)} %refs_0_.1, ...), custom_call_target="tpu_custom_call" | custom-call | tf_op jit(solution)/shard_map/pallas_call | solution.py:567
  262.3 260.4 %shard_map.230 = (f32[128,3072]{1,0:T(8,128)}, f32[128,3072]{1,0:T(8,128)}, f32[128,3072]{1,0:T(8,128)}, f32[128,1024]{1,0:T(8,128)}, f32[128,1024]{1,0:T(8,128)...) custom-call(bf16[3,2048,512]{2,1,0:T(8,128)(2,1)} %get-tuple-element, ...), custom_call_target="tpu_custom_call" | custom-call | tf_op jit(solution)/shard_map/pallas_call | solution.py:1131
  522.8 7.5 %shard_map.231 = (bf16[256,2048]{1,0:T(8,128)(2,1)}, bf16[256,2048]{1,0:T(8,128)(2,1)}, f32[128,1024]{1,0:T(8,128)}, f32[128,512]{1,0:T(8,128)}, f32[128,512]{1,...) custom-call(f32[8,128]{1,0:T(8,128)} %get-tuple-element.55.refs_0_, ...), custom_call_target="tpu_custom_call" | custom-call | tf_op jit(solution)/shard_map/pallas_call | solution.py:1239

commit v9 on v8

--- a/solution.py
+++ b/solution.py
@@ -907,7 +907,7 @@
     sends = [send_part(0, peer.at[0], 0)]
     sends[0].start()
     fetch(3, 0, 0, hidden).start()
-    events(4)
+    events(3)
     sends[0].wait_recv()
     sends[0].wait_send()
     strip = 32
@@ -983,7 +983,7 @@
         )
 
     fetch_columns(0).start()
-    events(1)
+    events(2)
     remote(part.at[0], d_full.at[theirs], swap_sem.at[1, 0], swap_sem.at[1, 1], twin).wait_recv()
     flip_into(d_full, d_flip, stage, stage_sem)
     qk_sum[...] = jnp.zeros_like(qk_sum)

time: 532 us -> 532 us (level)
  no operation moved by 1% of the time
where the time goes in v9:
time: 532 us; the launch traced here: 530 us
  Pallas kernels  528 us (99%)
    pallas_call x1, Pallas kernels, backward_block(): pl.pallas_call(functools.partial(backward_kernel, n, (q_heads, kv_heads,...  260 us
    pallas_call x1, Pallas kernels, forward_block(): pl.pallas_call(functools.partial(forward_kernel, n, (q_heads, kv_heads, s...  260 us

profile of v9, /device:TPU:0, one launch (start us, length us, event | category | flops | bytes accessed | tf_op | source)
XLA Modules:
  0.0 530.5 jit_solution(13345371591472994428)
XLA Ops:
  0.6 1.8 copy.26
  2.4 259.9 %shard_map.229 = (bf16[8192,3072]{1,0:T(8,128)(2,1)}, f32[512,2048]{1,0:T(8,128)}, bf16[512,1024]{1,0:T(8,128)(2,1)}, f32[256,2048]{1,0:T(8,128)}, bf16[3,2048,5...) custom-call(bf16[128,1024]{1,0:T(8,128)(2,1)} %refs_0_.1, ...), custom_call_target="tpu_custom_call" | custom-call | tf_op jit(solution)/shard_map/pallas_call | solution.py:567
  262.3 260.4 %shard_map.230 = (f32[128,3072]{1,0:T(8,128)}, f32[128,3072]{1,0:T(8,128)}, f32[128,3072]{1,0:T(8,128)}, f32[128,1024]{1,0:T(8,128)}, f32[128,1024]{1,0:T(8,128)...) custom-call(bf16[3,2048,512]{2,1,0:T(8,128)(2,1)} %get-tuple-element, ...), custom_call_target="tpu_custom_call" | custom-call | tf_op jit(solution)/shard_map/pallas_call | solution.py:1131
  522.8 7.5 %shard_map.231 = (bf16[256,2048]{1,0:T(8,128)(2,1)}, bf16[256,2048]{1,0:T(8,128)(2,1)}, f32[128,1024]{1,0:T(8,128)}, f32[128,512]{1,0:T(8,128)}, f32[128,512]{1,...) custom-call(f32[8,128]{1,0:T(8,128)} %get-tuple-element.55.refs_0_, ...), custom_call_target="tpu_custom_call" | custom-call | tf_op jit(solution)/shard_map/pallas_call | solution.py:1239
